TPU v7x, 256 devices: a 4x2x16 block of a 4x16x16 slice. The times are simulated.
256 devices in a mesh: parts: 2 (over y), rows: 128 (over z, x, core).
Axes of the slice: x: 4, y: 2, z: 16, core: 2. Of those that a mesh axis runs over, the one named last changes fastest.
The devices are a block of a 4x16x16 slice.
Arguments:
- latent: bfloat16 [4, 128, 160, 384], P('parts', 'rows'), parts along dimension 0, may hold values from -40 to 40
- conv_cache: bfloat16 [4, 128, 160, 384], P('parts', 'rows'), parts along dimension 0, may hold values from -6 to 6
- time_cache: bfloat16 [4, 128, 160, 384], P('parts', 'rows'), parts along dimension 0, may hold values from -6 to 6
- norm_gain: float32 [384], replicated, may hold values from 0.5 to 2
- norm_shift: float32 [384], replicated, may hold values from -3 to 3
- conv_weight: bfloat16 [3, 3, 3, 384, 384], replicated, may hold values from -0.0625 to 0.0625
- conv_bias: float32 [384], replicated, may hold values from -2 to 2
- time_weight: bfloat16 [3, 384, 768], replicated, may hold values from -0.1875 to 0.1875
- time_bias: float32 [768], replicated, may hold values from -2 to 2
- up_weight: bfloat16 [3, 3, 384, 192], replicated, may hold values from -0.109375 to 0.109375
- up_bias: float32 [192], replicated, may hold values from -2 to 2
Outputs:
- frames_out: bfloat16 [8, 256, 320, 192], P('parts', 'rows'), parts along dimension 0
There are 2 independent parts, one for each index of `parts`. A program takes and returns all parts, laid end to end along the dimension named above; an argument that names none is the same for every part. Nothing has to cross between parts.
All inputs are finite; a program needn't handle non-finite values.
Results may differ from a plain program's by a relative error of at most 0.0056.
Values may be sent and summed in bfloat16 or wider, within the bound.
No kernel may reach another device: no remote copies, remote signals or barrier semaphores. Data moves between devices by JAX's collectives and lax.ppermute only.
A program may use at most 64 MiB of HBM per device.

v0:
```python
import jax
import jax.numpy as jnp
from jax import lax
from jax.sharding import Mesh
from jax.sharding import PartitionSpec as P

GROUPS = 32
ROWS = ("rows_0", "rows_1", "rows_2")


EPSILON = 1e-06


def over_axes(value, axes):
    for axis in axes:
        value = lax.psum(value, axis)
    return value


def with_halo(value, sides, width):
    for axis, dim in sides:
        devices, length = (lax.axis_size(axis), value.shape[dim])
        up = [(i, (i + 1) % devices) for i in range(devices - 1)]
        down = [(j, i) for i, j in up]
        last = lax.slice_in_dim(value, length - width, length, axis=dim)
        initial = lax.slice_in_dim(value, 0, width, axis=dim)
        before = lax.ppermute(last, axis, up)
        after = lax.ppermute(initial, axis, down)
        value = jnp.concatenate([before, value, after], axis=dim)
    return value


def conv_taps(padded, kernel, row_count, col_count):
    channels = padded.shape[-1]
    total = jnp.zeros((padded.shape[0] * row_count * col_count, kernel.shape[-1]), jnp.float32)
    for row_tap in range(3):
        window = jnp.concatenate(
            [
                padded[:, row_tap : row_tap + row_count, col_tap : col_tap + col_count]
                for col_tap in range(3)
            ],
            axis=-1,
        )
        total = total + jnp.dot(
            window.reshape(-1, 3 * channels),
            kernel[row_tap].reshape(3 * channels, -1),
            preferred_element_type=jnp.float32,
        )
    return total


def temporal(block, time_cache, time_weight, time_bias):
    frame_count = block.shape[0]
    channels = block.shape[-1]
    joined = jnp.concatenate([time_cache, block], axis=0)
    window = jnp.concatenate(
        [joined[frame_tap : frame_tap + frame_count] for frame_tap in range(3)], axis=-1
    )
    mixed = (
        jnp.dot(
            window.reshape(-1, 3 * channels),
            time_weight.reshape(3 * channels, -1),
            preferred_element_type=jnp.float32,
        )
        + time_bias
    )
    mixed = mixed.astype(jnp.bfloat16).reshape(block.shape[:-1] + (2, channels))
    return jnp.moveaxis(mixed, 3, 1).reshape((2 * frame_count,) + block.shape[1:])


def on_device(
    latent,
    conv_cache,
    time_cache,
    norm_gain,
    norm_shift,
    conv_weight,
    conv_bias,
    time_weight,
    time_bias,
    up_weight,
    up_bias,
):
    frame_count, row_count, col_count, channels = latent.shape
    signal = latent.astype(jnp.float32)
    grouped = signal.reshape(frame_count, row_count, col_count, GROUPS, channels // GROUPS)
    entries = float(
        frame_count * row_count * lax.axis_size(ROWS) * col_count * (channels // GROUPS)
    )
    total_sum, square_sum = (
        over_axes(jnp.sum(grouped, axis=(0, 1, 2, 4)), ROWS),
        over_axes(jnp.sum(grouped * grouped, axis=(0, 1, 2, 4)), ROWS),
    )
    center = (total_sum / entries).reshape(1, 1, 1, GROUPS, 1)
    spread = square_sum.reshape(1, 1, 1, GROUPS, 1) / entries - center * center
    normed = ((grouped - center) * lax.rsqrt(spread + EPSILON)).reshape(signal.shape)
    active = jax.nn.silu(normed * norm_gain + norm_shift).astype(jnp.bfloat16)
    joined = jnp.concatenate([conv_cache, active], axis=0)
    rimmed = with_halo(joined, ((ROWS, 1),), 1)
    padded = jnp.pad(rimmed, ((0, 0), (0, 0), (1, 1), (0, 0)))
    summed = conv_bias + jnp.zeros((frame_count * row_count * col_count, channels), jnp.float32)
    for frame_tap in range(3):
        summed = summed + conv_taps(
            padded[frame_tap : frame_tap + frame_count],
            conv_weight[frame_tap],
            row_count,
            col_count,
        )
    block = (signal + summed.reshape(signal.shape)).astype(jnp.bfloat16)
    doubled = temporal(block, time_cache, time_weight, time_bias)
    upsampled = jnp.repeat(jnp.repeat(doubled, 2, axis=1), 2, axis=2)
    upsampled = with_halo(upsampled, ((ROWS, 1),), 1)
    padded_up = jnp.pad(upsampled, ((0, 0), (0, 0), (1, 1), (0, 0)))
    result = conv_taps(padded_up, up_weight, 2 * row_count, 2 * col_count) + up_bias
    return result.astype(jnp.bfloat16).reshape(
        2 * frame_count, 2 * row_count, 2 * col_count, up_weight.shape[-1]
    )


def solution(mesh):
    finer = Mesh(
        mesh.devices.reshape(mesh.shape["parts"], 16, 4, 2), ("parts", "rows_0", "rows_1", "rows_2")
    )
    placed = (
        P("parts", ROWS, None, None),
        P("parts", ROWS, None, None),
        P("parts", ROWS, None, None),
        P(),
        P(),
        P(),
        P(),
        P(),
        P(),
        P(),
        P(),
    )
    return jax.shard_map(
        on_device,
        mesh=finer,
        in_specs=placed,
        out_specs=P("parts", ROWS, None, None),
        check_vma=False,
    )
```

profile of v0, /device:TPU:33, one launch (start us, length us, event | category | flops | bytes accessed | tf_op | source)
XLA Modules:
  0.0 132.9 jit_solution(4475981144398984496)
XLA Ops:
  0.0 1.2 convert_reduce_fusion
  1.6 43.2 %all-reduce.2 = (f32[32]{0:T(128)S(1)}, f32[32]{0:T(128)S(1)}) all-reduce(f32[32]{0:T(128)S(1)} %reduce_sum.37, f32[32]{0:T(128)S(1)} %reduce_sum.25), channel_id=1, replica_groups=mesh['parts'=2,'rows_0'=16,'rows_1'=4,'rows_2'=2] {'rows_0'}, use_global_device_ids=true, to_apply=%region_7.0 | all-reduce | flops 64 | bytes 512 | tf_op jit(solution)/shard_map/psum | solution.py:16
  44.8 8.9 %all-reduce.3 = (f32[32]{0:T(128)S(1)}, f32[32]{0:T(128)S(1)}) all-reduce(f32[32]{0:T(128)S(1)} %get-tuple-element.7, f32[32]{0:T(128)S(1)} %get-tuple-element.8), channel_id=1, replica_groups=mesh['parts'=2,'rows_0'=16,'rows_1'=4,'rows_2'=2] {'rows_1'}, use_global_device_ids=true, to_apply=%region_8.9 | all-reduce | flops 64 | bytes 512 | tf_op jit(solution)/shard_map/psum | solution.py:16
  53.7 11.8 %all-reduce.4 = (f32[32]{0:T(128)S(1)}, f32[32]{0:T(128)S(1)}) all-reduce(f32[32]{0:T(128)S(1)} %get-tuple-element.9, f32[32]{0:T(128)S(1)} %get-tuple-element.10), channel_id=1, replica_groups=mesh['parts'=2,'rows_0'=16,'rows_1'=4,'rows_2'=2] {'rows_2'}, use_global_device_ids=true, to_apply=%region_9.10 | all-reduce | flops 64 | bytes 512 | tf_op jit(solution)/shard_map/psum | solution.py:16
  65.9 1.1 fusion.31
  67.1 1.0 pad_maximum_fusion.13
  68.1 2.0 %collective-permute-start = (bf16[4,1,160,384]{3,2,1,0:T(8,128)(2,1)S(1)}, bf16[4,1,160,384]{3,2,1,0:T(8,128)(2,1)S(1)}, u32[]{:S(2)}, u32[]{:S(2)}) collective-permute-start(bf16[4,1,160,384]{3,2,1,0:T(8,128)(2,1)S(1)} %pad_maximum_fusion.13), channel_id=1, source_target_pairs={{0,1},{1,2},{2,3},{3,4},{4,5},{5,6},{6,7},{7,8},{8,9},{9,10},{10,1... | collective-permute-start | bytes 1474568 | tf_op jit(solution)/shard_map/ppermute | solution.py:27
  70.1 2.5 %collective-permute-start.1 = (bf16[4,1,160,384]{3,2,1,0:T(8,128)(2,1)S(1)}, bf16[4,1,160,384]{3,2,1,0:T(8,128)(2,1)S(1)}, u32[]{:S(2)}, u32[]{:S(2)}) collective-permute-start(bf16[4,1,160,384]{3,2,1,0:T(8,128)(2,1)S(1)} %pad_maximum_fusion.13), channel_id=1, source_target_pairs={{1,0},{2,1},{3,2},{4,3},{5,4},{6,5},{7,6},{8,7},{9,8},{10,9},{11,1... | collective-permute-start | bytes 1474568 | tf_op jit(solution)/shard_map/ppermute | solution.py:28
  72.6 3.9 %fusion.35 = (bf16[1,1,3,384,384]{4,3,2,1,0:T(8,128)(2,1)S(1)}, bf16[1,1,3,384,384]{4,3,2,1,0:T(8,128)(2,1)S(1)}, bf16[1,1,3,384,384]{4,3,2,1,0:T(8,128)(2,1)S(1...) fusion(bf16[3,3,3,384,384]{4,3,2,1,0:T(8,128)(2,1)} %param.16), kind=kLoop, calls=%fused_computation.71 | loop fusion | bytes 15925248 | tf_op jit(solution)/shard_map/slice | solution.py:46
  76.6 3.7 %collective-permute-done.1 = bf16[4,1,160,384]{3,2,1,0:T(8,128)(2,1)S(1)} collective-permute-done((bf16[4,1,160,384]{3,2,1,0:T(8,128)(2,1)S(1)}, bf16[4,1,160,384]{3,2,1,0:T(8,128)(2,1)S(1)}, u32[]{:S(2)}, u32[]{:S(2)}) %collective-permute-start.1) | collective-permute-done | bytes 491552 | tf_op jit(solution)/shard_map/ppermute | solution.py:28
  80.2 0.5 select_maximum_fusion
  80.7 0.7 fusion.37
  81.4 0.1 pad_maximum_fusion.10
  81.6 0.6 fusion.43
  82.4 0.6 fusion.42
  83.0 0.2 pad_maximum_fusion.4
  83.1 0.6 fusion.41
  83.7 0.6 convolution_add_fusion.3
  84.5 0.6 convolution_add_fusion.5
  85.1 0.6 convolution_add_fusion.7
  85.7 0.6 fusion.18
  86.3 0.6 fusion.19
  87.0 0.6 fusion.20
  87.6 0.3 copy-done.5
  88.1 0.8 fusion.17
  89.1 0.5 broadcast_in_dim.6
  89.6 1.3 slice.254
  90.9 1.9 %collective-permute-start.2 = (bf16[4,1,320,384]{3,2,0,1:T(8,128)(2,1)}, bf16[4,1,320,384]{3,2,0,1:T(8,128)(2,1)S(1)}, u32[]{:S(2)}, u32[]{:S(2)}) collective-permute-start(bf16[4,1,320,384]{3,2,0,1:T(8,128)(2,1)} %slice.254), channel_id=1, source_target_pairs={{0,1},{1,2},{2,3},{3,4},{4,5},{5,6},{6,7},{7,8},{8,9},{9,10},{10,1... | collective-permute-start | bytes 2949128 | tf_op jit(solution)/shard_map/ppermute | solution.py:27
  92.9 2.7 %collective-permute-start.3 = (bf16[4,1,320,384]{3,2,0,1:T(8,128)(2,1)}, bf16[4,1,320,384]{3,2,0,1:T(8,128)(2,1)S(1)}, u32[]{:S(2)}, u32[]{:S(2)}) collective-permute-start(bf16[4,1,320,384]{3,2,0,1:T(8,128)(2,1)} %slice.254), channel_id=1, source_target_pairs={{1,0},{2,1},{3,2},{4,3},{5,4},{6,5},{7,6},{8,7},{9,8},{10,9},{11,1... | collective-permute-start | bytes 2949128 | tf_op jit(solution)/shard_map/ppermute | solution.py:28
  95.6 1.4 %fusion.38 = (bf16[1,3,384,192]{2,3,1,0:T(8,128)(2,1)S(1)}, bf16[1,3,384,192]{2,3,1,0:T(8,128)(2,1)S(1)}, bf16[1,3,384,192]{2,3,1,0:T(8,128)(2,1)S(1)}) fusion(bf16[3,3,384,192]{2,3,1,0:T(8,128)(2,1)} %param.20), kind=kLoop, calls=%fused_computation.74 | loop fusion | bytes 2654208 | tf_op jit(solution)/shard_map/slice | solution.py:46
  97.0 0.4 copy.24
  97.4 0.9 copy.29
  98.3 0.4 copy.26
  98.7 0.9 copy.30
  99.5 0.4 copy.23
  99.9 0.9 copy.28
  100.8 1.3 broadcast_in_dim.14
  102.1 2.1 %collective-permute-done.2 = bf16[4,1,320,384]{3,2,0,1:T(8,128)(2,1)S(1)} collective-permute-done((bf16[4,1,320,384]{3,2,0,1:T(8,128)(2,1)}, bf16[4,1,320,384]{3,2,0,1:T(8,128)(2,1)S(1)}, u32[]{:S(2)}, u32[]{:S(2)}) %collective-permute-start.2) | collective-permute-done | bytes 983072 | tf_op jit(solution)/shard_map/ppermute | solution.py:27
  104.2 4.3 %collective-permute-done.3 = bf16[4,1,320,384]{3,2,0,1:T(8,128)(2,1)S(1)} collective-permute-done((bf16[4,1,320,384]{3,2,0,1:T(8,128)(2,1)}, bf16[4,1,320,384]{3,2,0,1:T(8,128)(2,1)S(1)}, u32[]{:S(2)}, u32[]{:S(2)}) %collective-permute-start.3) | collective-permute-done | bytes 983072 | tf_op jit(solution)/shard_map/ppermute | solution.py:28
  108.6 1.7 %broadcast_in_dim.15 = bf16[4,2,320,384]{3,2,1,0:T(8,128)(2,1)S(1)} broadcast(bf16[4,320,384]{2,1,0:T(8,128)(2,1)} %broadcast_in_dim.14), dimensions={0,2,3} | broadcast | bytes 2949120 | tf_op jit(solution)/shard_map/broadcast_in_dim | solution.py:111
  110.3 1.3 fusion.9
  111.6 3.5 %fusion.36 = (bf16[4,2,320,384]{3,2,1,0:T(8,128)(2,1)S(1)}, bf16[4,2,320,384]{3,2,1,0:T(8,128)(2,1)S(1)}, bf16[4,2,320,384]{3,2,1,0:T(8,128)(2,1)S(1)}, bf16[4,2...) fusion(bf16[4,4,322,384]{3,2,1,0:T(8,128)(2,1)S(1)} %fusion.9), kind=kLoop, calls=%fused_computation.72 | loop fusion | bytes 23592960 | tf_op jit(solution)/shard_map/slice | solution.py:39
  115.1 5.8 %fusion.4 = (bf16[4,2,320,1152]{3,2,1,0:T(8,128)(2,1)S(1)}, bf16[4,2,320,1152]{3,2,1,0:T(8,128)(2,1)S(1)}, bf16[4,2,320,1152]{3,2,1,0:T(8,128)(2,1)S(1)}) fusion(bf16[4,2,320,384]{3,2,1,0:T(8,128)(2,1)S(1)} %broadcast_in_dim.15, bf16[4,1,320,384]{3,2,1,0:T(8,128)(2,1)} %bitcast.81, bf16[4,2,320,384]{3,2,1,0:T(8,128)(2,1)} %get-tuple-element.26, ...), kind=kLoop, calls=%fused_computation.8 | loop fusion | flops 64880640 | bytes 33423360 | tf_op jit(solution)/shard_map/concatenate | solution.py:37
  121.0 3.2 %fusion.44 = f32[2560,192]{0,1:T(8,128)S(1)} fusion(bf16[2560,1152]{1,0:T(8,128)(2,1)S(1)} %bitcast.79, bf16[1152,192]{0,1:T(8,128)(2,1)} %bitcast.107), kind=kOutput, calls=%fused_computation.80 | convolution fusion | flops 1132462080 | bytes 8306688 | tf_op jit(solution)/shard_map/dot_general | solution.py:44
  124.1 2.1 %fusion.45 = f32[2560,192]{0,1:T(8,128)S(1)} fusion(bf16[2560,1152]{1,0:T(8,128)(2,1)S(1)} %bitcast.78, bf16[1152,192]{0,1:T(8,128)(2,1)S(1)} %bitcast.108), kind=kOutput, calls=%fused_computation.81 | convolution fusion | flops 1132462080 | bytes 8306688 | tf_op jit(solution)/shard_map/dot_general | solution.py:44
  126.3 2.1 %fusion.12 = bf16[2560,192]{0,1:T(8,128)(2,1)S(1)} fusion(f32[2560,192]{0,1:T(8,128)S(1)} %fusion.45, f32[2560,192]{0,1:T(8,128)S(1)} %fusion.44, bf16[2560,1152]{1,0:T(8,128)(2,1)S(1)} %bitcast.77, bf16[1152,192]{0,1:T(8,128)(2,1)S(1)} %bitcast.109, f32[192]{0:T(256)S(1)} %copy-done.9), kind=kOutput, calls=%fused_computation.20 | convolution fusion | flops 1134428160 | bytes 11256576 | tf_op jit(solution)/shard_map/dot_general | solution.py:44
  128.4 2.1 %reshape.144 = bf16[4,2,320,192]{2,1,0,3:T(2,128)(2,1)} reshape(bf16[2560,192]{0,1:T(8,128)(2,1)S(1)} %fusion.12) | data formatting | bytes 1966080 | tf_op jit(solution)/shard_map/reshape | solution.py:115
  130.5 2.4 %copy.27 = bf16[4,2,320,192]{2,3,1,0:T(8,128)(2,1)} copy(bf16[4,2,320,192]{2,1,0,3:T(2,128)(2,1)} %reshape.144) | data formatting | bytes 1966080 | tf_op jit(solution)/shard_map/reshape | solution.py:115
  (43 shorter events, 1.7 us)
Async XLA Ops:
  0.0 88.1 %copy-start = (bf16[3,384,768]{2,1,0:T(8,128)(2,1)S(1)}, bf16[3,384,768]{2,1,0:T(8,128)(2,1)}, u32[]{:S(2)}) copy-start(bf16[3,384,768]{2,1,0:T(8,128)(2,1)} %param.18) | copy-start | bytes 5308420
  0.0 72.5 %copy-start.4 = (bf16[2,1,160,384]{3,2,1,0:T(8,128)(2,1)S(1)}, bf16[2,1,160,384]{3,2,1,0:T(8,128)(2,1)}, u32[]{:S(2)}) copy-start(bf16[2,1,160,384]{3,2,1,0:T(8,128)(2,1)} %param.12) | copy-start | bytes 737284
  68.1 8.4 %collective-permute-start = (bf16[4,1,160,384]{3,2,1,0:T(8,128)(2,1)S(1)}, bf16[4,1,160,384]{3,2,1,0:T(8,128)(2,1)S(1)}, u32[]{:S(2)}, u32[]{:S(2)}) collective-permute-start(bf16[4,1,160,384]{3,2,1,0:T(8,128)(2,1)S(1)} %pad_maximum_fusion.13), channel_id=1, source_target_pairs={{0,1},{1,2},{2,3},{3,4},{4,5},{5,6},{6,7},{7,8},{8,9},{9,10},{10,1... | collective-permute-start | bytes 1474568 | tf_op jit(solution)/shard_map/ppermute | solution.py:27
  70.1 10.2 %collective-permute-start.1 = (bf16[4,1,160,384]{3,2,1,0:T(8,128)(2,1)S(1)}, bf16[4,1,160,384]{3,2,1,0:T(8,128)(2,1)S(1)}, u32[]{:S(2)}, u32[]{:S(2)}) collective-permute-start(bf16[4,1,160,384]{3,2,1,0:T(8,128)(2,1)S(1)} %pad_maximum_fusion.13), channel_id=1, source_target_pairs={{1,0},{2,1},{3,2},{4,3},{5,4},{6,5},{7,6},{8,7},{9,8},{10,9},{11,1... | collective-permute-start | bytes 1474568 | tf_op jit(solution)/shard_map/ppermute | solution.py:28
  85.1 0.7 copy-start.10
  87.0 0.9 copy-start.5
  87.0 1.1 copy-start.8
  87.0 1.1 copy-start.11
  90.9 13.3 %collective-permute-start.2 = (bf16[4,1,320,384]{3,2,0,1:T(8,128)(2,1)}, bf16[4,1,320,384]{3,2,0,1:T(8,128)(2,1)S(1)}, u32[]{:S(2)}, u32[]{:S(2)}) collective-permute-start(bf16[4,1,320,384]{3,2,0,1:T(8,128)(2,1)} %slice.254), channel_id=1, source_target_pairs={{0,1},{1,2},{2,3},{3,4},{4,5},{5,6},{6,7},{7,8},{8,9},{9,10},{10,1... | collective-permute-start | bytes 2949128 | tf_op jit(solution)/shard_map/ppermute | solution.py:27
  92.9 15.7 %collective-permute-start.3 = (bf16[4,1,320,384]{3,2,0,1:T(8,128)(2,1)}, bf16[4,1,320,384]{3,2,0,1:T(8,128)(2,1)S(1)}, u32[]{:S(2)}, u32[]{:S(2)}) collective-permute-start(bf16[4,1,320,384]{3,2,0,1:T(8,128)(2,1)} %slice.254), channel_id=1, source_target_pairs={{1,0},{2,1},{3,2},{4,3},{5,4},{6,5},{7,6},{8,7},{9,8},{10,9},{11,1... | collective-permute-start | bytes 2949128 | tf_op jit(solution)/shard_map/ppermute | solution.py:28
  104.2 6.1 %copy-start.2 = (bf16[4,1,320,384]{3,2,0,1:T(8,128)(2,1)}, bf16[4,1,320,384]{3,2,0,1:T(8,128)(2,1)S(1)}, u32[]{:S(2)}) copy-start(bf16[4,1,320,384]{3,2,0,1:T(8,128)(2,1)S(1)} %collective-permute-done.2) | copy-start | bytes 2949124
  108.6 1.7 %copy-start.3 = (bf16[4,1,320,384]{3,2,0,1:T(8,128)(2,1)}, bf16[4,1,320,384]{3,2,0,1:T(8,128)(2,1)S(1)}, u32[]{:S(2)}) copy-start(bf16[4,1,320,384]{3,2,0,1:T(8,128)(2,1)S(1)} %collective-permute-done.3) | copy-start | bytes 2949124
  120.9 3.2 %copy-start.6 = (bf16[24,8,3,384]{3,1,2,0:T(8,128)(2,1)S(1)}, bf16[24,8,3,384]{3,1,2,0:T(8,128)(2,1)}, u32[]{:S(2)}) copy-start(bf16[24,8,3,384]{3,1,2,0:T(8,128)(2,1)} %copy.30) | copy-start | bytes 1327108
  124.1 2.1 %copy-start.7 = (bf16[24,8,3,384]{3,1,2,0:T(8,128)(2,1)S(1)}, bf16[24,8,3,384]{3,1,2,0:T(8,128)(2,1)}, u32[]{:S(2)}) copy-start(bf16[24,8,3,384]{3,1,2,0:T(8,128)(2,1)} %copy.28) | copy-start | bytes 1327108
  124.1 2.1 %copy-start.9 = (f32[192]{0:T(256)S(1)}, f32[192]{0:T(256)}, u32[]{:S(2)}) copy-start(f32[192]{0:T(256)} %param.21) | copy-start | bytes 2308
  126.3 6.6 %copy-start.1 = (bf16[3,384,768]{2,1,0:T(8,128)(2,1)S(1)}, bf16[3,384,768]{2,1,0:T(8,128)(2,1)}, u32[]{:S(2)}) copy-start(bf16[3,384,768]{2,1,0:T(8,128)(2,1)} %param.18) | copy-start | bytes 5308420
where the time goes:
time: 135 us; the launch traced here: 133 us
  blocking collectives  63.9 us (47%)
  local copies, waits for them, and re-layouts  24 us (18%)
  matrix products  13.5 us (10%)
  other arithmetic  11.9 us (9%)
  waiting for transfers between devices  10.2 us (8%)
  starting transfers between devices  9.03 us (7%)
    psum x3, blocking collectives, over_axes(): value = lax.psum(value, axis)  63.9 us
    dot_general x12, matrix products, conv_taps(): jnp.dot(window.reshape(-1, 3 * channels), kernel[row_tap].reshape(3 * cha...  12.7 us
    ppermute x2, waiting for transfers between devices, with_halo(): after = lax.ppermute(initial, axis, down)  8.01 us
    slice x5, local copies, waits for them, and re-layouts, conv_taps(): kernel[row_tap].reshape(3 * channels, -1)  6.51 us
    concatenate x6, other arithmetic, conv_taps(): jnp.concatenate([padded[:, row_tap:row_tap + row_count, col_tap:col_tap +...  6.42 us
    ppermute x2, starting transfers between devices, with_halo(): after = lax.ppermute(initial, axis, down)  5.14 us
    reshape x2, local copies, waits for them, and re-layouts, on_device(): result.astype(jnp.bfloat16)  4.54 us
    slice x4, local copies, waits for them, and re-layouts, conv_taps(): padded[:, row_tap:row_tap + row_count, col_tap:col_tap + col_count]  4.29 us
  transfers between devices with their start and end apart: 4, of which 3 were waited for; matrix products, arithmetic and copies ran while one was open for 8% of the time, Pallas kernels for 0%

commit v1 on v0

v1 whole, which is shorter than its diff:
```python
import jax
import jax.numpy as jnp
from jax import lax
from jax.sharding import PartitionSpec as P

GROUPS = 32
ROWS = "rows"
EPSILON = 1e-06


def sum_over_rows(value):
    spread_out = jnp.broadcast_to(value, (lax.axis_size(ROWS),) + value.shape)
    return jnp.sum(lax.all_to_all(spread_out, ROWS, 0, 0), axis=0)


def neighbours(value):
    devices = lax.axis_size(ROWS)
    up = [(i, i + 1) for i in range(devices - 1)]
    down = [(j, i) for i, j in up]
    return lax.ppermute(value, ROWS, up), lax.ppermute(value, ROWS, down)


def conv_taps(padded, kernel, row_count, col_count):
    channels = padded.shape[-1]
    total = jnp.zeros((padded.shape[0] * row_count * col_count, kernel.shape[-1]), jnp.float32)
    for row_tap in range(3):
        window = jnp.concatenate(
            [
                padded[:, row_tap : row_tap + row_count, col_tap : col_tap + col_count]
                for col_tap in range(3)
            ],
            axis=-1,
        )
        total = total + jnp.dot(
            window.reshape(-1, 3 * channels),
            kernel[row_tap].reshape(3 * channels, -1),
            preferred_element_type=jnp.float32,
        )
    return total


def temporal(block, time_cache, time_weight, time_bias):
    frame_count = block.shape[0]
    channels = block.shape[-1]
    joined = jnp.concatenate([time_cache, block], axis=0)
    window = jnp.concatenate(
        [joined[frame_tap : frame_tap + frame_count] for frame_tap in range(3)], axis=-1
    )
    mixed = (
        jnp.dot(
            window.reshape(-1, 3 * channels),
            time_weight.reshape(3 * channels, -1),
            preferred_element_type=jnp.float32,
        )
        + time_bias
    )
    mixed = mixed.astype(jnp.bfloat16).reshape(block.shape[:-1] + (2, channels))
    return jnp.moveaxis(mixed, 3, 1).reshape((2 * frame_count,) + block.shape[1:])


def on_device(
    latent,
    conv_cache,
    time_cache,
    norm_gain,
    norm_shift,
    conv_weight,
    conv_bias,
    time_weight,
    time_bias,
    up_weight,
    up_bias,
):
    frame_count, row_count, col_count, channels = latent.shape
    me, devices = lax.axis_index(ROWS), lax.axis_size(ROWS)
    raw = jnp.concatenate([latent, conv_cache], axis=0)
    raw_before, raw_after = neighbours(raw)
    signal = latent.astype(jnp.float32)
    grouped = signal.reshape(frame_count, row_count, col_count, GROUPS, channels // GROUPS)
    entries = float(frame_count * row_count * devices * col_count * (channels // GROUPS))
    sums = jnp.concatenate(
        [jnp.sum(grouped, axis=(0, 1, 2, 4)), jnp.sum(grouped * grouped, axis=(0, 1, 2, 4))]
    )
    sums = sum_over_rows(sums)
    center = sums[:GROUPS] / entries
    spread = sums[GROUPS:] / entries - center * center
    center = jnp.repeat(center, channels // GROUPS)
    scale = jnp.repeat(lax.rsqrt(spread + EPSILON), channels // GROUPS)
    raw = jnp.concatenate([raw_before, raw, raw_after], axis=1)
    wide = raw[:frame_count].astype(jnp.float32)
    active = jax.nn.silu((wide - center) * scale * norm_gain + norm_shift).astype(jnp.bfloat16)
    row = me * row_count + lax.broadcasted_iota(jnp.int32, (1, row_count + 2, 1, 1), 1)
    inside = (row >= 1) & (row <= devices * row_count)
    active = jnp.where(inside, active, jnp.zeros_like(active))
    joined = jnp.concatenate([raw[frame_count:], active], axis=0)
    padded = jnp.pad(joined, ((0, 0), (0, 0), (1, 1), (0, 0)))
    summed = conv_bias + jnp.zeros((frame_count * row_count * col_count, channels), jnp.float32)
    for frame_tap in range(3):
        summed = summed + conv_taps(
            padded[frame_tap : frame_tap + frame_count],
            conv_weight[frame_tap],
            row_count,
            col_count,
        )
    block = (signal + summed.reshape(signal.shape)).astype(jnp.bfloat16)
    doubled = temporal(block, time_cache, time_weight, time_bias)
    before, after = neighbours(doubled)
    upsampled = jnp.concatenate([before, doubled, doubled, after], axis=1)
    upsampled = jnp.repeat(upsampled, 2, axis=2)
    padded_up = jnp.pad(upsampled, ((0, 0), (0, 0), (1, 1), (0, 0)))
    result = conv_taps(padded_up, up_weight, 2 * row_count, 2 * col_count) + up_bias
    return result.astype(jnp.bfloat16).reshape(
        2 * frame_count, 2 * row_count, 2 * col_count, up_weight.shape[-1]
    )


def solution(mesh):
    placed = P("parts", ROWS, None, None)
    return jax.shard_map(
        on_device,
        mesh=mesh,
        in_specs=(placed,) * 3 + (P(),) * 8,
        out_specs=placed,
        check_vma=False,
    )
```

time: 135 us -> 135 us (level)
  blocking collectives: 63.9 us -> 0 us
  starting transfers between devices: 9.03 us -> 41.5 us
  local copies, waits for them, and re-layouts: 24 us -> 50.4 us
  waiting for transfers between devices: 10.2 us -> 14.5 us
    psum x3 -> x0, blocking collectives: 63.9 us -> none  [over_axes(): value = lax.psum(value, axis)]
    ppermute x4, starting transfers between devices: 9.03 us -> 29.2 us  [neighbours(): return (lax.ppermute(value, ROWS, up), lax.ppermute(value, ROWS, down))]
    all_to_all x0 -> x1, starting transfers between devices: none -> 12.3 us  [sum_over_rows(): return jnp.sum(lax.all_to_all(spread_out, ROWS, 0, 0), axis=0)]
    slice x4 -> x5, local copies, waits for them, and re-layouts: 4.29 us -> 13.5 us  [conv_taps(): padded[:, row_tap:row_tap + row_count, col_tap:col_tap + col_count]]
    reshape x0 -> x1, local copies, waits for them, and re-layouts: none -> 9.06 us  [on_device(): upsampled = jnp.repeat(upsampled, 2, axis=2)]
    all_to_all x0 -> x1, waiting for transfers between devices: none -> 8.02 us  [sum_over_rows(): return jnp.sum(lax.all_to_all(spread_out, ROWS, 0, 0), axis=0)]
    unnamed x27 -> x46, local copies, waits for them, and re-layouts: 3.04 us -> 7.69 us
    ppermute x4, waiting for transfers between devices: 10.2 us -> 6.48 us  [neighbours(): return (lax.ppermute(value, ROWS, up), lax.ppermute(value, ROWS, down))]
  transfers between devices with their start and end apart: 4 -> 5, of which waited for: 3 -> 3; matrix products, arithmetic and copies ran while one was open for 8% -> 10% of each run, Pallas kernels for 0% -> 0%
where the time goes in v1:
time: 135 us; the launch traced here: 133 us
  local copies, waits for them, and re-layouts  50.4 us (37%)
  starting transfers between devices  41.5 us (31%)
  waiting for transfers between devices  14.5 us (11%)
  matrix products  14.2 us (11%)
  other arithmetic  11.8 us (9%)
    ppermute x4, starting transfers between devices, neighbours(): return (lax.ppermute(value, ROWS, up), lax.ppermute(value, ROWS, down))  29.2 us
    slice x5, local copies, waits for them, and re-layouts, conv_taps(): padded[:, row_tap:row_tap + row_count, col_tap:col_tap + col_count]  13.5 us
    dot_general x12, matrix products, conv_taps(): jnp.dot(window.reshape(-1, 3 * channels), kernel[row_tap].reshape(3 * cha...  12.6 us
    all_to_all x1, starting transfers between devices, sum_over_rows(): return jnp.sum(lax.all_to_all(spread_out, ROWS, 0, 0), axis=0)  12.3 us
    reshape x1, local copies, waits for them, and re-layouts, on_device(): upsampled = jnp.repeat(upsampled, 2, axis=2)  9.06 us
    all_to_all x1, waiting for transfers between devices, sum_over_rows(): return jnp.sum(lax.all_to_all(spread_out, ROWS, 0, 0), axis=0)  8.02 us
    unnamed x46, local copies, waits for them, and re-layouts  7.69 us
    slice x5, local copies, waits for them, and re-layouts, conv_taps(): kernel[row_tap].reshape(3 * channels, -1)  6.72 us
  transfers between devices with their start and end apart: 5, of which 3 were waited for; matrix products, arithmetic and copies ran while one was open for 10% of the time, Pallas kernels for 0%

profile of v1, /device:TPU:33, one launch (start us, length us, event | category | flops | bytes accessed | tf_op | source)
XLA Modules:
  0.0 132.9 jit_solution(16993354151153600778)
XLA Ops:
  0.0 1.8 %constant_dynamic-update-slice_fusion.1 = bf16[4,1,160,384]{3,2,1,0:T(8,128)(2,1)} fusion(bf16[2,1,160,384]{3,2,1,0:T(8,128)(2,1)} %param.11), kind=kLoop, calls=%fused_computation.56 | loop fusion | bytes 491520
  1.8 1.7 %constant_dynamic-update-slice_fusion = bf16[4,1,160,384]{3,2,1,0:T(8,128)(2,1)} fusion(bf16[4,1,160,384]{3,2,1,0:T(8,128)(2,1)} %constant_dynamic-update-slice_fusion.1, bf16[2,1,160,384]{3,2,1,0:T(8,128)(2,1)} %param.12), kind=kLoop, calls=%fused_computation.55 | loop fusion | bytes 491520 | tf_op jit(solution)/shard_map/concatenate | solution.py:76
  3.5 4.6 %collective-permute-start = (bf16[4,1,160,384]{3,2,1,0:T(8,128)(2,1)}, bf16[4,1,160,384]{3,2,1,0:T(8,128)(2,1)}, u32[]{:S(2)}, u32[]{:S(2)}) collective-permute-start(bf16[4,1,160,384]{3,2,1,0:T(8,128)(2,1)} %constant_dynamic-update-slice_fusion), channel_id=1, source_target_pairs={{0,1},{1,2},{2,3},{3,4},{4,5},{5,6},{6,7},{7,8},{8,9},{9,10},{10,1... | collective-permute-start | bytes 1474568 | tf_op jit(solution)/shard_map/ppermute | solution.py:20
  8.1 19.8 %collective-permute-start.1 = (bf16[4,1,160,384]{3,2,1,0:T(8,128)(2,1)}, bf16[4,1,160,384]{3,2,1,0:T(8,128)(2,1)}, u32[]{:S(2)}, u32[]{:S(2)}) collective-permute-start(bf16[4,1,160,384]{3,2,1,0:T(8,128)(2,1)} %constant_dynamic-update-slice_fusion), channel_id=1, source_target_pairs={{1,0},{2,1},{3,2},{4,3},{5,4},{6,5},{7,6},{8,7},{9,8},{10,9},{11,1... | collective-permute-start | bytes 1474568 | tf_op jit(solution)/shard_map/ppermute | solution.py:20
  27.9 1.0 convert_reduce_fusion
  29.5 0.7 broadcast_in_dim.29
  30.1 12.3 %all-to-all-start = ((f32[128,1,64]{2,1,0:T(1,128)}), f32[128,1,64]{2,1,0:T(1,128)}, u32[]{:S(2)}, u32[]{:S(2)}) async-start(f32[128,1,64]{2,1,0:T(1,128)} %broadcast_in_dim.29), calls=%async_computation | async-start | bytes 131072 | tf_op jit(solution)/shard_map/all_to_all | solution.py:13
  42.4 5.4 %fusion.14 = (bf16[1,1,3,384,384]{4,3,2,1,0:T(8,128)(2,1)S(1)}, bf16[1,1,3,384,384]{4,3,2,1,0:T(8,128)(2,1)}, bf16[1,1,3,384,384]{4,3,2,1,0:T(8,128)(2,1)S(1)}, ...) fusion(bf16[3,3,3,384,384]{4,3,2,1,0:T(8,128)(2,1)} %param.16), kind=kLoop, calls=%fused_computation.79 | loop fusion | bytes 15925248 | tf_op jit(solution)/shard_map/slice | solution.py:36
  47.9 0.6 compare_and_fusion
  48.5 8.0 %all-to-all-done = f32[128,1,64]{2,1,0:T(1,128)} async-done(((f32[128,1,64]{2,1,0:T(1,128)}), f32[128,1,64]{2,1,0:T(1,128)}, u32[]{:S(2)}, u32[]{:S(2)}) %all-to-all-start) | async-done | bytes 32800 | tf_op jit(solution)/shard_map/all_to_all | solution.py:13
  56.5 1.0 reduce_sum.47
  58.1 0.7 mul.33
  58.8 0.7 broadcast_in_dim.30
  59.5 0.7 sub.13
  60.3 1.5 %pad_maximum_fusion.5 = bf16[4,3,160,384]{3,2,1,0:T(8,128)(2,1)S(1)} fusion(bf16[4,1,160,384]{3,2,1,0:T(8,128)(2,1)} %collective-permute-done.1, bf16[4,1,160,384]{3,2,1,0:T(8,128)(2,1)} %constant_dynamic-update-slice_fusion, bf16[4,1,160,384]{3,2,1,0:T(8,128)(2,1)} %collective-permute-done), kind=kLoop, calls=%fused_computation.21 | loop fusion | flops 1474560 | bytes 2949120 | tf_op jit(solution)/shard_map/concatenate | solution.py:89
  61.9 0.6 fusion.15
  63.9 1.0 copy-done.8
  64.9 0.6 fusion.19
  65.5 1.0 slice.287
  66.6 1.0 copy-done.7
  67.6 0.6 fusion.18
  68.2 1.0 slice.286
  69.3 1.0 copy-done.6
  70.3 0.6 fusion.17
  71.5 0.6 convolution_add_fusion.4
  72.3 1.0 copy-done.4
  73.3 0.6 convolution_add_fusion.6
  73.9 0.6 convolution_add_fusion.8
  75.0 0.6 fusion.3
  75.6 0.6 fusion.4
  76.3 0.6 fusion.5
  77.6 1.6 %fusion.2 = bf16[320,768]{1,0:T(8,128)(2,1)} fusion(bf16[320,1152]{1,0:T(8,128)(2,1)S(1)} %bitcast.103, bf16[1152,768]{1,0:T(8,128)(2,1)S(1)} %bitcast.72, f32[768]{0:T(1024)S(1)} %copy-done.19), kind=kOutput, calls=%fused_computation.24 | convolution fusion | flops 566722560 | bytes 3001344 | tf_op jit(solution)/shard_map/dot_general | solution.py:50
  79.2 1.2 reshape.116
  80.5 2.6 %collective-permute-start.2 = (bf16[4,1,160,384]{3,2,0,1:T(8,128)(2,1)S(1)}, bf16[4,1,160,384]{3,2,0,1:T(8,128)(2,1)S(1)}, u32[]{:S(2)}, u32[]{:S(2)}) collective-permute-start(bf16[4,1,160,384]{3,2,0,1:T(8,128)(2,1)S(1)} %bitcast.97), channel_id=1, source_target_pairs={{0,1},{1,2},{2,3},{3,4},{4,5},{5,6},{6,7},{7,8},{8,9},{9,10},{10,1... | collective-permute-start | bytes 1474568 | tf_op jit(solution)/shard_map/ppermute | solution.py:20
  83.1 2.2 %collective-permute-start.3 = (bf16[4,1,160,384]{3,2,0,1:T(8,128)(2,1)S(1)}, bf16[4,1,160,384]{3,2,0,1:T(8,128)(2,1)S(1)}, u32[]{:S(2)}, u32[]{:S(2)}) collective-permute-start(bf16[4,1,160,384]{3,2,0,1:T(8,128)(2,1)S(1)} %bitcast.98), channel_id=1, source_target_pairs={{1,0},{2,1},{3,2},{4,3},{5,4},{6,5},{7,6},{8,7},{9,8},{10,9},{11,1... | collective-permute-start | bytes 1474568 | tf_op jit(solution)/shard_map/ppermute | solution.py:20
  86.8 2.0 %collective-permute-done.2 = bf16[4,1,160,384]{3,2,0,1:T(8,128)(2,1)S(1)} collective-permute-done((bf16[4,1,160,384]{3,2,0,1:T(8,128)(2,1)S(1)}, bf16[4,1,160,384]{3,2,0,1:T(8,128)(2,1)S(1)}, u32[]{:S(2)}, u32[]{:S(2)}) %collective-permute-start.2) | collective-permute-done | bytes 491552 | tf_op jit(solution)/shard_map/ppermute | solution.py:20
  88.9 4.4 %collective-permute-done.3 = bf16[4,1,160,384]{3,2,0,1:T(8,128)(2,1)S(1)} collective-permute-done((bf16[4,1,160,384]{3,2,0,1:T(8,128)(2,1)S(1)}, bf16[4,1,160,384]{3,2,0,1:T(8,128)(2,1)S(1)}, u32[]{:S(2)}, u32[]{:S(2)}) %collective-permute-start.3) | collective-permute-done | bytes 491552 | tf_op jit(solution)/shard_map/ppermute | solution.py:20
  93.8 3.5 %broadcast_in_dim.33 = bf16[4,4,160,2,384]{4,3,2,1,0:T(2,128)(2,1)} broadcast(bf16[4,4,160,384]{3,2,1,0:T(8,128)(2,1)S(1)} %copy.31), dimensions={0,1,2,4} | broadcast | bytes 5898240 | tf_op jit(solution)/shard_map/broadcast_in_dim | solution.py:109
  97.3 9.1 %reshape.118 = bf16[4,4,320,384]{3,2,1,0:T(8,128)(2,1)} reshape(bf16[4,4,160,2,384]{4,3,2,1,0:T(2,128)(2,1)} %broadcast_in_dim.33) | data formatting | bytes 7864320 | tf_op jit(solution)/shard_map/reshape | solution.py:109
  106.4 10.7 %pad_slice_fusion.7 = (bf16[4,2,320,384]{3,2,1,0:T(8,128)(2,1)S(1)}, bf16[4,2,320,384]{3,2,1,0:T(8,128)(2,1)S(1)}, bf16[4,2,320,384]{3,2,1,0:T(8,128)(2,1)S(1)},...) fusion(bf16[4,4,320,384]{3,2,1,0:T(8,128)(2,1)} %reshape.118), kind=kLoop, calls=%fused_computation.16 | loop fusion | bytes 27525120 | tf_op jit(solution)/shard_map/slice | solution.py:29
  117.0 2.8 %pad_maximum_fusion = bf16[4,2,320,1152]{3,2,1,0:T(8,128)(2,1)S(1)} fusion(bf16[4,2,320,384]{3,2,1,0:T(8,128)(2,1)S(1)} %get-tuple-element.17, bf16[4,2,320,384]{3,2,1,0:T(8,128)(2,1)S(1)} %get-tuple-element.23, bf16[4,2,320,384]{3,2,1,0:T(8,128)(2,1)} %get-tuple-element.24), kind=kLoop, calls=%fused_computation | loop fusion | flops 17694720 | bytes 11796480 | tf_op jit(solution)/shard_map/concatenate | solution.py:27
  119.8 2.1 %fusion.20 = f32[2560,192]{0,1:T(8,128)S(1)} fusion(bf16[2560,1152]{1,0:T(8,128)(2,1)S(1)} %bitcast.74, bf16[1152,192]{0,1:T(8,128)(2,1)S(1)} %bitcast.102), kind=kOutput, calls=%fused_computation.85 | convolution fusion | flops 1132462080 | bytes 8306688 | tf_op jit(solution)/shard_map/dot_general | solution.py:34
  121.9 1.0 pad_maximum_fusion.2
  123.0 1.0 pad_maximum_fusion.1
  124.0 2.1 %convolution_add_fusion.1 = f32[2560,192]{0,1:T(8,128)S(1)} fusion(f32[2560,192]{0,1:T(8,128)S(1)} %fusion.20, bf16[2560,1152]{1,0:T(8,128)(2,1)S(1)} %bitcast.73, bf16[1152,192]{0,1:T(8,128)(2,1)S(1)} %bitcast.101), kind=kOutput, calls=%fused_computation.5 | convolution fusion | flops 1132953600 | bytes 10272768 | tf_op jit(solution)/shard_map/dot_general | solution.py:34
  126.2 3.0 %fusion.1 = bf16[2560,192]{0,1:T(8,128)(2,1)} fusion(f32[2560,192]{0,1:T(8,128)S(1)} %convolution_add_fusion.1, bf16[2560,1152]{1,0:T(8,128)(2,1)S(1)} %bitcast.75, bf16[1152,192]{0,1:T(8,128)(2,1)S(1)} %bitcast.104, f32[192]{0:T(256)S(1)} %copy-done.20), kind=kOutput, calls=%fused_computation.6 | convolution fusion | flops 1133936640 | bytes 9290496 | tf_op jit(solution)/shard_map/dot_general | solution.py:34
  129.2 2.5 %reshape.122 = bf16[4,2,320,192]{2,1,0,3:T(2,128)(2,1)S(1)} reshape(bf16[2560,192]{0,1:T(8,128)(2,1)} %fusion.1) | data formatting | bytes 1966080 | tf_op jit(solution)/shard_map/reshape | solution.py:112
  131.7 1.2 copy.35
  (68 shorter events, 6.8 us)
Async XLA Ops:
  0.0 77.4 %copy-start = (bf16[3,384,768]{2,1,0:T(8,128)(2,1)S(1)}, bf16[3,384,768]{2,1,0:T(8,128)(2,1)}, u32[]{:S(2)}) copy-start(bf16[3,384,768]{2,1,0:T(8,128)(2,1)} %param.18) | copy-start | bytes 5308420
  3.5 56.8 %collective-permute-start = (bf16[4,1,160,384]{3,2,1,0:T(8,128)(2,1)}, bf16[4,1,160,384]{3,2,1,0:T(8,128)(2,1)}, u32[]{:S(2)}, u32[]{:S(2)}) collective-permute-start(bf16[4,1,160,384]{3,2,1,0:T(8,128)(2,1)} %constant_dynamic-update-slice_fusion), channel_id=1, source_target_pairs={{0,1},{1,2},{2,3},{3,4},{4,5},{5,6},{6,7},{7,8},{8,9},{9,10},{10,1... | collective-permute-start | bytes 1474568 | tf_op jit(solution)/shard_map/ppermute | solution.py:20
  8.1 52.2 %collective-permute-start.1 = (bf16[4,1,160,384]{3,2,1,0:T(8,128)(2,1)}, bf16[4,1,160,384]{3,2,1,0:T(8,128)(2,1)}, u32[]{:S(2)}, u32[]{:S(2)}) collective-permute-start(bf16[4,1,160,384]{3,2,1,0:T(8,128)(2,1)} %constant_dynamic-update-slice_fusion), channel_id=1, source_target_pairs={{1,0},{2,1},{3,2},{4,3},{5,4},{6,5},{7,6},{8,7},{9,8},{10,9},{11,1... | collective-permute-start | bytes 1474568 | tf_op jit(solution)/shard_map/ppermute | solution.py:20
  30.1 26.3 %all-to-all-start = ((f32[128,1,64]{2,1,0:T(1,128)}), f32[128,1,64]{2,1,0:T(1,128)}, u32[]{:S(2)}, u32[]{:S(2)}) async-start(f32[128,1,64]{2,1,0:T(1,128)} %broadcast_in_dim.29), calls=%async_computation | async-start | bytes 131072 | tf_op jit(solution)/shard_map/all_to_all | solution.py:13
  60.2 1.6 %copy-start.13 = (f32[384]{0:T(512)S(1)}, f32[384]{0:T(512)}, u32[]{:S(2)}) copy-start(f32[384]{0:T(512)} %mul.33) | copy-start | bytes 4612
  60.2 1.6 %copy-start.14 = (f32[384]{0:T(512)S(1)}, f32[384]{0:T(512)}, u32[]{:S(2)}) copy-start(f32[384]{0:T(512)} %sub.13) | copy-start | bytes 4612
  60.2 1.6 %copy-start.15 = (f32[384]{0:T(512)S(1)}, f32[384]{0:T(512)}, u32[]{:S(2)}) copy-start(f32[384]{0:T(512)} %param.15) | copy-start | bytes 4612
  60.2 1.6 %copy-start.16 = (f32[384]{0:T(512)S(1)}, f32[384]{0:T(512)}, u32[]{:S(2)}) copy-start(f32[384]{0:T(512)} %param.14) | copy-start | bytes 4612
  60.3 1.6 %copy-start.18 = (pred[3]{0:T(512)(128)(4,1)S(1)}, pred[3]{0:T(512)(128)(4,1)}, u32[]{:S(2)}) copy-start(pred[3]{0:T(512)(128)(4,1)} %compare_and_fusion) | copy-start | bytes 13
  63.7 1.2 copy-start.8
  66.4 1.2 copy-start.7
  66.6 2.6 %copy-start.11 = (bf16[2,1,160,384]{3,2,1,0:T(8,128)(2,1)S(1)}, bf16[2,1,160,384]{3,2,1,0:T(8,128)(2,1)}, u32[]{:S(2)}) copy-start(bf16[2,1,160,384]{3,2,1,0:T(8,128)(2,1)} %param.12) | copy-start | bytes 737284
  69.2 1.2 copy-start.6
  70.3 1.2 copy-start.5
  72.1 1.2 copy-start.4
  72.2 1.6 %copy-start.3 = (bf16[1,1,3,384,384]{4,3,2,1,0:T(8,128)(2,1)S(1)}, bf16[1,1,3,384,384]{4,3,2,1,0:T(8,128)(2,1)}, u32[]{:S(2)}) copy-start(bf16[1,1,3,384,384]{4,3,2,1,0:T(8,128)(2,1)} %get-tuple-element.13) | copy-start | bytes 2654212
  73.9 1.2 copy-start.2
  73.9 1.2 copy-start.17
  76.2 0.9 copy-start.9
  76.3 1.1 copy-start.12
  76.9 0.7 copy-start.19
  79.2 6.1 %copy-start.10 = (bf16[3,3,384,192]{2,3,1,0:T(8,128)(2,1)S(1)}, bf16[3,3,384,192]{2,3,1,0:T(8,128)(2,1)}, u32[]{:S(2)}) copy-start(bf16[3,3,384,192]{2,3,1,0:T(8,128)(2,1)} %param.20) | copy-start | bytes 3981316
  80.5 8.4 %collective-permute-start.2 = (bf16[4,1,160,384]{3,2,0,1:T(8,128)(2,1)S(1)}, bf16[4,1,160,384]{3,2,0,1:T(8,128)(2,1)S(1)}, u32[]{:S(2)}, u32[]{:S(2)}) collective-permute-start(bf16[4,1,160,384]{3,2,0,1:T(8,128)(2,1)S(1)} %bitcast.97), channel_id=1, source_target_pairs={{0,1},{1,2},{2,3},{3,4},{4,5},{5,6},{6,7},{7,8},{8,9},{9,10},{10,1... | collective-permute-start | bytes 1474568 | tf_op jit(solution)/shard_map/ppermute | solution.py:20
  83.1 10.2 %collective-permute-start.3 = (bf16[4,1,160,384]{3,2,0,1:T(8,128)(2,1)S(1)}, bf16[4,1,160,384]{3,2,0,1:T(8,128)(2,1)S(1)}, u32[]{:S(2)}, u32[]{:S(2)}) collective-permute-start(bf16[4,1,160,384]{3,2,0,1:T(8,128)(2,1)S(1)} %bitcast.98), channel_id=1, source_target_pairs={{1,0},{2,1},{3,2},{4,3},{5,4},{6,5},{7,6},{8,7},{9,8},{10,9},{11,1... | collective-permute-start | bytes 1474568 | tf_op jit(solution)/shard_map/ppermute | solution.py:20
  124.0 2.1 %copy-start.20 = (f32[192]{0:T(256)S(1)}, f32[192]{0:T(256)}, u32[]{:S(2)}) copy-start(f32[192]{0:T(256)} %param.21) | copy-start | bytes 2308
  129.2 3.7 %copy-start.1 = (bf16[3,384,768]{2,1,0:T(8,128)(2,1)S(1)}, bf16[3,384,768]{2,1,0:T(8,128)(2,1)}, u32[]{:S(2)}) copy-start(bf16[3,384,768]{2,1,0:T(8,128)(2,1)} %param.18) | copy-start | bytes 5308420

commit v2 on v1

v2 whole, which is shorter than its diff:
```python
import functools

import jax
import jax.numpy as jnp
from jax import lax
from jax.experimental import pallas as pl
from jax.experimental.pallas import tpu as pltpu
from jax.sharding import PartitionSpec as P

GROUPS = 32
ROWS = "rows"
EPSILON = 1e-06
LANES = 128
F32 = jnp.float32
BF16 = jnp.bfloat16
ALL_VMEM = 67043328
VMEM = pl.BlockSpec(memory_space=pltpu.VMEM)
HBM = pl.BlockSpec(memory_space=pltpu.HBM)
SMEM = pl.BlockSpec(memory_space=pltpu.SMEM)


def group_matrix(channels, first, flip):
    size = channels // GROUPS
    shape = (LANES, channels) if flip else (channels, LANES)
    lane = lax.broadcasted_iota(jnp.int32, shape, 0 if flip else 1) - first
    channel = lax.broadcasted_iota(jnp.int32, shape, 1 if flip else 0)
    return ((channel >= lane * size) & (channel < lane * size + size) & (lane >= 0)).astype(F32)


def exact_dot(a, b):
    return jnp.dot(a, b, preferred_element_type=F32, precision=lax.Precision.HIGHEST)


def pack_kernel(latent, conv_cache, time_cache, near, far, sums, sems):
    frames, _, _, channels = latent.shape
    jobs = []
    for n, source in enumerate((latent, conv_cache, time_cache)):
        for t in range(frames):
            jobs.append((source.at[t, 0], near.at[n * frames + t]))
            if n < 2:
                jobs.append((source.at[t, 0], far.at[n * frames + t]))
    copies = [pltpu.make_async_copy(a, b, sems.at[i]) for i, (a, b) in enumerate(jobs)]
    for copy in copies:
        copy.start()
    total = jnp.zeros((8, channels), F32)
    square = jnp.zeros((8, channels), F32)
    for t in range(frames):
        copies[2 * t].wait()
        wide = near[t].astype(F32).reshape(-1, 8, channels)
        total = total + jnp.sum(wide, axis=0)
        square = square + jnp.sum(wide * wide, axis=0)
    grouped = exact_dot(total, group_matrix(channels, 0, False))
    grouped = grouped + exact_dot(square, group_matrix(channels, GROUPS, False))
    row = jnp.sum(grouped, axis=0, keepdims=True)
    sums[...] = jnp.broadcast_to(row[None], sums.shape)
    for copy in copies[1 : 2 * frames : 2] + copies[2 * frames :]:
        copy.wait()


def shifted(value, step):
    length = value.shape[0]
    rolled = pltpu.roll(value, (-step) % length, 0)
    row = lax.broadcasted_iota(jnp.int32, value.shape, 0)
    return jnp.where((row + step >= 0) & (row + step < length), rolled, 0.0)


def main_kernel(entries, place, *refs):
    n_in = 10
    far_refs, out = refs[:n_in], refs[n_in]
    near_refs, (taps, acc, time_taps, up_taps, sems) = refs[n_in + 1 : 2 * n_in + 1], refs[2 * n_in + 1 :]
    stats, vectors, own, before, after, before_far, after_far, weight, time_weight, up_weight = near_refs
    channels = own.shape[-1]
    width = own.shape[1]
    frames = own.shape[0] // 3
    copies = []
    for n in range(n_in):
        if n != 7:
            copies.append(pltpu.make_async_copy(far_refs[n], near_refs[n], sems.at[n]))
    taps_in = []
    for c in range(3):
        for a in range(3):
            for b in range(3):
                rows = pl.ds((a * 3 + b) * channels, channels)
                taps_in.append(
                    pltpu.make_async_copy(
                        far_refs[7].at[a, b, c], weight.at[c, rows, :], sems.at[n_in + len(taps_in)]
                    )
                )
    for copy in copies[:7] + taps_in + copies[7:]:
        copy.start()
    copies[0].wait()
    copies[1].wait()
    gain, shift, conv_bias = (vectors[n : n + 1, :channels] for n in range(3))
    time_bias, up_bias = vectors[3:4, :], vectors[4:5, : 2 * out.shape[-2]]
    me, last = place[0], place[1]
    total = jnp.sum(stats[:, 0, :], axis=0, keepdims=True)
    total = jnp.broadcast_to(total, (8, LANES))
    center = exact_dot(total, group_matrix(channels, 0, True))[:1] / entries
    spread = exact_dot(total, group_matrix(channels, GROUPS, True))[:1] / entries
    spread = spread - center * center
    scale = lax.rsqrt(spread + EPSILON) * gain
    offset = shift

    sources = (before_far, before, own, after, after_far)
    rows_of = lambda t, r: pl.ds((t * 3 + r) * width, width)

    def place_row(frame, r, value):
        for a in range(3):
            t = frame - a
            if 0 <= t < frames:
                for b in range(3):
                    if 0 <= r - b < 3:
                        k = (a * 3 + b) * channels
                        taps[rows_of(t, r - b), k : k + channels] = value

    for copy in copies[2:7]:
        copy.wait()
    for r in range(5):
        row = me + (r - 2)
        inside = ((row >= 0) & (row <= last)).astype(F32)
        for t in range(frames):
            place_row(t, r, sources[r][frames + t])
            value = sources[r][t].astype(F32)
            value = (value - center) * scale + offset
            value = value / (1.0 + jnp.exp(-value)) * inside
            place_row(frames + t, r, value.astype(BF16))

    for c in range(3):
        for copy in taps_in[c * 9 : c * 9 + 9]:
            copy.wait()
        acc[c] = jnp.dot(taps[...], weight[c], preferred_element_type=F32)

    for r in range(3):
        for t in range(frames):
            rows = rows_of(t, r)
            value = acc[1, rows, :] + shifted(acc[0, rows, :], -1) + shifted(acc[2, rows, :], 1)
            value = value + conv_bias + sources[r + 1][t].astype(F32)
            block = value.astype(BF16)
            cached = sources[r + 1][2 * frames + t]
            for frame, item in ((t, cached), (frames + t, block)):
                for a in range(3):
                    if 0 <= frame - a < frames:
                        k = a * channels
                        time_taps[rows_of(frame - a, r), k : k + channels] = item

    copies[7].wait()
    for t in range(frames):
        for r in range(3):
            row = me + (r - 1)
            inside = ((row >= 0) & (row <= last)).astype(F32)
            weights = time_weight[...].reshape(3 * channels, 2 * channels)
            mixed = jnp.dot(time_taps[rows_of(t, r), :], weights, preferred_element_type=F32)
            mixed = ((mixed + time_bias) * inside).astype(BF16)
            for k in range(2):
                part = mixed[:, k * channels : (k + 1) * channels]
                lines = pl.ds((2 * t + k) * width, width)
                for p in range(2):
                    if 0 <= r - p < 2:
                        up_taps[p, lines, (r - p) * channels : (r - p + 1) * channels] = part

    copies[8].wait()
    outputs = out.shape[-2]
    lane = lax.broadcasted_iota(jnp.int32, (width, 2 * outputs), 1)
    low = lax.broadcasted_iota(jnp.int32, (width, 2 * width), 0)
    high = lax.broadcasted_iota(jnp.int32, (width, 2 * width), 1)
    spread_even = (high == 2 * low).astype(F32).astype(BF16)
    spread_odd = (high == 2 * low + 1).astype(F32).astype(BF16)
    for f in range(2 * frames):
        for p in range(2):
            lines = pl.ds(f * width, width)
            value = dot_nt(up_taps[p, lines, :], up_weight[p])
            inner, outer = value[:, : 2 * outputs], value[:, 2 * outputs :]
            outer = jnp.where(lane < outputs, shifted(outer, -1), shifted(outer, 1))
            value = (inner + outer + up_bias).T.astype(BF16)
            even = jnp.dot(value[:outputs], spread_even, preferred_element_type=F32)
            odd = jnp.dot(value[outputs:], spread_odd, preferred_element_type=F32)
            out[f, p] = (even + odd).astype(BF16)


def dot_nt(a, b):
    return lax.dot_general(a, b, (((1,), (1,)), ((), ())), preferred_element_type=F32)


def small_kernel(up_weight, gain, shift, conv_bias, time_bias, up_bias, out, vectors):
    outputs, channels = up_weight.shape[2:]
    for n, item in enumerate((gain, shift, conv_bias)):
        vectors[n : n + 1, :channels] = item[...].reshape(1, -1)
    vectors[3:4, :] = time_bias[...].reshape(1, -1)
    vectors[4:5, :outputs] = up_bias[...].reshape(1, -1)
    vectors[4:5, outputs : 2 * outputs] = up_bias[...].reshape(1, -1)
    columns = lambda b: [up_weight[b, c].astype(F32) for c in range(3)]
    first, middle, final = columns(0), columns(1), columns(2)
    add = lambda u, v: [x + y for x, y in zip(u, v)]
    by_row = ((first, add(middle, final)), (add(first, middle), final))
    for p in range(2):
        for j in range(2):
            v = by_row[p][j]
            for n, item in enumerate((v[1] + v[2], v[0] + v[1], v[0], v[2])):
                rows = pl.ds(n * outputs, outputs)
                out[p, rows, j * channels : (j + 1) * channels] = item.astype(BF16)


def moved(value, step):
    devices = lax.axis_size(ROWS)
    pairs = [(i, i + step) for i in range(devices) if 0 <= i + step < devices]
    return lax.ppermute(value, ROWS, pairs)


def on_device(
    latent,
    conv_cache,
    time_cache,
    norm_gain,
    norm_shift,
    conv_weight,
    conv_bias,
    time_weight,
    time_bias,
    up_weight,
    up_bias,
):
    frames, row_count, width, channels = latent.shape
    outputs = up_weight.shape[-1]
    me, devices = lax.axis_index(ROWS), lax.axis_size(ROWS)
    near, far, sums = pl.pallas_call(
        pack_kernel,
        out_shape=(
            jax.ShapeDtypeStruct((3 * frames, width, channels), BF16),
            jax.ShapeDtypeStruct((2 * frames, width, channels), BF16),
            jax.ShapeDtypeStruct((devices, 1, LANES), F32),
        ),
        in_specs=[HBM] * 3,
        out_specs=(VMEM,) * 3,
        scratch_shapes=[pltpu.SemaphoreType.DMA((5 * frames,))],
        compiler_params=pltpu.CompilerParams(vmem_limit_bytes=ALL_VMEM),
        cost_estimate=pl.CostEstimate(flops=2**21, bytes_accessed=2**21, transcendentals=0),
        name="pack",
    )(latent, conv_cache, time_cache)
    before_far, after_far = moved(far, 2), moved(far, -2)
    before, after = moved(near, 1), moved(near, -1)
    stats = lax.all_to_all(sums, ROWS, 0, 0)
    entries = float(frames * row_count * devices * width * (channels // GROUPS))
    place = jnp.stack([me, jnp.int32(devices - 1)]).astype(jnp.int32)
    subpixel, vectors = pl.pallas_call(
        small_kernel,
        out_shape=(
            jax.ShapeDtypeStruct((2, 4 * outputs, 2 * channels), BF16),
            jax.ShapeDtypeStruct((8, 2 * channels), F32),
        ),
        in_specs=[VMEM] * 6,
        out_specs=(VMEM, VMEM),
        compiler_params=pltpu.CompilerParams(vmem_limit_bytes=ALL_VMEM),
        cost_estimate=pl.CostEstimate(flops=2**21, bytes_accessed=2**22, transcendentals=0),
        name="small",
    )(jnp.swapaxes(up_weight, 2, 3), norm_gain, norm_shift, conv_bias, time_bias, up_bias)
    inputs = (stats, vectors, near, before, after, before_far, after_far, conv_weight, time_weight, subpixel)
    flops = 2 * frames * 3 * width * channels * channels * 27
    out = pl.pallas_call(
        functools.partial(main_kernel, entries),
        out_shape=jax.ShapeDtypeStruct((2 * frames, 2, outputs, 2 * width), BF16),
        in_specs=[SMEM] + [HBM] * 10,
        out_specs=VMEM,
        scratch_shapes=[
            *[pltpu.VMEM(item.shape, item.dtype) for item in inputs[:7]],
            pltpu.VMEM((3, 9 * channels, channels), BF16),
            *[pltpu.VMEM(item.shape, item.dtype) for item in inputs[8:]],
            pltpu.VMEM((frames * 3 * width, 9 * channels), BF16),
            pltpu.VMEM((3, frames * 3 * width, channels), F32),
            pltpu.VMEM((frames * 3 * width, 3 * channels), BF16),
            pltpu.VMEM((2, 2 * frames * width, 2 * channels), BF16),
            pltpu.SemaphoreType.DMA((len(inputs) + 27,)),
        ],
        compiler_params=pltpu.CompilerParams(vmem_limit_bytes=ALL_VMEM),
        cost_estimate=pl.CostEstimate(flops=flops, bytes_accessed=2**24, transcendentals=2**20),
        name="decode",
    )(place, *inputs)
    return jnp.swapaxes(out, 2, 3)


def solution(mesh):
    placed = P("parts", ROWS, None, None)
    return jax.shard_map(
        on_device,
        mesh=mesh,
        in_specs=(placed,) * 3 + (P(),) * 8,
        out_specs=placed,
        check_vma=False,
    )
```

time: 135 us -> 88.9 us (0.66); the launches traced: 133 us -> 88.6 us
  local copies, waits for them, and re-layouts: 50.4 us -> 0 us
  Pallas kernels: 0 us -> 30.3 us
  matrix products: 14.2 us -> 0 us
  other arithmetic: 11.8 us -> 0.61 us
  starting transfers between devices: 41.5 us -> 47.8 us
  waiting for transfers between devices: 14.5 us -> 9.74 us
    pallas_call x0 -> x3, Pallas kernels: none -> 30.3 us  [the longest x1 24.2 us: on_device(): pl.pallas_call(functools.partial(main_kernel, entries), out_shape=jax.Sha...]
    slice x10 -> x0, local copies, waits for them, and re-layouts: 20.2 us -> none  [the longest x5 13.5 us: conv_taps(): padded[:, row_tap:row_tap + row_count, col_tap:col_tap + col_count]]
    dot_general x13 -> x0, matrix products: 14.2 us -> none  [the longest x12 12.6 us: conv_taps(): jnp.dot(window.reshape(-1, 3 * channels), kernel[row_tap].reshape(3 * cha...]
    reshape x5 -> x0, local copies, waits for them, and re-layouts: 14 us -> none  [the longest x1 9.06 us: on_device(): upsampled = jnp.repeat(upsampled, 2, axis=2)]
    concatenate x14 -> x0, other arithmetic: 7.74 us -> none  [the longest x8 5.47 us: conv_taps(): jnp.concatenate([padded[:, row_tap:row_tap + row_count, col_tap:col_tap +...]
    unnamed x46 -> x0, local copies, waits for them, and re-layouts: 7.69 us -> none
    ppermute x4, waiting for transfers between devices: 6.48 us -> 0.01 us  [moved(): return lax.ppermute(value, ROWS, pairs)]
    all_to_all x1, starting transfers between devices: 12.3 us -> 17.3 us  [on_device(): stats = lax.all_to_all(sums, ROWS, 0, 0)]
  transfers between devices with their start and end apart: 5 -> 5, of which waited for: 3 -> 1; matrix products, arithmetic and copies ran while one was open for 10% -> 1% of each run, Pallas kernels for 0% -> 4%
where the time goes in v2:
time: 88.9 us; the launch traced here: 88.6 us
  starting transfers between devices  47.8 us (54%)
  Pallas kernels  30.3 us (34%)
  waiting for transfers between devices  9.74 us (11%)
    ppermute x4, starting transfers between devices, moved(): return lax.ppermute(value, ROWS, pairs)  30.5 us
    pallas_call x1, Pallas kernels, on_device(): pl.pallas_call(functools.partial(main_kernel, entries), out_shape=jax.Sha...  24.2 us
    all_to_all x1, starting transfers between devices, on_device(): stats = lax.all_to_all(sums, ROWS, 0, 0)  17.3 us
    all_to_all x1, waiting for transfers between devices, on_device(): stats = lax.all_to_all(sums, ROWS, 0, 0)  9.73 us
    pallas_call x1, Pallas kernels, on_device(): pl.pallas_call(small_kernel, out_shape=(jax.ShapeDtypeStruct((2, 4 * outp...  3.49 us
    pallas_call x1, Pallas kernels, on_device(): pl.pallas_call(pack_kernel, out_shape=(jax.ShapeDtypeStruct((3 * frames,...  2.63 us
  transfers between devices with their start and end apart: 5, of which 1 were waited for; matrix products, arithmetic and copies ran while one was open for 1% of the time, Pallas kernels for 4%

profile of v2, /device:TPU:33, one launch (start us, length us, event | category | flops | bytes accessed | tf_op | source)
XLA Modules:
  0.0 88.6 jit_solution(4938972291087652967)
XLA Ops:
  0.0 2.6 %pack.1 = (bf16[6,160,384]{2,1,0:T(8,128)(2,1)}, bf16[4,160,384]{2,1,0:T(8,128)(2,1)}, f32[128,1,128]{2,1,0:T(1,128)}) custom-call(bf16[2,1,160,384]{3,2,1,0:T(8,128)(2,1)} %latent.1, bf16[2,1,160,384]{3,2,1,0:T(8,128)(2,1)} %conv_cache.1, bf16[2,1,160,384]{3,2,1,0:T(8,128)(2,1)} %time_cache.1), custom_call_target="tpu_custom_call" | custom-call | flops 2097152 | bytes 2097152 | tf_op jit(solution)/shard_map/pack/pallas_call | solution.py:225
  2.6 22.4 %collective-permute-start.1 = (bf16[6,160,384]{2,1,0:T(8,128)(2,1)}, bf16[6,160,384]{2,1,0:T(8,128)(2,1)}, u32[]{:S(2)}, u32[]{:S(2)}) collective-permute-start(bf16[6,160,384]{2,1,0:T(8,128)(2,1)} %get-tuple-element.12.refs_2_), channel_id=1, source_target_pairs={{1,0},{2,1},{3,2},{4,3},{5,4},{6,5},{7,6},{8,7},{9,8},{10,9},{11,1... | collective-permute-start | bytes 2211848 | tf_op jit(solution)/shard_map/ppermute | solution.py:206
  25.0 2.0 %collective-permute-start = (bf16[6,160,384]{2,1,0:T(8,128)(2,1)}, bf16[6,160,384]{2,1,0:T(8,128)(2,1)}, u32[]{:S(2)}, u32[]{:S(2)}) collective-permute-start(bf16[6,160,384]{2,1,0:T(8,128)(2,1)} %get-tuple-element.12.refs_2_), channel_id=1, source_target_pairs={{0,1},{1,2},{2,3},{3,4},{4,5},{5,6},{6,7},{7,8},{8,9},{9,10},{10,1... | collective-permute-start | bytes 2211848 | tf_op jit(solution)/shard_map/ppermute | solution.py:206
  27.0 1.3 %collective-permute-start.3 = (bf16[4,160,384]{2,1,0:T(8,128)(2,1)}, bf16[4,160,384]{2,1,0:T(8,128)(2,1)}, u32[]{:S(2)}, u32[]{:S(2)}) collective-permute-start(bf16[4,160,384]{2,1,0:T(8,128)(2,1)} %get-tuple-element.13), channel_id=1, source_target_pairs={{2,0},{3,1},{4,2},{5,3},{6,4},{7,5},{8,6},{9,7},{10,8},{11,9},{12,... | collective-permute-start | bytes 1474568 | tf_op jit(solution)/shard_map/ppermute | solution.py:206
  28.3 4.8 %collective-permute-start.2 = (bf16[4,160,384]{2,1,0:T(8,128)(2,1)}, bf16[4,160,384]{2,1,0:T(8,128)(2,1)}, u32[]{:S(2)}, u32[]{:S(2)}) collective-permute-start(bf16[4,160,384]{2,1,0:T(8,128)(2,1)} %get-tuple-element.13), channel_id=1, source_target_pairs={{0,2},{1,3},{2,4},{3,5},{4,6},{5,7},{6,8},{7,9},{8,10},{9,11},{10,... | collective-permute-start | bytes 1474568 | tf_op jit(solution)/shard_map/ppermute | solution.py:206
  33.1 17.3 %all-to-all-start = ((f32[128,1,128]{2,1,0:T(1,128)}), f32[128,1,128]{2,1,0:T(1,128)}, u32[]{:S(2)}, u32[]{:S(2)}) async-start(f32[128,1,128]{2,1,0:T(1,128)} %get-tuple-element.10), calls=%async_computation | async-start | bytes 131072 | tf_op jit(solution)/shard_map/all_to_all | solution.py:241
  50.5 3.5 %small.1 = (bf16[2,768,768]{2,1,0:T(8,128)(2,1)}, f32[8,768]{1,0:T(8,128)}) custom-call(bf16[3,3,192,384]{3,2,1,0:T(8,128)(2,1)} %bitcast.3, f32[384]{0:T(512)} %gain.1, f32[384]{0:T(512)} %shift.1, f32[384]{0:T(512)} %conv_bias.1, f32[768]{0:T(1024)} %time_bias.1, f32[192]{0:T(256)} %up_bias.1), custom_call_target="tpu_custom_call" | custom-call | flops 2097152 | bytes 4194304 | tf_op jit(solution)/shard_map/small/pallas_call | solution.py:244
  54.0 0.6 pad_add_fusion.place
  54.6 9.7 %all-to-all-done.refs_0_ = f32[128,1,128]{2,1,0:T(1,128)} async-done(((f32[128,1,128]{2,1,0:T(1,128)}), f32[128,1,128]{2,1,0:T(1,128)}, u32[]{:S(2)}, u32[]{:S(2)}) %all-to-all-start) | async-done | bytes 65568 | tf_op jit(solution)/shard_map/all_to_all | solution.py:241
  64.3 0.0 collective-permute-done.3.refs_6_
  64.3 0.0 collective-permute-done.2.refs_5_
  64.3 0.0 collective-permute-done.1.refs_4_
  64.3 0.0 collective-permute-done.refs_3_
  64.3 24.2 %decode.1 = bf16[4,2,192,320]{3,2,1,0:T(8,128)(2,1)} custom-call(s32[2]{0:T(128)} %pad_add_fusion.place, f32[128,1,128]{2,1,0:T(1,128)} %all-to-all-done.refs_0_, f32[8,768]{1,0:T(8,128)} %get-tuple-element.11.refs_1_, bf16[6,160,384]{2,1,0:T(8,128)(2,1)} %get-tuple-element.12.refs_2_, bf16[6,160,384]{2,1,0:T(8,128)(2,1)} %collective-permute-done.refs_3_, ...), custom_call_target="tpu_custom_call" | custom-call | flops 7644119040 | bytes 16777216 | tf_op jit(solution)/shard_map/decode/pallas_call | solution.py:258
Async XLA Ops:
  2.6 61.7 %collective-permute-start.1 = (bf16[6,160,384]{2,1,0:T(8,128)(2,1)}, bf16[6,160,384]{2,1,0:T(8,128)(2,1)}, u32[]{:S(2)}, u32[]{:S(2)}) collective-permute-start(bf16[6,160,384]{2,1,0:T(8,128)(2,1)} %get-tuple-element.12.refs_2_), channel_id=1, source_target_pairs={{1,0},{2,1},{3,2},{4,3},{5,4},{6,5},{7,6},{8,7},{9,8},{10,9},{11,1... | collective-permute-start | bytes 2211848 | tf_op jit(solution)/shard_map/ppermute | solution.py:206
  25.0 39.3 %collective-permute-start = (bf16[6,160,384]{2,1,0:T(8,128)(2,1)}, bf16[6,160,384]{2,1,0:T(8,128)(2,1)}, u32[]{:S(2)}, u32[]{:S(2)}) collective-permute-start(bf16[6,160,384]{2,1,0:T(8,128)(2,1)} %get-tuple-element.12.refs_2_), channel_id=1, source_target_pairs={{0,1},{1,2},{2,3},{3,4},{4,5},{5,6},{6,7},{7,8},{8,9},{9,10},{10,1... | collective-permute-start | bytes 2211848 | tf_op jit(solution)/shard_map/ppermute | solution.py:206
  27.0 37.3 %collective-permute-start.3 = (bf16[4,160,384]{2,1,0:T(8,128)(2,1)}, bf16[4,160,384]{2,1,0:T(8,128)(2,1)}, u32[]{:S(2)}, u32[]{:S(2)}) collective-permute-start(bf16[4,160,384]{2,1,0:T(8,128)(2,1)} %get-tuple-element.13), channel_id=1, source_target_pairs={{2,0},{3,1},{4,2},{5,3},{6,4},{7,5},{8,6},{9,7},{10,8},{11,9},{12,... | collective-permute-start | bytes 1474568 | tf_op jit(solution)/shard_map/ppermute | solution.py:206
  28.3 36.0 %collective-permute-start.2 = (bf16[4,160,384]{2,1,0:T(8,128)(2,1)}, bf16[4,160,384]{2,1,0:T(8,128)(2,1)}, u32[]{:S(2)}, u32[]{:S(2)}) collective-permute-start(bf16[4,160,384]{2,1,0:T(8,128)(2,1)} %get-tuple-element.13), channel_id=1, source_target_pairs={{0,2},{1,3},{2,4},{3,5},{4,6},{5,7},{6,8},{7,9},{8,10},{9,11},{10,... | collective-permute-start | bytes 1474568 | tf_op jit(solution)/shard_map/ppermute | solution.py:206
  33.1 31.2 %all-to-all-start = ((f32[128,1,128]{2,1,0:T(1,128)}), f32[128,1,128]{2,1,0:T(1,128)}, u32[]{:S(2)}, u32[]{:S(2)}) async-start(f32[128,1,128]{2,1,0:T(1,128)} %get-tuple-element.10), calls=%async_computation | async-start | bytes 131072 | tf_op jit(solution)/shard_map/all_to_all | solution.py:241

commit v3 on v2

v3 whole, which is shorter than its diff:
```python
import functools

import jax
import jax.numpy as jnp
from jax import lax
from jax.experimental import pallas as pl
from jax.experimental.pallas import tpu as pltpu
from jax.sharding import PartitionSpec as P

GROUPS = 32
ROWS = "rows"
EPSILON = 1e-06
LANES = 128
F32 = jnp.float32
BF16 = jnp.bfloat16
ALL_VMEM = 67043328
VMEM = pl.BlockSpec(memory_space=pltpu.VMEM)
HBM = pl.BlockSpec(memory_space=pltpu.HBM)
SMEM = pl.BlockSpec(memory_space=pltpu.SMEM)


def group_matrix(channels, first, flip):
    size = channels // GROUPS
    shape = (LANES, channels) if flip else (channels, LANES)
    lane = lax.broadcasted_iota(jnp.int32, shape, 0 if flip else 1) - first
    channel = lax.broadcasted_iota(jnp.int32, shape, 1 if flip else 0)
    return ((channel >= lane * size) & (channel < lane * size + size) & (lane >= 0)).astype(F32)


def exact_dot(a, b):
    return jnp.dot(a, b, preferred_element_type=F32, precision=lax.Precision.HIGHEST)


def pack_kernel(latent, conv_cache, time_cache, near, sums, sems):
    frames, _, _, channels = latent.shape
    jobs = []
    for n, source in enumerate((latent, conv_cache, time_cache)):
        for t in range(frames):
            jobs.append((source.at[t, 0], near.at[n * frames + t]))
    copies = [pltpu.make_async_copy(a, b, sems.at[i]) for i, (a, b) in enumerate(jobs)]
    for copy in copies:
        copy.start()
    total = jnp.zeros((8, channels), F32)
    square = jnp.zeros((8, channels), F32)
    for t in range(frames):
        copies[t].wait()
        wide = near[t].astype(F32).reshape(-1, 8, channels)
        total = total + jnp.sum(wide, axis=0)
        square = square + jnp.sum(wide * wide, axis=0)
    grouped = exact_dot(total, group_matrix(channels, 0, False))
    grouped = grouped + exact_dot(square, group_matrix(channels, GROUPS, False))
    row = jnp.sum(grouped, axis=0, keepdims=True)
    sums[...] = jnp.broadcast_to(row[None], sums.shape)
    for copy in copies[frames:]:
        copy.wait()


def shifted(value, step):
    length = value.shape[0]
    rolled = pltpu.roll(value, (-step) % length, 0)
    row = lax.broadcasted_iota(jnp.int32, value.shape, 0)
    return jnp.where((row + step >= 0) & (row + step < length), rolled, 0.0)


def start_copies(refs, sems):
    copies = [pltpu.make_async_copy(a, b, sems.at[n]) for n, (a, b) in enumerate(refs)]
    for copy in copies:
        copy.start()
    return copies


def conv_kernel(entries, place, *refs):
    far_refs, weight_far, out = refs[:5], refs[5], refs[6]
    near_refs, (weight, taps, acc, sems) = refs[7:12], refs[12:]
    stats, vectors, own, before, after = near_refs
    channels = own.shape[-1]
    width = own.shape[1]
    frames = own.shape[0] // 3
    moves = list(zip(far_refs, near_refs))
    for c in range(3):
        for a in range(3):
            for b in range(3):
                rows = pl.ds((a * 3 + b) * channels, channels)
                moves.append((weight_far.at[a, b, c], weight.at[c, rows, :]))
    copies = start_copies(moves, sems)
    copies[0].wait()
    copies[1].wait()
    gain, shift, conv_bias = (vectors[n : n + 1, :channels] for n in range(3))
    total = jnp.sum(stats[:, 0, :], axis=0, keepdims=True)
    total = jnp.broadcast_to(total, (8, LANES))
    center = exact_dot(total, group_matrix(channels, 0, True))[:1] / entries
    spread = exact_dot(total, group_matrix(channels, GROUPS, True))[:1] / entries
    spread = spread - center * center
    scale = lax.rsqrt(spread + EPSILON) * gain

    def place_row(frame, b, value):
        for a in range(3):
            t = frame - a
            if 0 <= t < frames:
                k = (a * 3 + b) * channels
                taps[t * width : (t + 1) * width, k : k + channels] = value

    for copy in copies[2:5]:
        copy.wait()
    for b, source in enumerate((before, own, after)):
        row = place[0] + (b - 1)
        inside = ((row >= 0) & (row <= place[1])).astype(F32)
        for t in range(frames):
            place_row(t, b, source[frames + t])
            value = source[t].astype(F32)
            value = (value - center) * scale + shift
            value = value / (1.0 + jnp.exp(-value)) * inside
            place_row(frames + t, b, value.astype(BF16))

    for c in range(3):
        for copy in copies[5 + c * 9 : 14 + c * 9]:
            copy.wait()
        acc[c] = jnp.dot(taps[...], weight[c], preferred_element_type=F32)

    for t in range(frames):
        rows = pl.ds(t * width, width)
        value = acc[1, rows, :] + shifted(acc[0, rows, :], -1) + shifted(acc[2, rows, :], 1)
        value = value + conv_bias + own[t].astype(F32)
        out[t] = value.astype(BF16)


def up_kernel(place, *refs):
    far_refs, out = refs[:9], refs[9]
    near_refs, (time_taps, mixed, up_taps, lifted, turned, sems) = refs[10:19], refs[19:]
    own, before, after, block, block_before, block_after, vectors, time_weight, up_weight = near_refs
    frames, width, channels = block.shape
    outputs = out.shape[-2]
    moves = [(a, b) for a, b in zip(far_refs, near_refs)]
    for n in range(3):
        moves[n] = (far_refs[n].at[pl.ds(2 * frames, frames)], near_refs[n])
    copies = start_copies(moves, sems)
    for copy in copies[:6]:
        copy.wait()
    rows_of = lambda t, r: pl.ds((t * 3 + r) * width, width)
    sources = ((before, block_before), (own, block), (after, block_after))
    for r in range(3):
        for t in range(frames):
            for frame, item in ((t, sources[r][0][t]), (frames + t, sources[r][1][t])):
                for a in range(3):
                    if 0 <= frame - a < frames:
                        k = a * channels
                        time_taps[rows_of(frame - a, r), k : k + channels] = item
    copies[6].wait()
    copies[7].wait()
    time_bias, up_bias = vectors[3:4, :], vectors[4:5, : 2 * outputs]
    weights = time_weight[...].reshape(3 * channels, 2 * channels)
    mixed[...] = jnp.dot(time_taps[...], weights, preferred_element_type=F32)
    for r in range(3):
        row = place[0] + (r - 1)
        inside = ((row >= 0) & (row <= place[1])).astype(F32)
        for t in range(frames):
            value = ((mixed[rows_of(t, r), :] + time_bias) * inside).astype(BF16)
            for k in range(2):
                part = value[:, k * channels : (k + 1) * channels]
                lines = pl.ds((2 * t + k) * width, width)
                for p in range(2):
                    if 0 <= r - p < 2:
                        up_taps[p, lines, (r - p) * channels : (r - p + 1) * channels] = part

    copies[8].wait()
    lane = lax.broadcasted_iota(jnp.int32, (width, 2 * outputs), 1)
    low = lax.broadcasted_iota(jnp.int32, (width, 2 * width), 0)
    high = lax.broadcasted_iota(jnp.int32, (width, 2 * width), 1)
    spread_out = [(high == 2 * low + q).astype(F32).astype(BF16) for q in range(2)]
    for p in range(2):
        lifted[...] = dot_nt(up_taps[p], up_weight[p])
        for f in range(2 * frames):
            lines = pl.ds(f * width, width)
            inner, outer = lifted[lines, : 2 * outputs], lifted[lines, 2 * outputs :]
            outer = jnp.where(lane < outputs, shifted(outer, -1), shifted(outer, 1))
            value = (inner + outer + up_bias).T.astype(BF16)
            for q in range(2):
                turned[q, pl.ds(f * outputs, outputs), :] = value[q * outputs : (q + 1) * outputs]
        value = jnp.dot(turned[0], spread_out[0], preferred_element_type=F32)
        value = value + jnp.dot(turned[1], spread_out[1], preferred_element_type=F32)
        out[:, p] = value.astype(BF16).reshape(2 * frames, outputs, 2 * width)


def dot_nt(a, b):
    return lax.dot_general(a, b, (((1,), (1,)), ((), ())), preferred_element_type=F32)


def small_kernel(up_weight, gain, shift, conv_bias, time_bias, up_bias, out, vectors):
    outputs, channels = up_weight.shape[2:]
    for n, item in enumerate((gain, shift, conv_bias)):
        vectors[n : n + 1, :channels] = item[...].reshape(1, -1)
    vectors[3:4, :] = time_bias[...].reshape(1, -1)
    vectors[4:5, :outputs] = up_bias[...].reshape(1, -1)
    vectors[4:5, outputs : 2 * outputs] = up_bias[...].reshape(1, -1)
    columns = lambda b: [up_weight[b, c].astype(F32) for c in range(3)]
    first, middle, final = columns(0), columns(1), columns(2)
    add = lambda u, v: [x + y for x, y in zip(u, v)]
    by_row = ((first, add(middle, final)), (add(first, middle), final))
    for p in range(2):
        for j in range(2):
            v = by_row[p][j]
            for n, item in enumerate((v[1] + v[2], v[0] + v[1], v[0], v[2])):
                rows = pl.ds(n * outputs, outputs)
                out[p, rows, j * channels : (j + 1) * channels] = item.astype(BF16)


def moved(value, step):
    devices = lax.axis_size(ROWS)
    pairs = [(i, i + step) for i in range(devices) if 0 <= i + step < devices]
    return lax.ppermute(value, ROWS, pairs)


def on_device(
    latent,
    conv_cache,
    time_cache,
    norm_gain,
    norm_shift,
    conv_weight,
    conv_bias,
    time_weight,
    time_bias,
    up_weight,
    up_bias,
):
    frames, row_count, width, channels = latent.shape
    outputs = up_weight.shape[-1]
    me, devices = lax.axis_index(ROWS), lax.axis_size(ROWS)
    near, sums = pl.pallas_call(
        pack_kernel,
        out_shape=(
            jax.ShapeDtypeStruct((3 * frames, width, channels), BF16),
            jax.ShapeDtypeStruct((devices, 1, LANES), F32),
        ),
        in_specs=[HBM] * 3,
        out_specs=(VMEM,) * 2,
        scratch_shapes=[pltpu.SemaphoreType.DMA((3 * frames,))],
        compiler_params=pltpu.CompilerParams(vmem_limit_bytes=ALL_VMEM),
        cost_estimate=pl.CostEstimate(flops=2**21, bytes_accessed=2**21, transcendentals=0),
        name="pack",
    )(latent, conv_cache, time_cache)
    before, after = moved(near, 1), moved(near, -1)
    stats = lax.all_to_all(sums, ROWS, 0, 0)
    entries = float(frames * row_count * devices * width * (channels // GROUPS))
    place = jnp.stack([me, jnp.int32(devices - 1)]).astype(jnp.int32)
    subpixel, vectors = pl.pallas_call(
        small_kernel,
        out_shape=(
            jax.ShapeDtypeStruct((2, 4 * outputs, 2 * channels), BF16),
            jax.ShapeDtypeStruct((8, 2 * channels), F32),
        ),
        in_specs=[VMEM] * 6,
        out_specs=(VMEM, VMEM),
        compiler_params=pltpu.CompilerParams(vmem_limit_bytes=ALL_VMEM),
        cost_estimate=pl.CostEstimate(flops=2**21, bytes_accessed=2**22, transcendentals=0),
        name="small",
    )(jnp.swapaxes(up_weight, 2, 3), norm_gain, norm_shift, conv_bias, time_bias, up_bias)
    params = pltpu.CompilerParams(vmem_limit_bytes=ALL_VMEM)
    copy_of = lambda item: pltpu.VMEM(item.shape, item.dtype)
    inputs = (stats, vectors, near, before, after)
    pixels = frames * width
    block = pl.pallas_call(
        functools.partial(conv_kernel, entries),
        out_shape=jax.ShapeDtypeStruct((frames, width, channels), BF16),
        in_specs=[SMEM] + [HBM] * 6,
        out_specs=VMEM,
        scratch_shapes=[
            *[copy_of(item) for item in inputs],
            pltpu.VMEM((3, 9 * channels, channels), BF16),
            pltpu.VMEM((pixels, 9 * channels), BF16),
            pltpu.VMEM((3, pixels, channels), F32),
            pltpu.SemaphoreType.DMA((32,)),
        ],
        compiler_params=params,
        cost_estimate=pl.CostEstimate(
            flops=2 * pixels * 27 * channels * channels, bytes_accessed=2**24, transcendentals=2**20
        ),
        name="conv",
    )(place, *inputs, conv_weight)
    caches = (near, before, after)
    inputs = (block, moved(block, 1), moved(block, -1), vectors, time_weight, subpixel)
    out = pl.pallas_call(
        up_kernel,
        out_shape=jax.ShapeDtypeStruct((2 * frames, 2, outputs, 2 * width), BF16),
        in_specs=[SMEM] + [HBM] * 9,
        out_specs=VMEM,
        scratch_shapes=[
            *[copy_of(block) for _ in caches],
            *[copy_of(item) for item in inputs],
            pltpu.VMEM((3 * pixels, 3 * channels), BF16),
            pltpu.VMEM((3 * pixels, 2 * channels), F32),
            pltpu.VMEM((2, 2 * pixels, 2 * channels), BF16),
            pltpu.VMEM((2 * pixels, 4 * outputs), F32),
            pltpu.VMEM((2, 2 * frames * outputs, width), BF16),
            pltpu.SemaphoreType.DMA((9,)),
        ],
        compiler_params=params,
        cost_estimate=pl.CostEstimate(
            flops=8 * pixels * 4 * channels * outputs * 2, bytes_accessed=2**23, transcendentals=0
        ),
        name="up",
    )(place, *caches, *inputs)
    return jnp.swapaxes(out, 2, 3)


def solution(mesh):
    placed = P("parts", ROWS, None, None)
    return jax.shard_map(
        on_device,
        mesh=mesh,
        in_specs=(placed,) * 3 + (P(),) * 8,
        out_specs=placed,
        check_vma=False,
    )
```

time: 88.9 us -> 85.1 us (0.957)
  the two profiles are of different devices: /device:TPU:33 before, /device:TPU:160 now
where the time goes in v3:
time: 85.1 us; the launch traced here: 84.8 us
  starting transfers between devices  42.2 us (50%)
  Pallas kernels  24.2 us (28%)
  waiting for transfers between devices  17.5 us (21%)
    all_to_all x1, starting transfers between devices, on_device(): stats = lax.all_to_all(sums, ROWS, 0, 0)  31.5 us
    ppermute x4, starting transfers between devices, moved(): return lax.ppermute(value, ROWS, pairs)  10.7 us
    pallas_call x1, Pallas kernels, on_device(): pl.pallas_call(up_kernel, out_shape=jax.ShapeDtypeStruct((2 * frames, 2,...  10.2 us
    all_to_all x1, waiting for transfers between devices, on_device(): stats = lax.all_to_all(sums, ROWS, 0, 0)  9.7 us
    pallas_call x1, Pallas kernels, on_device(): pl.pallas_call(functools.partial(conv_kernel, entries), out_shape=jax.Sha...  8.15 us
    ppermute x4, waiting for transfers between devices, moved(): return lax.ppermute(value, ROWS, pairs)  7.84 us
    pallas_call x1, Pallas kernels, on_device(): pl.pallas_call(small_kernel, out_shape=(jax.ShapeDtypeStruct((2, 4 * outp...  3.49 us
    pallas_call x1, Pallas kernels, on_device(): pl.pallas_call(pack_kernel, out_shape=(jax.ShapeDtypeStruct((3 * frames,...  2.37 us
  transfers between devices with their start and end apart: 5, of which 3 were waited for; matrix products, arithmetic and copies ran while one was open for 1% of the time, Pallas kernels for 4%

profile of v3, /device:TPU:160, one launch (start us, length us, event | category | flops | bytes accessed | tf_op | source)
XLA Modules:
  0.0 84.8 jit_solution(15819387147238870596)
XLA Ops:
  0.0 2.4 %pack.1 = (bf16[6,160,384]{2,1,0:T(8,128)(2,1)}, f32[128,1,128]{2,1,0:T(1,128)}) custom-call(bf16[2,1,160,384]{3,2,1,0:T(8,128)(2,1)} %latent.1, bf16[2,1,160,384]{3,2,1,0:T(8,128)(2,1)} %conv_cache.1, bf16[2,1,160,384]{3,2,1,0:T(8,128)(2,1)} %time_cache.1), custom_call_target="tpu_custom_call" | custom-call | flops 2097152 | bytes 2097152 | tf_op jit(solution)/shard_map/pack/pallas_call | solution.py:229
  2.4 3.3 %collective-permute-start.1 = (bf16[6,160,384]{2,1,0:T(8,128)(2,1)}, bf16[6,160,384]{2,1,0:T(8,128)(2,1)}, u32[]{:S(2)}, u32[]{:S(2)}) collective-permute-start(bf16[6,160,384]{2,1,0:T(8,128)(2,1)} %get-tuple-element.9.refs_2_.refs_0_), channel_id=1, source_target_pairs={{1,0},{2,1},{3,2},{4,3},{5,4},{6,5},{7,6},{8,7},{9,8},{10,9},{11,1... | collective-permute-start | bytes 2211848 | tf_op jit(solution)/shard_map/ppermute | solution.py:210
  5.7 2.0 %collective-permute-start = (bf16[6,160,384]{2,1,0:T(8,128)(2,1)}, bf16[6,160,384]{2,1,0:T(8,128)(2,1)}, u32[]{:S(2)}, u32[]{:S(2)}) collective-permute-start(bf16[6,160,384]{2,1,0:T(8,128)(2,1)} %get-tuple-element.9.refs_2_.refs_0_), channel_id=1, source_target_pairs={{0,1},{1,2},{2,3},{3,4},{4,5},{5,6},{6,7},{7,8},{8,9},{9,10},{10,1... | collective-permute-start | bytes 2211848 | tf_op jit(solution)/shard_map/ppermute | solution.py:210
  7.6 31.5 %all-to-all-start = ((f32[128,1,128]{2,1,0:T(1,128)}), f32[128,1,128]{2,1,0:T(1,128)}, u32[]{:S(2)}, u32[]{:S(2)}) async-start(f32[128,1,128]{2,1,0:T(1,128)} %get-tuple-element.10), calls=%async_computation | async-start | bytes 131072 | tf_op jit(solution)/shard_map/all_to_all | solution.py:243
  39.2 3.5 %small.1 = (bf16[2,768,768]{2,1,0:T(8,128)(2,1)}, f32[8,768]{1,0:T(8,128)}) custom-call(bf16[3,3,192,384]{3,2,1,0:T(8,128)(2,1)} %bitcast.3, f32[384]{0:T(512)} %gain.1, f32[384]{0:T(512)} %shift.1, f32[384]{0:T(512)} %conv_bias.1, f32[768]{0:T(1024)} %time_bias.1, f32[192]{0:T(256)} %up_bias.1), custom_call_target="tpu_custom_call" | custom-call | flops 2097152 | bytes 4194304 | tf_op jit(solution)/shard_map/small/pallas_call | solution.py:246
  42.7 0.6 pad_add_fusion.place
  43.3 9.7 %all-to-all-done.refs_0_ = f32[128,1,128]{2,1,0:T(1,128)} async-done(((f32[128,1,128]{2,1,0:T(1,128)}), f32[128,1,128]{2,1,0:T(1,128)}, u32[]{:S(2)}, u32[]{:S(2)}) %all-to-all-start) | async-done | bytes 65568 | tf_op jit(solution)/shard_map/all_to_all | solution.py:243
  53.0 0.0 collective-permute-done.1.refs_4_.refs_2_
  53.0 0.0 collective-permute-done.refs_3_.refs_1_
  53.0 8.1 %conv.1.refs_3_ = bf16[2,160,384]{2,1,0:T(8,128)(2,1)} custom-call(s32[2]{0:T(128)} %pad_add_fusion.place, f32[128,1,128]{2,1,0:T(1,128)} %all-to-all-done.refs_0_, f32[8,768]{1,0:T(8,128)} %get-tuple-element.11.refs_1_.refs_6_, bf16[6,160,384]{2,1,0:T(8,128)(2,1)} %get-tuple-element.9.refs_2_.refs_0_, ...), custom_call_target="tpu_custom_call" | custom-call | flops 2548039680 | bytes 16777216 | tf_op jit(solution)/shard_map/conv/pallas_call | solution.py:262
  61.1 3.3 %collective-permute-start.3 = (bf16[2,160,384]{2,1,0:T(8,128)(2,1)}, bf16[2,160,384]{2,1,0:T(8,128)(2,1)}, u32[]{:S(2)}, u32[]{:S(2)}) collective-permute-start(bf16[2,160,384]{2,1,0:T(8,128)(2,1)} %conv.1.refs_3_), channel_id=1, source_target_pairs={{1,0},{2,1},{3,2},{4,3},{5,4},{6,5},{7,6},{8,7},{9,8},{10,9},{11,1... | collective-permute-start | bytes 737288 | tf_op jit(solution)/shard_map/ppermute | solution.py:210
  64.5 2.1 %collective-permute-start.2 = (bf16[2,160,384]{2,1,0:T(8,128)(2,1)}, bf16[2,160,384]{2,1,0:T(8,128)(2,1)}, u32[]{:S(2)}, u32[]{:S(2)}) collective-permute-start(bf16[2,160,384]{2,1,0:T(8,128)(2,1)} %conv.1.refs_3_), channel_id=1, source_target_pairs={{0,1},{1,2},{2,3},{3,4},{4,5},{5,6},{6,7},{7,8},{8,9},{9,10},{10,1... | collective-permute-start | bytes 737288 | tf_op jit(solution)/shard_map/ppermute | solution.py:210
  66.6 1.9 %collective-permute-done.3.refs_5_ = bf16[2,160,384]{2,1,0:T(8,128)(2,1)} collective-permute-done((bf16[2,160,384]{2,1,0:T(8,128)(2,1)}, bf16[2,160,384]{2,1,0:T(8,128)(2,1)}, u32[]{:S(2)}, u32[]{:S(2)}) %collective-permute-start.3) | collective-permute-done | bytes 245792 | tf_op jit(solution)/shard_map/ppermute | solution.py:210
  68.5 6.0 %collective-permute-done.2.refs_4_ = bf16[2,160,384]{2,1,0:T(8,128)(2,1)} collective-permute-done((bf16[2,160,384]{2,1,0:T(8,128)(2,1)}, bf16[2,160,384]{2,1,0:T(8,128)(2,1)}, u32[]{:S(2)}, u32[]{:S(2)}) %collective-permute-start.2) | collective-permute-done | bytes 245792 | tf_op jit(solution)/shard_map/ppermute | solution.py:210
  74.4 10.2 %up.1 = bf16[4,2,192,320]{3,2,1,0:T(8,128)(2,1)} custom-call(s32[2]{0:T(128)} %pad_add_fusion.place, bf16[6,160,384]{2,1,0:T(8,128)(2,1)} %get-tuple-element.9.refs_2_.refs_0_, bf16[6,160,384]{2,1,0:T(8,128)(2,1)} %collective-permute-done.refs_3_.refs_1_, bf16[6,160,384]{2,1,0:T(8,128)(2,1)} %collective-permute-done.1.refs_4_.refs_2_, ...), custom_call_target="tpu_custom_call" | custom-call | flops 1509949440 | bytes 8388608 | tf_op jit(solution)/shard_map/up/pallas_call | solution.py:282
Async XLA Ops:
  2.4 50.6 %collective-permute-start.1 = (bf16[6,160,384]{2,1,0:T(8,128)(2,1)}, bf16[6,160,384]{2,1,0:T(8,128)(2,1)}, u32[]{:S(2)}, u32[]{:S(2)}) collective-permute-start(bf16[6,160,384]{2,1,0:T(8,128)(2,1)} %get-tuple-element.9.refs_2_.refs_0_), channel_id=1, source_target_pairs={{1,0},{2,1},{3,2},{4,3},{5,4},{6,5},{7,6},{8,7},{9,8},{10,9},{11,1... | collective-permute-start | bytes 2211848 | tf_op jit(solution)/shard_map/ppermute | solution.py:210
  5.7 47.3 %collective-permute-start = (bf16[6,160,384]{2,1,0:T(8,128)(2,1)}, bf16[6,160,384]{2,1,0:T(8,128)(2,1)}, u32[]{:S(2)}, u32[]{:S(2)}) collective-permute-start(bf16[6,160,384]{2,1,0:T(8,128)(2,1)} %get-tuple-element.9.refs_2_.refs_0_), channel_id=1, source_target_pairs={{0,1},{1,2},{2,3},{3,4},{4,5},{5,6},{6,7},{7,8},{8,9},{9,10},{10,1... | collective-permute-start | bytes 2211848 | tf_op jit(solution)/shard_map/ppermute | solution.py:210
  7.6 45.3 %all-to-all-start = ((f32[128,1,128]{2,1,0:T(1,128)}), f32[128,1,128]{2,1,0:T(1,128)}, u32[]{:S(2)}, u32[]{:S(2)}) async-start(f32[128,1,128]{2,1,0:T(1,128)} %get-tuple-element.10), calls=%async_computation | async-start | bytes 131072 | tf_op jit(solution)/shard_map/all_to_all | solution.py:243
  61.1 7.3 %collective-permute-start.3 = (bf16[2,160,384]{2,1,0:T(8,128)(2,1)}, bf16[2,160,384]{2,1,0:T(8,128)(2,1)}, u32[]{:S(2)}, u32[]{:S(2)}) collective-permute-start(bf16[2,160,384]{2,1,0:T(8,128)(2,1)} %conv.1.refs_3_), channel_id=1, source_target_pairs={{1,0},{2,1},{3,2},{4,3},{5,4},{6,5},{7,6},{8,7},{9,8},{10,9},{11,1... | collective-permute-start | bytes 737288 | tf_op jit(solution)/shard_map/ppermute | solution.py:210
  64.5 10.0 %collective-permute-start.2 = (bf16[2,160,384]{2,1,0:T(8,128)(2,1)}, bf16[2,160,384]{2,1,0:T(8,128)(2,1)}, u32[]{:S(2)}, u32[]{:S(2)}) collective-permute-start(bf16[2,160,384]{2,1,0:T(8,128)(2,1)} %conv.1.refs_3_), channel_id=1, source_target_pairs={{0,1},{1,2},{2,3},{3,4},{4,5},{5,6},{6,7},{7,8},{8,9},{9,10},{10,1... | collective-permute-start | bytes 737288 | tf_op jit(solution)/shard_map/ppermute | solution.py:210

commit v4 on v3

--- a/solution.py
+++ b/solution.py
@@ -14,9 +14,10 @@
 F32 = jnp.float32
 BF16 = jnp.bfloat16
 ALL_VMEM = 67043328
+CONV_VMEM = 50 * 2**20
+UP_VMEM = 24 * 2**20
 VMEM = pl.BlockSpec(memory_space=pltpu.VMEM)
 HBM = pl.BlockSpec(memory_space=pltpu.HBM)
-SMEM = pl.BlockSpec(memory_space=pltpu.SMEM)
 
 
 def group_matrix(channels, first, flip):
@@ -62,6 +63,19 @@
     return jnp.where((row + step >= 0) & (row + step < length), rolled, 0.0)
 
 
+def inside_image(step):
+    row = lax.axis_index(ROWS) + step
+    return ((row >= 0) & (row < lax.axis_size(ROWS))).astype(F32)
+
+
+def row_at(b, own, partner, outer, frame):
+    if b == 1:
+        return own[frame]
+    even = lax.axis_index(ROWS) % 2 == 0
+    first, second = (outer, partner) if b == 0 else (partner, outer)
+    return jnp.where(even, first[frame], second[frame])
+
+
 def start_copies(refs, sems):
     copies = [pltpu.make_async_copy(a, b, sems.at[n]) for n, (a, b) in enumerate(refs)]
     for copy in copies:
@@ -69,23 +83,18 @@
     return copies
 
 
-def conv_kernel(entries, place, *refs):
-    far_refs, weight_far, out = refs[:5], refs[5], refs[6]
-    near_refs, (weight, taps, acc, sems) = refs[7:12], refs[12:]
-    stats, vectors, own, before, after = near_refs
+def conv_kernel(entries, stats, vectors, own, partner, outer, weight_far, out, weight, taps, acc, sems):
     channels = own.shape[-1]
     width = own.shape[1]
     frames = own.shape[0] // 3
-    moves = list(zip(far_refs, near_refs))
+    moves = []
     for c in range(3):
         for a in range(3):
             for b in range(3):
                 rows = pl.ds((a * 3 + b) * channels, channels)
                 moves.append((weight_far.at[a, b, c], weight.at[c, rows, :]))
     copies = start_copies(moves, sems)
-    copies[0].wait()
-    copies[1].wait()
-    gain, shift, conv_bias = (vectors[n : n + 1, :channels] for n in range(3))
+    gain, shift, conv_bias = (vectors[:, n * channels : (n + 1) * channels] for n in range(3))
     total = jnp.sum(stats[:, 0, :], axis=0, keepdims=True)
     total = jnp.broadcast_to(total, (8, LANES))
     center = exact_dot(total, group_matrix(channels, 0, True))[:1] / entries
@@ -100,20 +109,17 @@
                 k = (a * 3 + b) * channels
                 taps[t * width : (t + 1) * width, k : k + channels] = value
 
-    for copy in copies[2:5]:
-        copy.wait()
-    for b, source in enumerate((before, own, after)):
-        row = place[0] + (b - 1)
-        inside = ((row >= 0) & (row <= place[1])).astype(F32)
+    for b in range(3):
+        inside = inside_image(b - 1)
         for t in range(frames):
-            place_row(t, b, source[frames + t])
-            value = source[t].astype(F32)
+            place_row(t, b, row_at(b, own, partner, outer, frames + t))
+            value = row_at(b, own, partner, outer, t).astype(F32)
             value = (value - center) * scale + shift
             value = value / (1.0 + jnp.exp(-value)) * inside
             place_row(frames + t, b, value.astype(BF16))
 
     for c in range(3):
-        for copy in copies[5 + c * 9 : 14 + c * 9]:
+        for copy in copies[9 * c : 9 * c + 9]:
             copy.wait()
         acc[c] = jnp.dot(taps[...], weight[c], preferred_element_type=F32)
 
@@ -124,35 +130,40 @@
         out[t] = value.astype(BF16)
 
 
-def up_kernel(place, *refs):
-    far_refs, out = refs[:9], refs[9]
-    near_refs, (time_taps, mixed, up_taps, lifted, turned, sems) = refs[10:19], refs[19:]
-    own, before, after, block, block_before, block_after, vectors, time_weight, up_weight = near_refs
+def up_kernel(
+    own,
+    partner,
+    outer,
+    block,
+    block_partner,
+    block_outer,
+    vectors,
+    time_weight,
+    up_weight,
+    out,
+    time_taps,
+    mixed,
+    up_taps,
+    lifted,
+    turned,
+):
     frames, width, channels = block.shape
     outputs = out.shape[-2]
-    moves = [(a, b) for a, b in zip(far_refs, near_refs)]
-    for n in range(3):
-        moves[n] = (far_refs[n].at[pl.ds(2 * frames, frames)], near_refs[n])
-    copies = start_copies(moves, sems)
-    for copy in copies[:6]:
-        copy.wait()
     rows_of = lambda t, r: pl.ds((t * 3 + r) * width, width)
-    sources = ((before, block_before), (own, block), (after, block_after))
     for r in range(3):
         for t in range(frames):
-            for frame, item in ((t, sources[r][0][t]), (frames + t, sources[r][1][t])):
+            cached = row_at(r, own, partner, outer, 2 * frames + t)
+            for frame, item in ((t, cached), (frames + t, row_at(r, block, block_partner, block_outer, t))):
                 for a in range(3):
                     if 0 <= frame - a < frames:
                         k = a * channels
                         time_taps[rows_of(frame - a, r), k : k + channels] = item
-    copies[6].wait()
-    copies[7].wait()
-    time_bias, up_bias = vectors[3:4, :], vectors[4:5, : 2 * outputs]
+    time_bias = vectors[:, 3 * channels : 5 * channels]
+    up_bias = vectors[:, 5 * channels :]
     weights = time_weight[...].reshape(3 * channels, 2 * channels)
     mixed[...] = jnp.dot(time_taps[...], weights, preferred_element_type=F32)
     for r in range(3):
-        row = place[0] + (r - 1)
-        inside = ((row >= 0) & (row <= place[1])).astype(F32)
+        inside = inside_image(r - 1)
         for t in range(frames):
             value = ((mixed[rows_of(t, r), :] + time_bias) * inside).astype(BF16)
             for k in range(2):
@@ -162,7 +173,6 @@
                     if 0 <= r - p < 2:
                         up_taps[p, lines, (r - p) * channels : (r - p + 1) * channels] = part
 
-    copies[8].wait()
     lane = lax.broadcasted_iota(jnp.int32, (width, 2 * outputs), 1)
     low = lax.broadcasted_iota(jnp.int32, (width, 2 * width), 0)
     high = lax.broadcasted_iota(jnp.int32, (width, 2 * width), 1)
@@ -185,13 +195,8 @@
     return lax.dot_general(a, b, (((1,), (1,)), ((), ())), preferred_element_type=F32)
 
 
-def small_kernel(up_weight, gain, shift, conv_bias, time_bias, up_bias, out, vectors):
+def subpixel_kernel(up_weight, out):
     outputs, channels = up_weight.shape[2:]
-    for n, item in enumerate((gain, shift, conv_bias)):
-        vectors[n : n + 1, :channels] = item[...].reshape(1, -1)
-    vectors[3:4, :] = time_bias[...].reshape(1, -1)
-    vectors[4:5, :outputs] = up_bias[...].reshape(1, -1)
-    vectors[4:5, outputs : 2 * outputs] = up_bias[...].reshape(1, -1)
     columns = lambda b: [up_weight[b, c].astype(F32) for c in range(3)]
     first, middle, final = columns(0), columns(1), columns(2)
     add = lambda u, v: [x + y for x, y in zip(u, v)]
@@ -204,10 +209,12 @@
                 out[p, rows, j * channels : (j + 1) * channels] = item.astype(BF16)
 
 
-def moved(value, step):
+def swapped(value):
     devices = lax.axis_size(ROWS)
-    pairs = [(i, i + step) for i in range(devices) if 0 <= i + step < devices]
-    return lax.ppermute(value, ROWS, pairs)
+    across = [(i, i - 1 if i % 2 == 0 else i + 1) for i in range(devices)]
+    across = [(i, j) for i, j in across if 0 <= j < devices]
+    outer = lax.ppermute(value, ROWS, across)
+    return lax.ppermute(value, ROWS, [(i, i ^ 1) for i in range(devices)]), outer
 
 
 def on_device(
@@ -225,7 +232,7 @@
 ):
     frames, row_count, width, channels = latent.shape
     outputs = up_weight.shape[-1]
-    me, devices = lax.axis_index(ROWS), lax.axis_size(ROWS)
+    devices = lax.axis_size(ROWS)
     near, sums = pl.pallas_call(
         pack_kernel,
         out_shape=(
@@ -239,67 +246,57 @@
         cost_estimate=pl.CostEstimate(flops=2**21, bytes_accessed=2**21, transcendentals=0),
         name="pack",
     )(latent, conv_cache, time_cache)
-    before, after = moved(near, 1), moved(near, -1)
+    partner, outer = swapped(near)
     stats = lax.all_to_all(sums, ROWS, 0, 0)
     entries = float(frames * row_count * devices * width * (channels // GROUPS))
-    place = jnp.stack([me, jnp.int32(devices - 1)]).astype(jnp.int32)
-    subpixel, vectors = pl.pallas_call(
-        small_kernel,
-        out_shape=(
-            jax.ShapeDtypeStruct((2, 4 * outputs, 2 * channels), BF16),
-            jax.ShapeDtypeStruct((8, 2 * channels), F32),
-        ),
-        in_specs=[VMEM] * 6,
-        out_specs=(VMEM, VMEM),
-        compiler_params=pltpu.CompilerParams(vmem_limit_bytes=ALL_VMEM),
-        cost_estimate=pl.CostEstimate(flops=2**21, bytes_accessed=2**22, transcendentals=0),
-        name="small",
-    )(jnp.swapaxes(up_weight, 2, 3), norm_gain, norm_shift, conv_bias, time_bias, up_bias)
-    params = pltpu.CompilerParams(vmem_limit_bytes=ALL_VMEM)
-    copy_of = lambda item: pltpu.VMEM(item.shape, item.dtype)
-    inputs = (stats, vectors, near, before, after)
+    subpixel = pl.pallas_call(
+        subpixel_kernel,
+        out_shape=jax.ShapeDtypeStruct((2, 4 * outputs, 2 * channels), BF16),
+        in_specs=[VMEM],
+        out_specs=VMEM,
+        compiler_params=pltpu.CompilerParams(vmem_limit_bytes=12 * 2**20),
+        cost_estimate=pl.CostEstimate(flops=2**21, bytes_accessed=2**24, transcendentals=0),
+        name="subpixel",
+    )(jnp.swapaxes(up_weight, 2, 3))
+    vectors = jnp.concatenate([norm_gain, norm_shift, conv_bias, time_bias, up_bias, up_bias])
+    vectors = vectors.reshape(1, -1)
     pixels = frames * width
     block = pl.pallas_call(
         functools.partial(conv_kernel, entries),
         out_shape=jax.ShapeDtypeStruct((frames, width, channels), BF16),
-        in_specs=[SMEM] + [HBM] * 6,
+        in_specs=[VMEM] * 5 + [HBM],
         out_specs=VMEM,
         scratch_shapes=[
-            *[copy_of(item) for item in inputs],
             pltpu.VMEM((3, 9 * channels, channels), BF16),
             pltpu.VMEM((pixels, 9 * channels), BF16),
             pltpu.VMEM((3, pixels, channels), F32),
-            pltpu.SemaphoreType.DMA((32,)),
+            pltpu.SemaphoreType.DMA((27,)),
         ],
-        compiler_params=params,
+        compiler_params=pltpu.CompilerParams(vmem_limit_bytes=CONV_VMEM),
         cost_estimate=pl.CostEstimate(
             flops=2 * pixels * 27 * channels * channels, bytes_accessed=2**24, transcendentals=2**20
         ),
         name="conv",
-    )(place, *inputs, conv_weight)
-    caches = (near, before, after)
-    inputs = (block, moved(block, 1), moved(block, -1), vectors, time_weight, subpixel)
+    )(stats, vectors, near, partner, outer, conv_weight)
+    inputs = (near, partner, outer, block, *swapped(block), vectors, time_weight, subpixel)
     out = pl.pallas_call(
         up_kernel,
         out_shape=jax.ShapeDtypeStruct((2 * frames, 2, outputs, 2 * width), BF16),
-        in_specs=[SMEM] + [HBM] * 9,
+        in_specs=[VMEM] * 9,
         out_specs=VMEM,
         scratch_shapes=[
-            *[copy_of(block) for _ in caches],
-            *[copy_of(item) for item in inputs],
             pltpu.VMEM((3 * pixels, 3 * channels), BF16),
             pltpu.VMEM((3 * pixels, 2 * channels), F32),
             pltpu.VMEM((2, 2 * pixels, 2 * channels), BF16),
             pltpu.VMEM((2 * pixels, 4 * outputs), F32),
             pltpu.VMEM((2, 2 * frames * outputs, width), BF16),
-            pltpu.SemaphoreType.DMA((9,)),
         ],
-        compiler_params=params,
+        compiler_params=pltpu.CompilerParams(vmem_limit_bytes=UP_VMEM),
         cost_estimate=pl.CostEstimate(
             flops=8 * pixels * 4 * channels * outputs * 2, bytes_accessed=2**23, transcendentals=0
         ),
         name="up",
-    )(place, *caches, *inputs)
+    )(*inputs)
     return jnp.swapaxes(out, 2, 3)
 
 

time: 85.1 us -> 73.5 us (0.86)
  the two profiles are of different devices: /device:TPU:160 before, /device:TPU:33 now
where the time goes in v4:
time: 73.5 us; the launch traced here: 73.2 us
  starting transfers between devices  37.5 us (51%)
  waiting for transfers between devices  17.2 us (23%)
  Pallas kernels  16.5 us (22%)
  local copies, waits for them, and re-layouts  1.98 us (3%)
    ppermute x2, starting transfers between devices, swapped(): lax.ppermute(value, ROWS, [(i, i ^ 1) for i in range(devices)])  17 us
    all_to_all x1, starting transfers between devices, on_device(): stats = lax.all_to_all(sums, ROWS, 0, 0)  13.3 us
    all_to_all x1, waiting for transfers between devices, on_device(): stats = lax.all_to_all(sums, ROWS, 0, 0)  13.1 us
    ppermute x2, starting transfers between devices, swapped(): outer = lax.ppermute(value, ROWS, across)  7.22 us
    pallas_call x1, Pallas kernels, on_device(): pl.pallas_call(up_kernel, out_shape=jax.ShapeDtypeStruct((2 * frames, 2,...  7.08 us
    pallas_call x1, Pallas kernels, on_device(): pl.pallas_call(functools.partial(conv_kernel, entries), out_shape=jax.Sha...  6.58 us
    ppermute x2, waiting for transfers between devices, swapped(): outer = lax.ppermute(value, ROWS, across)  4.05 us
    pallas_call x1, Pallas kernels, on_device(): pl.pallas_call(pack_kernel, out_shape=(jax.ShapeDtypeStruct((3 * frames,...  2.36 us
  transfers between devices with their start and end apart: 5, of which 2 were waited for; matrix products, arithmetic and copies ran while one was open for 1% of the time, Pallas kernels for 1%

profile of v4, /device:TPU:33, one launch (start us, length us, event | category | flops | bytes accessed | tf_op | source)
XLA Modules:
  0.0 73.2 jit_solution(7624351216686435818)
XLA Ops:
  0.0 2.4 %pack.1 = (bf16[6,160,384]{2,1,0:T(8,128)(2,1)}, f32[128,1,128]{2,1,0:T(1,128)}) custom-call(bf16[2,1,160,384]{3,2,1,0:T(8,128)(2,1)} %latent.1, bf16[2,1,160,384]{3,2,1,0:T(8,128)(2,1)} %conv_cache.1, bf16[2,1,160,384]{3,2,1,0:T(8,128)(2,1)} %time_cache.1), custom_call_target="tpu_custom_call" | custom-call | flops 2097152 | bytes 2097152 | tf_op jit(solution)/shard_map/pack/pallas_call | solution.py:236
  2.4 4.6 %collective-permute-start.1 = (bf16[6,160,384]{2,1,0:T(8,128)(2,1)}, bf16[6,160,384]{2,1,0:T(8,128)(2,1)S(1)}, u32[]{:S(2)}, u32[]{:S(2)}) collective-permute-start(bf16[6,160,384]{2,1,0:T(8,128)(2,1)} %get-tuple-element.7.own), channel_id=1, source_target_pairs={{1,2},{2,1},{3,4},{4,3},{5,6},{6,5},{7,8},{8,7},{9,10},{10,9},{11,... | collective-permute-start | bytes 2211848 | tf_op jit(solution)/shard_map/ppermute | solution.py:216
  7.0 16.6 %collective-permute-start = (bf16[6,160,384]{2,1,0:T(8,128)(2,1)}, bf16[6,160,384]{2,1,0:T(8,128)(2,1)S(1)}, u32[]{:S(2)}, u32[]{:S(2)}) collective-permute-start(bf16[6,160,384]{2,1,0:T(8,128)(2,1)} %get-tuple-element.7.own), channel_id=1, source_target_pairs={{0,1},{1,0},{2,3},{3,2},{4,5},{5,4},{6,7},{7,6},{8,9},{9,8},{10,11... | collective-permute-start | bytes 2211848 | tf_op jit(solution)/shard_map/ppermute | solution.py:217
  23.6 13.3 %all-to-all-start = ((f32[128,1,128]{2,1,0:T(1,128)}), f32[128,1,128]{2,1,0:T(1,128)S(1)}, u32[]{:S(2)}, u32[]{:S(2)}) async-start(f32[128,1,128]{2,1,0:T(1,128)} %get-tuple-element.8), calls=%async_computation | async-start | bytes 131072 | tf_op jit(solution)/shard_map/all_to_all | solution.py:250
  36.9 0.8 %concatenate.3 = f32[2304]{0:T(1024)S(1)} concatenate(f32[384]{0:T(512)} %param.14, f32[384]{0:T(512)} %param.15, f32[384]{0:T(512)} %param.17, f32[768]{0:T(1024)} %param.19, f32[192]{0:T(256)} %param.21, f32[192]{0:T(256)} %param.21), dimensions={0} | concatenate | bytes 18432 | tf_op jit(solution)/shard_map/concatenate | solution.py:261
  37.7 13.1 %all-to-all-done.stats = f32[128,1,128]{2,1,0:T(1,128)S(1)} async-done(((f32[128,1,128]{2,1,0:T(1,128)}), f32[128,1,128]{2,1,0:T(1,128)S(1)}, u32[]{:S(2)}, u32[]{:S(2)}) %all-to-all-start) | async-done | bytes 65568 | tf_op jit(solution)/shard_map/all_to_all | solution.py:250
  50.9 0.0 collective-permute-done.1.outer
  50.9 0.0 collective-permute-done.partner
  50.9 0.0 copy-start
  50.9 1.1 %copy-done = bf16[6,160,384]{2,1,0:T(8,128)(2,1)S(1)} copy-done((bf16[6,160,384]{2,1,0:T(8,128)(2,1)S(1)}, bf16[6,160,384]{2,1,0:T(8,128)(2,1)}, u32[]{:S(2)}) %copy-start) | copy-done | bytes 737304
  52.0 0.0 copy-start.2
  52.0 6.6 %conv.1.block = bf16[2,160,384]{2,1,0:T(8,128)(2,1)S(1)} custom-call(f32[128,1,128]{2,1,0:T(1,128)S(1)} %all-to-all-done.stats, f32[1,2304]{1,0:T(1,128)S(1)} %reshape.3.vectors, bf16[6,160,384]{2,1,0:T(8,128)(2,1)S(1)} %copy-done, bf16[6,160,384]{2,1,0:T(8,128)(2,1)S(1)} %collective-permute-done.partner, ...), custom_call_target="tpu_custom_call" | custom-call | flops 2548039680 | bytes 16777216 | tf_op jit(solution)/shard_map/conv/pallas_call | solution.py:264
  58.6 2.6 %collective-permute-start.3 = (bf16[2,160,384]{2,1,0:T(8,128)(2,1)S(1)}, bf16[2,160,384]{2,1,0:T(8,128)(2,1)S(1)}, u32[]{:S(2)}, u32[]{:S(2)}) collective-permute-start(bf16[2,160,384]{2,1,0:T(8,128)(2,1)S(1)} %conv.1.block), channel_id=1, source_target_pairs={{1,2},{2,1},{3,4},{4,3},{5,6},{6,5},{7,8},{8,7},{9,10},{10,9},{11,... | collective-permute-start | bytes 737288 | tf_op jit(solution)/shard_map/ppermute | solution.py:216
  61.2 0.3 collective-permute-start.2
  61.6 0.0 copy-done.2
  61.6 0.0 copy-start.1
  61.6 0.5 subpixel.1.up_weight
  62.1 4.0 %collective-permute-done.3.block_outer = bf16[2,160,384]{2,1,0:T(8,128)(2,1)S(1)} collective-permute-done((bf16[2,160,384]{2,1,0:T(8,128)(2,1)S(1)}, bf16[2,160,384]{2,1,0:T(8,128)(2,1)S(1)}, u32[]{:S(2)}, u32[]{:S(2)}) %collective-permute-start.3) | collective-permute-done | bytes 245792 | tf_op jit(solution)/shard_map/ppermute | solution.py:216
  66.1 0.0 collective-permute-done.2.block_partner
  66.1 0.0 copy-done.1
  66.1 7.1 %up.1 = bf16[4,2,192,320]{3,2,1,0:T(8,128)(2,1)} custom-call(bf16[6,160,384]{2,1,0:T(8,128)(2,1)S(1)} %copy-done, bf16[6,160,384]{2,1,0:T(8,128)(2,1)S(1)} %collective-permute-done.partner, bf16[6,160,384]{2,1,0:T(8,128)(2,1)S(1)} %collective-permute-done.1.outer, bf16[2,160,384]{2,1,0:T(8,128)(2,1)S(1)} %conv.1.block, ...), custom_call_target="tpu_custom_call" | custom-call | flops 1509949440 | bytes 8388608 | tf_op jit(solution)/shard_map/up/pallas_call | solution.py:282
  (1 shorter events, 0.0 us)
Async XLA Ops:
  2.4 48.5 %collective-permute-start.1 = (bf16[6,160,384]{2,1,0:T(8,128)(2,1)}, bf16[6,160,384]{2,1,0:T(8,128)(2,1)S(1)}, u32[]{:S(2)}, u32[]{:S(2)}) collective-permute-start(bf16[6,160,384]{2,1,0:T(8,128)(2,1)} %get-tuple-element.7.own), channel_id=1, source_target_pairs={{1,2},{2,1},{3,4},{4,3},{5,6},{6,5},{7,8},{8,7},{9,10},{10,9},{11,... | collective-permute-start | bytes 2211848 | tf_op jit(solution)/shard_map/ppermute | solution.py:216
  7.0 43.9 %collective-permute-start = (bf16[6,160,384]{2,1,0:T(8,128)(2,1)}, bf16[6,160,384]{2,1,0:T(8,128)(2,1)S(1)}, u32[]{:S(2)}, u32[]{:S(2)}) collective-permute-start(bf16[6,160,384]{2,1,0:T(8,128)(2,1)} %get-tuple-element.7.own), channel_id=1, source_target_pairs={{0,1},{1,0},{2,3},{3,2},{4,5},{5,4},{6,7},{7,6},{8,9},{9,8},{10,11... | collective-permute-start | bytes 2211848 | tf_op jit(solution)/shard_map/ppermute | solution.py:217
  23.6 27.3 %all-to-all-start = ((f32[128,1,128]{2,1,0:T(1,128)}), f32[128,1,128]{2,1,0:T(1,128)S(1)}, u32[]{:S(2)}, u32[]{:S(2)}) async-start(f32[128,1,128]{2,1,0:T(1,128)} %get-tuple-element.8), calls=%async_computation | async-start | bytes 131072 | tf_op jit(solution)/shard_map/all_to_all | solution.py:250
  50.9 1.1 %copy-start = (bf16[6,160,384]{2,1,0:T(8,128)(2,1)S(1)}, bf16[6,160,384]{2,1,0:T(8,128)(2,1)}, u32[]{:S(2)}) copy-start(bf16[6,160,384]{2,1,0:T(8,128)(2,1)} %get-tuple-element.7.own) | copy-start | bytes 2211844
  52.0 9.6 %copy-start.2 = (bf16[3,3,384,192]{2,3,1,0:T(8,128)(2,1)S(1)}, bf16[3,3,384,192]{2,3,1,0:T(8,128)(2,1)}, u32[]{:S(2)}) copy-start(bf16[3,3,384,192]{2,3,1,0:T(8,128)(2,1)} %param.20) | copy-start | bytes 3981316
  58.6 7.5 %collective-permute-start.3 = (bf16[2,160,384]{2,1,0:T(8,128)(2,1)S(1)}, bf16[2,160,384]{2,1,0:T(8,128)(2,1)S(1)}, u32[]{:S(2)}, u32[]{:S(2)}) collective-permute-start(bf16[2,160,384]{2,1,0:T(8,128)(2,1)S(1)} %conv.1.block), channel_id=1, source_target_pairs={{1,2},{2,1},{3,4},{4,3},{5,6},{6,5},{7,8},{8,7},{9,10},{10,9},{11,... | collective-permute-start | bytes 737288 | tf_op jit(solution)/shard_map/ppermute | solution.py:216
  61.2 4.9 %collective-permute-start.2 = (bf16[2,160,384]{2,1,0:T(8,128)(2,1)S(1)}, bf16[2,160,384]{2,1,0:T(8,128)(2,1)S(1)}, u32[]{:S(2)}, u32[]{:S(2)}) collective-permute-start(bf16[2,160,384]{2,1,0:T(8,128)(2,1)S(1)} %conv.1.block), channel_id=1, source_target_pairs={{0,1},{1,0},{2,3},{3,2},{4,5},{5,4},{6,7},{7,6},{8,9},{9,8},{10,11... | collective-permute-start | bytes 737288 | tf_op jit(solution)/shard_map/ppermute | solution.py:217
  61.6 4.6 %copy-start.1 = (bf16[3,384,768]{2,1,0:T(8,128)(2,1)S(1)}, bf16[3,384,768]{2,1,0:T(8,128)(2,1)}, u32[]{:S(2)}) copy-start(bf16[3,384,768]{2,1,0:T(8,128)(2,1)} %time_weight.1) | copy-start | bytes 5308420

commit v5 on v4

--- a/solution.py
+++ b/solution.py
@@ -14,6 +14,7 @@
 F32 = jnp.float32
 BF16 = jnp.bfloat16
 ALL_VMEM = 67043328
+CACHED_VMEM = 44 * 2**20
 CONV_VMEM = 50 * 2**20
 UP_VMEM = 24 * 2**20
 VMEM = pl.BlockSpec(memory_space=pltpu.VMEM)
@@ -83,51 +84,67 @@
     return copies
 
 
-def conv_kernel(entries, stats, vectors, own, partner, outer, weight_far, out, weight, taps, acc, sems):
-    channels = own.shape[-1]
-    width = own.shape[1]
-    frames = own.shape[0] // 3
+def weight_copies(weight_far, weight, taken, sems):
+    channels = weight.shape[-1]
     moves = []
     for c in range(3):
-        for a in range(3):
+        for n, a in enumerate(taken):
             for b in range(3):
-                rows = pl.ds((a * 3 + b) * channels, channels)
-                moves.append((weight_far.at[a, b, c], weight.at[c, rows, :]))
-    copies = start_copies(moves, sems)
-    gain, shift, conv_bias = (vectors[:, n * channels : (n + 1) * channels] for n in range(3))
+                rows = pl.ds(b * channels, channels)
+                moves.append((weight_far.at[a, b, c], weight.at[c, n, rows, :]))
+    return start_copies(moves, sems)
+
+
+def tap_sums(copies, taps, weight, acc, shared, single, rows):
+    source, target = rows
+    for c in range(3):
+        for copy in copies[6 * c : 6 * c + 6]:
+            copy.wait()
+        acc[c] = jnp.dot(taps[...], weight[c, shared], preferred_element_type=F32)
+        more = jnp.dot(taps[source, :], weight[c, single], preferred_element_type=F32)
+        acc[c, target, :] = acc[c, target, :] + more
+
+
+def joined_columns(acc, rows):
+    return acc[1, rows, :] + shifted(acc[0, rows, :], -1) + shifted(acc[2, rows, :], 1)
+
+
+def cached_kernel(vectors, own, partner, outer, weight_far, out, weight, taps, acc, sems):
+    width, channels = own.shape[1:]
+    copies = weight_copies(weight_far, weight, (0, 1), sems)
+    first, second = pl.ds(0, width), pl.ds(width, width)
+    for b in range(3):
+        for t, lines in enumerate((first, second)):
+            taps[lines, b * channels : (b + 1) * channels] = row_at(b, own, partner, outer, 2 + t)
+    tap_sums(copies, taps, weight, acc, 0, 1, (second, first))
+    conv_bias = vectors[:, 2 * channels : 3 * channels]
+    for t, lines in enumerate((first, second)):
+        latent = own[t].astype(F32)
+        out[t] = joined_columns(acc, lines) + conv_bias + latent
+        out[2 + t] = latent
+
+
+def conv_kernel(entries, stats, vectors, own, partner, outer, weight_far, out, weight, taps, acc, sems):
+    width, channels = own.shape[1:]
+    copies = weight_copies(weight_far, weight, (1, 2), sems)
+    gain, shift = (vectors[:, n * channels : (n + 1) * channels] for n in range(2))
     total = jnp.sum(stats[:, 0, :], axis=0, keepdims=True)
     total = jnp.broadcast_to(total, (8, LANES))
     center = exact_dot(total, group_matrix(channels, 0, True))[:1] / entries
     spread = exact_dot(total, group_matrix(channels, GROUPS, True))[:1] / entries
     spread = spread - center * center
     scale = lax.rsqrt(spread + EPSILON) * gain
-
-    def place_row(frame, b, value):
-        for a in range(3):
-            t = frame - a
-            if 0 <= t < frames:
-                k = (a * 3 + b) * channels
-                taps[t * width : (t + 1) * width, k : k + channels] = value
-
+    first, second = pl.ds(0, width), pl.ds(width, width)
     for b in range(3):
         inside = inside_image(b - 1)
-        for t in range(frames):
-            place_row(t, b, row_at(b, own, partner, outer, frames + t))
-            value = row_at(b, own, partner, outer, t).astype(F32)
+        for t, lines in enumerate((first, second)):
+            value = own[2 + t] if b == 1 else row_at(b, own, partner, outer, t).astype(F32)
             value = (value - center) * scale + shift
             value = value / (1.0 + jnp.exp(-value)) * inside
-            place_row(frames + t, b, value.astype(BF16))
-
-    for c in range(3):
-        for copy in copies[9 * c : 9 * c + 9]:
-            copy.wait()
-        acc[c] = jnp.dot(taps[...], weight[c], preferred_element_type=F32)
-
-    for t in range(frames):
-        rows = pl.ds(t * width, width)
-        value = acc[1, rows, :] + shifted(acc[0, rows, :], -1) + shifted(acc[2, rows, :], 1)
-        value = value + conv_bias + own[t].astype(F32)
-        out[t] = value.astype(BF16)
+            taps[lines, b * channels : (b + 1) * channels] = value.astype(BF16)
+    tap_sums(copies, taps, weight, acc, 1, 0, (first, second))
+    for t, lines in enumerate((first, second)):
+        out[t] = (joined_columns(acc, lines) + own[t]).astype(BF16)
 
 
 def up_kernel(
@@ -140,15 +157,18 @@
     vectors,
     time_weight,
     up_weight,
+    far_out,
     out,
     time_taps,
     mixed,
     up_taps,
     lifted,
     turned,
+    sems,
 ):
     frames, width, channels = block.shape
     outputs = out.shape[-2]
+    copies = []
     rows_of = lambda t, r: pl.ds((t * 3 + r) * width, width)
     for r in range(3):
         for t in range(frames):
@@ -188,7 +208,11 @@
                 turned[q, pl.ds(f * outputs, outputs), :] = value[q * outputs : (q + 1) * outputs]
         value = jnp.dot(turned[0], spread_out[0], preferred_element_type=F32)
         value = value + jnp.dot(turned[1], spread_out[1], preferred_element_type=F32)
-        out[:, p] = value.astype(BF16).reshape(2 * frames, outputs, 2 * width)
+        out[p] = value.astype(BF16).reshape(2 * frames, outputs, 2 * width)
+        copies.append(pltpu.make_async_copy(out.at[p], far_out.at[:, p], sems.at[p]))
+        copies[p].start()
+    for copy in copies:
+        copy.wait()
 
 
 def dot_nt(a, b):
@@ -261,35 +285,47 @@
     vectors = jnp.concatenate([norm_gain, norm_shift, conv_bias, time_bias, up_bias, up_bias])
     vectors = vectors.reshape(1, -1)
     pixels = frames * width
+    flops = pixels * 27 * channels * channels
+    scratch = [
+        pltpu.VMEM((3, 2, 3 * channels, channels), BF16),
+        pltpu.VMEM((pixels, 3 * channels), BF16),
+        pltpu.VMEM((3, pixels, channels), F32),
+        pltpu.SemaphoreType.DMA((18,)),
+    ]
+    base = pl.pallas_call(
+        cached_kernel,
+        out_shape=jax.ShapeDtypeStruct((2 * frames, width, channels), F32),
+        in_specs=[VMEM] * 4 + [HBM],
+        out_specs=VMEM,
+        scratch_shapes=scratch,
+        compiler_params=pltpu.CompilerParams(vmem_limit_bytes=CACHED_VMEM),
+        cost_estimate=pl.CostEstimate(flops=flops, bytes_accessed=2**23, transcendentals=0),
+        name="cached",
+    )(vectors, near, partner, outer, conv_weight)
     block = pl.pallas_call(
         functools.partial(conv_kernel, entries),
         out_shape=jax.ShapeDtypeStruct((frames, width, channels), BF16),
         in_specs=[VMEM] * 5 + [HBM],
         out_specs=VMEM,
-        scratch_shapes=[
-            pltpu.VMEM((3, 9 * channels, channels), BF16),
-            pltpu.VMEM((pixels, 9 * channels), BF16),
-            pltpu.VMEM((3, pixels, channels), F32),
-            pltpu.SemaphoreType.DMA((27,)),
-        ],
+        scratch_shapes=scratch,
         compiler_params=pltpu.CompilerParams(vmem_limit_bytes=CONV_VMEM),
-        cost_estimate=pl.CostEstimate(
-            flops=2 * pixels * 27 * channels * channels, bytes_accessed=2**24, transcendentals=2**20
-        ),
+        cost_estimate=pl.CostEstimate(flops=flops, bytes_accessed=2**23, transcendentals=2**18),
         name="conv",
-    )(stats, vectors, near, partner, outer, conv_weight)
+    )(stats, vectors, base, partner, outer, conv_weight)
     inputs = (near, partner, outer, block, *swapped(block), vectors, time_weight, subpixel)
     out = pl.pallas_call(
         up_kernel,
         out_shape=jax.ShapeDtypeStruct((2 * frames, 2, outputs, 2 * width), BF16),
         in_specs=[VMEM] * 9,
-        out_specs=VMEM,
+        out_specs=HBM,
         scratch_shapes=[
+            pltpu.VMEM((2, 2 * frames, outputs, 2 * width), BF16),
             pltpu.VMEM((3 * pixels, 3 * channels), BF16),
             pltpu.VMEM((3 * pixels, 2 * channels), F32),
             pltpu.VMEM((2, 2 * pixels, 2 * channels), BF16),
             pltpu.VMEM((2 * pixels, 4 * outputs), F32),
             pltpu.VMEM((2, 2 * frames * outputs, width), BF16),
+            pltpu.SemaphoreType.DMA((2,)),
         ],
         compiler_params=pltpu.CompilerParams(vmem_limit_bytes=UP_VMEM),
         cost_estimate=pl.CostEstimate(

time: 73.5 us -> 70.3 us (0.956)
  waiting for transfers between devices: 17.2 us -> 12.1 us
  Pallas kernels: 16.5 us -> 18.2 us
    all_to_all x1, waiting for transfers between devices: 13.1 us -> 8.01 us  [on_device(): stats = lax.all_to_all(sums, ROWS, 0, 0)]
    pallas_call x0 -> x1, Pallas kernels: none -> 3.96 us  [on_device(): pl.pallas_call(cached_kernel, out_shape=jax.ShapeDtypeStruct((2 * frames,...]
    pallas_call x1, Pallas kernels: 6.58 us -> 4.47 us  [on_device(): pl.pallas_call(functools.partial(conv_kernel, entries), out_shape=jax.Sha...]
  transfers between devices with their start and end apart: 5 -> 5, of which waited for: 2 -> 2; matrix products, arithmetic and copies ran while one was open for 1% -> 1% of each run, Pallas kernels for 1% -> 6%
where the time goes in v5:
time: 70.3 us; the launch traced here: 70 us
  starting transfers between devices  37.4 us (53%)
  Pallas kernels  18.2 us (26%)
  waiting for transfers between devices  12.1 us (17%)
  local copies, waits for them, and re-layouts  1.98 us (3%)
    ppermute x2, starting transfers between devices, swapped(): lax.ppermute(value, ROWS, [(i, i ^ 1) for i in range(devices)])  17 us
    all_to_all x1, starting transfers between devices, on_device(): stats = lax.all_to_all(sums, ROWS, 0, 0)  13.3 us
    all_to_all x1, waiting for transfers between devices, on_device(): stats = lax.all_to_all(sums, ROWS, 0, 0)  8.01 us
    ppermute x2, starting transfers between devices, swapped(): outer = lax.ppermute(value, ROWS, across)  7.13 us
    pallas_call x1, Pallas kernels, on_device(): pl.pallas_call(up_kernel, out_shape=jax.ShapeDtypeStruct((2 * frames, 2,...  6.93 us
    pallas_call x1, Pallas kernels, on_device(): pl.pallas_call(functools.partial(conv_kernel, entries), out_shape=jax.Sha...  4.47 us
    ppermute x2, waiting for transfers between devices, swapped(): outer = lax.ppermute(value, ROWS, across)  4.13 us
    pallas_call x1, Pallas kernels, on_device(): pl.pallas_call(cached_kernel, out_shape=jax.ShapeDtypeStruct((2 * frames,...  3.96 us
  transfers between devices with their start and end apart: 5, of which 2 were waited for; matrix products, arithmetic and copies ran while one was open for 1% of the time, Pallas kernels for 6%

profile of v5, /device:TPU:33, one launch (start us, length us, event | category | flops | bytes accessed | tf_op | source)
XLA Modules:
  0.0 70.0 jit_solution(8191322959744473434)
XLA Ops:
  0.0 2.4 %pack.1 = (bf16[6,160,384]{2,1,0:T(8,128)(2,1)}, f32[128,1,128]{2,1,0:T(1,128)}) custom-call(bf16[2,1,160,384]{3,2,1,0:T(8,128)(2,1)} %latent.1, bf16[2,1,160,384]{3,2,1,0:T(8,128)(2,1)} %conv_cache.1, bf16[2,1,160,384]{3,2,1,0:T(8,128)(2,1)} %time_cache.1), custom_call_target="tpu_custom_call" | custom-call | flops 2097152 | bytes 2097152 | tf_op jit(solution)/shard_map/pack/pallas_call | solution.py:260
  2.4 4.6 %collective-permute-start.1 = (bf16[6,160,384]{2,1,0:T(8,128)(2,1)}, bf16[6,160,384]{2,1,0:T(8,128)(2,1)S(1)}, u32[]{:S(2)}, u32[]{:S(2)}) collective-permute-start(bf16[6,160,384]{2,1,0:T(8,128)(2,1)} %get-tuple-element.7.own), channel_id=1, source_target_pairs={{1,2},{2,1},{3,4},{4,3},{5,6},{6,5},{7,8},{8,7},{9,10},{10,9},{11,... | collective-permute-start | bytes 2211848 | tf_op jit(solution)/shard_map/ppermute | solution.py:240
  7.0 16.6 %collective-permute-start = (bf16[6,160,384]{2,1,0:T(8,128)(2,1)}, bf16[6,160,384]{2,1,0:T(8,128)(2,1)S(1)}, u32[]{:S(2)}, u32[]{:S(2)}) collective-permute-start(bf16[6,160,384]{2,1,0:T(8,128)(2,1)} %get-tuple-element.7.own), channel_id=1, source_target_pairs={{0,1},{1,0},{2,3},{3,2},{4,5},{5,4},{6,7},{7,6},{8,9},{9,8},{10,11... | collective-permute-start | bytes 2211848 | tf_op jit(solution)/shard_map/ppermute | solution.py:241
  23.6 13.3 %all-to-all-start = ((f32[128,1,128]{2,1,0:T(1,128)}), f32[128,1,128]{2,1,0:T(1,128)S(1)}, u32[]{:S(2)}, u32[]{:S(2)}) async-start(f32[128,1,128]{2,1,0:T(1,128)} %get-tuple-element.8), calls=%async_computation | async-start | bytes 131072 | tf_op jit(solution)/shard_map/all_to_all | solution.py:274
  36.9 0.8 %concatenate.3 = f32[2304]{0:T(1024)S(1)} concatenate(f32[384]{0:T(512)} %param.14, f32[384]{0:T(512)} %param.15, f32[384]{0:T(512)} %param.17, f32[768]{0:T(1024)} %param.19, f32[192]{0:T(256)} %param.21, f32[192]{0:T(256)} %param.21), dimensions={0} | concatenate | bytes 18432 | tf_op jit(solution)/shard_map/concatenate | solution.py:285
  37.7 0.0 collective-permute-done.1.outer
  37.8 0.0 collective-permute-done.partner
  37.8 0.0 copy-start
  37.8 1.1 %copy-done = bf16[6,160,384]{2,1,0:T(8,128)(2,1)S(1)} copy-done((bf16[6,160,384]{2,1,0:T(8,128)(2,1)S(1)}, bf16[6,160,384]{2,1,0:T(8,128)(2,1)}, u32[]{:S(2)}) %copy-start) | copy-done | bytes 737304
  38.9 4.0 %cached.1.own = f32[4,160,384]{2,1,0:T(8,128)S(1)} custom-call(f32[1,2304]{1,0:T(1,128)S(1)} %reshape.3.vectors, bf16[6,160,384]{2,1,0:T(8,128)(2,1)S(1)} %copy-done, bf16[6,160,384]{2,1,0:T(8,128)(2,1)S(1)} %collective-permute-done.partner, bf16[6,160,384]{2,1,0:T(8,128)(2,1)S(1)} %collective-permute-done.1.outer, bf16[3,3,3,384,384]{4,3,2,1,0:T(8,128)(2,1)} %weight_far.3), custom_call_target="tpu_custom_call" | custom-call | flops 1274019840 | bytes 8388608 | tf_op jit(solution)/shard_map/cached/pallas_call | solution.py:295
  42.9 8.0 %all-to-all-done.stats = f32[128,1,128]{2,1,0:T(1,128)S(1)} async-done(((f32[128,1,128]{2,1,0:T(1,128)}), f32[128,1,128]{2,1,0:T(1,128)S(1)}, u32[]{:S(2)}, u32[]{:S(2)}) %all-to-all-start) | async-done | bytes 65568 | tf_op jit(solution)/shard_map/all_to_all | solution.py:274
  50.9 0.0 copy-start.3
  50.9 4.5 %conv.1.block = bf16[2,160,384]{2,1,0:T(8,128)(2,1)S(1)} custom-call(f32[128,1,128]{2,1,0:T(1,128)S(1)} %all-to-all-done.stats, f32[1,2304]{1,0:T(1,128)S(1)} %reshape.3.vectors, f32[4,160,384]{2,1,0:T(8,128)S(1)} %cached.1.own, bf16[6,160,384]{2,1,0:T(8,128)(2,1)S(1)} %collective-permute-done.partner, ...), custom_call_target="tpu_custom_call" | custom-call | flops 1274019840 | bytes 8388608 | tf_op jit(solution)/shard_map/conv/pallas_call | solution.py:305
  55.3 2.5 %collective-permute-start.3 = (bf16[2,160,384]{2,1,0:T(8,128)(2,1)S(1)}, bf16[2,160,384]{2,1,0:T(8,128)(2,1)S(1)}, u32[]{:S(2)}, u32[]{:S(2)}) collective-permute-start(bf16[2,160,384]{2,1,0:T(8,128)(2,1)S(1)} %conv.1.block), channel_id=1, source_target_pairs={{1,2},{2,1},{3,4},{4,3},{5,6},{6,5},{7,8},{8,7},{9,10},{10,9},{11,... | collective-permute-start | bytes 737288 | tf_op jit(solution)/shard_map/ppermute | solution.py:240
  57.9 0.3 collective-permute-start.2
  58.2 0.0 copy-done.3
  58.2 0.0 copy-start.1
  58.2 0.0 copy-start.2
  58.2 0.5 subpixel.1.up_weight
  58.8 4.1 %collective-permute-done.3.block_outer = bf16[2,160,384]{2,1,0:T(8,128)(2,1)S(1)} collective-permute-done((bf16[2,160,384]{2,1,0:T(8,128)(2,1)S(1)}, bf16[2,160,384]{2,1,0:T(8,128)(2,1)S(1)}, u32[]{:S(2)}, u32[]{:S(2)}) %collective-permute-start.3) | collective-permute-done | bytes 245792 | tf_op jit(solution)/shard_map/ppermute | solution.py:240
  62.9 0.0 collective-permute-done.2.block_partner
  62.9 0.0 copy-done.1
  62.9 0.0 copy-done.2
  62.9 6.9 %up.1 = bf16[4,2,192,320]{3,2,1,0:T(8,128)(2,1)} custom-call(bf16[6,160,384]{2,1,0:T(8,128)(2,1)S(1)} %copy-done.1, bf16[6,160,384]{2,1,0:T(8,128)(2,1)S(1)} %collective-permute-done.partner, bf16[6,160,384]{2,1,0:T(8,128)(2,1)S(1)} %collective-permute-done.1.outer, bf16[2,160,384]{2,1,0:T(8,128)(2,1)S(1)} %conv.1.block, ...), custom_call_target="tpu_custom_call" | custom-call | flops 1509949440 | bytes 8388608 | tf_op jit(solution)/shard_map/up/pallas_call | solution.py:316
  (1 shorter events, 0.0 us)
Async XLA Ops:
  2.4 35.4 %collective-permute-start.1 = (bf16[6,160,384]{2,1,0:T(8,128)(2,1)}, bf16[6,160,384]{2,1,0:T(8,128)(2,1)S(1)}, u32[]{:S(2)}, u32[]{:S(2)}) collective-permute-start(bf16[6,160,384]{2,1,0:T(8,128)(2,1)} %get-tuple-element.7.own), channel_id=1, source_target_pairs={{1,2},{2,1},{3,4},{4,3},{5,6},{6,5},{7,8},{8,7},{9,10},{10,9},{11,... | collective-permute-start | bytes 2211848 | tf_op jit(solution)/shard_map/ppermute | solution.py:240
  7.0 30.8 %collective-permute-start = (bf16[6,160,384]{2,1,0:T(8,128)(2,1)}, bf16[6,160,384]{2,1,0:T(8,128)(2,1)S(1)}, u32[]{:S(2)}, u32[]{:S(2)}) collective-permute-start(bf16[6,160,384]{2,1,0:T(8,128)(2,1)} %get-tuple-element.7.own), channel_id=1, source_target_pairs={{0,1},{1,0},{2,3},{3,2},{4,5},{5,4},{6,7},{7,6},{8,9},{9,8},{10,11... | collective-permute-start | bytes 2211848 | tf_op jit(solution)/shard_map/ppermute | solution.py:241
  23.6 27.2 %all-to-all-start = ((f32[128,1,128]{2,1,0:T(1,128)}), f32[128,1,128]{2,1,0:T(1,128)S(1)}, u32[]{:S(2)}, u32[]{:S(2)}) async-start(f32[128,1,128]{2,1,0:T(1,128)} %get-tuple-element.8), calls=%async_computation | async-start | bytes 131072 | tf_op jit(solution)/shard_map/all_to_all | solution.py:274
  37.8 1.1 %copy-start = (bf16[6,160,384]{2,1,0:T(8,128)(2,1)S(1)}, bf16[6,160,384]{2,1,0:T(8,128)(2,1)}, u32[]{:S(2)}) copy-start(bf16[6,160,384]{2,1,0:T(8,128)(2,1)} %get-tuple-element.7.own) | copy-start | bytes 2211844
  50.9 7.3 %copy-start.3 = (bf16[3,3,384,192]{2,3,1,0:T(8,128)(2,1)S(1)}, bf16[3,3,384,192]{2,3,1,0:T(8,128)(2,1)}, u32[]{:S(2)}) copy-start(bf16[3,3,384,192]{2,3,1,0:T(8,128)(2,1)} %param.20) | copy-start | bytes 3981316
  55.3 7.5 %collective-permute-start.3 = (bf16[2,160,384]{2,1,0:T(8,128)(2,1)S(1)}, bf16[2,160,384]{2,1,0:T(8,128)(2,1)S(1)}, u32[]{:S(2)}, u32[]{:S(2)}) collective-permute-start(bf16[2,160,384]{2,1,0:T(8,128)(2,1)S(1)} %conv.1.block), channel_id=1, source_target_pairs={{1,2},{2,1},{3,4},{4,3},{5,6},{6,5},{7,8},{8,7},{9,10},{10,9},{11,... | collective-permute-start | bytes 737288 | tf_op jit(solution)/shard_map/ppermute | solution.py:240
  57.9 5.0 %collective-permute-start.2 = (bf16[2,160,384]{2,1,0:T(8,128)(2,1)S(1)}, bf16[2,160,384]{2,1,0:T(8,128)(2,1)S(1)}, u32[]{:S(2)}, u32[]{:S(2)}) collective-permute-start(bf16[2,160,384]{2,1,0:T(8,128)(2,1)S(1)} %conv.1.block), channel_id=1, source_target_pairs={{0,1},{1,0},{2,3},{3,2},{4,5},{5,4},{6,7},{7,6},{8,9},{9,8},{10,11... | collective-permute-start | bytes 737288 | tf_op jit(solution)/shard_map/ppermute | solution.py:241
  58.2 4.7 %copy-start.1 = (bf16[6,160,384]{2,1,0:T(8,128)(2,1)S(1)}, bf16[6,160,384]{2,1,0:T(8,128)(2,1)}, u32[]{:S(2)}) copy-start(bf16[6,160,384]{2,1,0:T(8,128)(2,1)} %get-tuple-element.7.own) | copy-start | bytes 2211844
  58.2 4.7 %copy-start.2 = (bf16[3,384,768]{2,1,0:T(8,128)(2,1)S(1)}, bf16[3,384,768]{2,1,0:T(8,128)(2,1)}, u32[]{:S(2)}) copy-start(bf16[3,384,768]{2,1,0:T(8,128)(2,1)} %time_weight.1) | copy-start | bytes 5308420

commit v6 on v5

--- a/solution.py
+++ b/solution.py
@@ -147,11 +147,33 @@
         out[t] = (joined_columns(acc, lines) + own[t]).astype(BF16)
 
 
+def mix_kernel(own, partner, outer, block, vectors, time_weight, doubled, partial, taps):
+    frames, width, channels = block.shape
+    time_bias = vectors[:, 3 * channels : 5 * channels]
+    joined = [own[4], own[5], block[0], block[1]]
+    for t in range(2):
+        for a in range(3):
+            taps[pl.ds(t * width, width), a * channels : (a + 1) * channels] = joined[t + a]
+    weights = time_weight[...].reshape(3 * channels, 2 * channels)
+    mixed = jnp.dot(taps[...], weights, preferred_element_type=F32) + time_bias
+    for t in range(2):
+        for k in range(2):
+            lines = pl.ds((2 * t + k) * width, width)
+            part = mixed[t * width : (t + 1) * width, k * channels : (k + 1) * channels]
+            doubled[lines, :] = part.astype(BF16)
+    for n, r in enumerate((0, 2)):
+        for t in range(2):
+            cached = row_at(r, own, partner, outer, 4 + t)
+            taps[pl.ds(n * width, width), t * channels : (t + 1) * channels] = cached
+    first = taps[:, : 2 * channels]
+    partial[0] = jnp.dot(first, weights[: 2 * channels], preferred_element_type=F32) + time_bias
+    second = taps[:, channels : 2 * channels]
+    partial[1] = jnp.dot(second, weights[:channels], preferred_element_type=F32) + time_bias
+
+
 def up_kernel(
-    own,
-    partner,
-    outer,
-    block,
+    doubled,
+    partial,
     block_partner,
     block_outer,
     vectors,
@@ -159,39 +181,33 @@
     up_weight,
     far_out,
     out,
-    time_taps,
-    mixed,
+    taps,
     up_taps,
     lifted,
     turned,
     sems,
 ):
-    frames, width, channels = block.shape
+    frames, width, channels = block_outer.shape
     outputs = out.shape[-2]
+    up_bias = vectors[:, 5 * channels :]
     copies = []
-    rows_of = lambda t, r: pl.ds((t * 3 + r) * width, width)
-    for r in range(3):
-        for t in range(frames):
-            cached = row_at(r, own, partner, outer, 2 * frames + t)
-            for frame, item in ((t, cached), (frames + t, row_at(r, block, block_partner, block_outer, t))):
-                for a in range(3):
-                    if 0 <= frame - a < frames:
-                        k = a * channels
-                        time_taps[rows_of(frame - a, r), k : k + channels] = item
-    time_bias = vectors[:, 3 * channels : 5 * channels]
-    up_bias = vectors[:, 5 * channels :]
-    weights = time_weight[...].reshape(3 * channels, 2 * channels)
-    mixed[...] = jnp.dot(time_taps[...], weights, preferred_element_type=F32)
-    for r in range(3):
-        inside = inside_image(r - 1)
-        for t in range(frames):
-            value = ((mixed[rows_of(t, r), :] + time_bias) * inside).astype(BF16)
+    for n, r in enumerate((0, 2)):
+        for t in range(2):
+            item = row_at(r, None, block_partner, block_outer, t)
+            taps[pl.ds(n * width, width), t * channels : (t + 1) * channels] = item
+    for p in range(2):
+        up_taps[p, :, (1 - p) * channels : (2 - p) * channels] = doubled[...]
+    first = jnp.dot(taps[:, :channels], time_weight[2], preferred_element_type=F32)
+    weights = time_weight[...].reshape(3 * channels, 2 * channels)[channels:]
+    second = jnp.dot(taps[...], weights, preferred_element_type=F32)
+    for t, sums in enumerate((first, second)):
+        for n, step in enumerate((-1, 1)):
+            rows = slice(n * width, (n + 1) * width)
+            value = ((sums[rows] + partial[t, rows, :]) * inside_image(step)).astype(BF16)
             for k in range(2):
+                lines = pl.ds((2 * t + k) * width, width)
                 part = value[:, k * channels : (k + 1) * channels]
-                lines = pl.ds((2 * t + k) * width, width)
-                for p in range(2):
-                    if 0 <= r - p < 2:
-                        up_taps[p, lines, (r - p) * channels : (r - p + 1) * channels] = part
+                up_taps[n, lines, n * channels : (n + 1) * channels] = part
 
     lane = lax.broadcasted_iota(jnp.int32, (width, 2 * outputs), 1)
     low = lax.broadcasted_iota(jnp.int32, (width, 2 * width), 0)
@@ -312,16 +328,28 @@
         cost_estimate=pl.CostEstimate(flops=flops, bytes_accessed=2**23, transcendentals=2**18),
         name="conv",
     )(stats, vectors, base, partner, outer, conv_weight)
-    inputs = (near, partner, outer, block, *swapped(block), vectors, time_weight, subpixel)
+    block_partner, block_outer = swapped(block)
+    doubled, partial = pl.pallas_call(
+        mix_kernel,
+        out_shape=(
+            jax.ShapeDtypeStruct((2 * pixels, channels), BF16),
+            jax.ShapeDtypeStruct((frames, pixels, 2 * channels), F32),
+        ),
+        in_specs=[VMEM] * 6,
+        out_specs=(VMEM, VMEM),
+        scratch_shapes=[pltpu.VMEM((pixels, 3 * channels), BF16)],
+        compiler_params=pltpu.CompilerParams(vmem_limit_bytes=16 * 2**20),
+        cost_estimate=pl.CostEstimate(flops=2**21, bytes_accessed=2**22, transcendentals=0),
+        name="mix",
+    )(near, partner, outer, block, vectors, time_weight)
     out = pl.pallas_call(
         up_kernel,
         out_shape=jax.ShapeDtypeStruct((2 * frames, 2, outputs, 2 * width), BF16),
-        in_specs=[VMEM] * 9,
+        in_specs=[VMEM] * 7,
         out_specs=HBM,
         scratch_shapes=[
             pltpu.VMEM((2, 2 * frames, outputs, 2 * width), BF16),
-            pltpu.VMEM((3 * pixels, 3 * channels), BF16),
-            pltpu.VMEM((3 * pixels, 2 * channels), F32),
+            pltpu.VMEM((pixels, 2 * channels), BF16),
             pltpu.VMEM((2, 2 * pixels, 2 * channels), BF16),
             pltpu.VMEM((2 * pixels, 4 * outputs), F32),
             pltpu.VMEM((2, 2 * frames * outputs, width), BF16),
@@ -332,7 +360,7 @@
             flops=8 * pixels * 4 * channels * outputs * 2, bytes_accessed=2**23, transcendentals=0
         ),
         name="up",
-    )(*inputs)
+    )(doubled, partial, block_partner, block_outer, vectors, time_weight, subpixel)
     return jnp.swapaxes(out, 2, 3)
 
 

time: 70.3 us -> 68.2 us (0.970)
  waiting for transfers between devices: 12.1 us -> 10.6 us
  Pallas kernels: 18.2 us -> 17.4 us
    pallas_call x1, Pallas kernels: 6.93 us -> 4.65 us  [on_device(): pl.pallas_call(up_kernel, out_shape=jax.ShapeDtypeStruct((2 * frames, 2,...]
    ppermute x2, waiting for transfers between devices: 4.13 us -> 2.56 us  [swapped(): outer = lax.ppermute(value, ROWS, across)]
    pallas_call x0 -> x1, Pallas kernels: none -> 1.47 us  [on_device(): pl.pallas_call(mix_kernel, out_shape=(jax.ShapeDtypeStruct((2 * pixels, c...]
  transfers between devices with their start and end apart: 5 -> 5, of which waited for: 2 -> 2; matrix products, arithmetic and copies ran while one was open for 1% -> 1% of each run, Pallas kernels for 6% -> 9%
where the time goes in v6:
time: 68.2 us; the launch traced here: 67.9 us
  starting transfers between devices  37.6 us (55%)
  Pallas kernels  17.4 us (26%)
  waiting for transfers between devices  10.6 us (16%)
  local copies, waits for them, and re-layouts  1.98 us (3%)
    ppermute x2, starting transfers between devices, swapped(): lax.ppermute(value, ROWS, [(i, i ^ 1) for i in range(devices)])  17 us
    all_to_all x1, starting transfers between devices, on_device(): stats = lax.all_to_all(sums, ROWS, 0, 0)  13.3 us
    all_to_all x1, waiting for transfers between devices, on_device(): stats = lax.all_to_all(sums, ROWS, 0, 0)  8.03 us
    ppermute x2, starting transfers between devices, swapped(): outer = lax.ppermute(value, ROWS, across)  7.36 us
    pallas_call x1, Pallas kernels, on_device(): pl.pallas_call(up_kernel, out_shape=jax.ShapeDtypeStruct((2 * frames, 2,...  4.65 us
    pallas_call x1, Pallas kernels, on_device(): pl.pallas_call(functools.partial(conv_kernel, entries), out_shape=jax.Sha...  4.49 us
    pallas_call x1, Pallas kernels, on_device(): pl.pallas_call(cached_kernel, out_shape=jax.ShapeDtypeStruct((2 * frames,...  3.98 us
    ppermute x2, waiting for transfers between devices, swapped(): outer = lax.ppermute(value, ROWS, across)  2.56 us
  transfers between devices with their start and end apart: 5, of which 2 were waited for; matrix products, arithmetic and copies ran while one was open for 1% of the time, Pallas kernels for 9%

profile of v6, /device:TPU:33, one launch (start us, length us, event | category | flops | bytes accessed | tf_op | source)
XLA Modules:
  0.0 67.9 jit_solution(15397932999761937167)
XLA Ops:
  0.0 2.4 %pack.1 = (bf16[6,160,384]{2,1,0:T(8,128)(2,1)}, f32[128,1,128]{2,1,0:T(1,128)}) custom-call(bf16[2,1,160,384]{3,2,1,0:T(8,128)(2,1)} %latent.1, bf16[2,1,160,384]{3,2,1,0:T(8,128)(2,1)} %conv_cache.1, bf16[2,1,160,384]{3,2,1,0:T(8,128)(2,1)} %time_cache.1), custom_call_target="tpu_custom_call" | custom-call | flops 2097152 | bytes 2097152 | tf_op jit(solution)/shard_map/pack/pallas_call | solution.py:276
  2.4 4.6 %collective-permute-start.1 = (bf16[6,160,384]{2,1,0:T(8,128)(2,1)}, bf16[6,160,384]{2,1,0:T(8,128)(2,1)S(1)}, u32[]{:S(2)}, u32[]{:S(2)}) collective-permute-start(bf16[6,160,384]{2,1,0:T(8,128)(2,1)} %get-tuple-element.9.own), channel_id=1, source_target_pairs={{1,2},{2,1},{3,4},{4,3},{5,6},{6,5},{7,8},{8,7},{9,10},{10,9},{11,... | collective-permute-start | bytes 2211848 | tf_op jit(solution)/shard_map/ppermute | solution.py:256
  7.0 16.6 %collective-permute-start = (bf16[6,160,384]{2,1,0:T(8,128)(2,1)}, bf16[6,160,384]{2,1,0:T(8,128)(2,1)S(1)}, u32[]{:S(2)}, u32[]{:S(2)}) collective-permute-start(bf16[6,160,384]{2,1,0:T(8,128)(2,1)} %get-tuple-element.9.own), channel_id=1, source_target_pairs={{0,1},{1,0},{2,3},{3,2},{4,5},{5,4},{6,7},{7,6},{8,9},{9,8},{10,11... | collective-permute-start | bytes 2211848 | tf_op jit(solution)/shard_map/ppermute | solution.py:257
  23.6 13.3 %all-to-all-start = ((f32[128,1,128]{2,1,0:T(1,128)}), f32[128,1,128]{2,1,0:T(1,128)S(1)}, u32[]{:S(2)}, u32[]{:S(2)}) async-start(f32[128,1,128]{2,1,0:T(1,128)} %get-tuple-element.10), calls=%async_computation | async-start | bytes 131072 | tf_op jit(solution)/shard_map/all_to_all | solution.py:290
  36.9 0.8 %concatenate.3 = f32[2304]{0:T(1024)S(1)} concatenate(f32[384]{0:T(512)} %param.14, f32[384]{0:T(512)} %param.15, f32[384]{0:T(512)} %param.17, f32[768]{0:T(1024)} %param.19, f32[192]{0:T(256)} %param.21, f32[192]{0:T(256)} %param.21), dimensions={0} | concatenate | bytes 18432 | tf_op jit(solution)/shard_map/concatenate | solution.py:301
  37.7 0.0 collective-permute-done.1.outer
  37.8 0.0 collective-permute-done.partner
  37.8 0.0 copy-start.1
  37.8 1.1 %copy-done.1 = bf16[6,160,384]{2,1,0:T(8,128)(2,1)S(1)} copy-done((bf16[6,160,384]{2,1,0:T(8,128)(2,1)S(1)}, bf16[6,160,384]{2,1,0:T(8,128)(2,1)}, u32[]{:S(2)}) %copy-start.1) | copy-done | bytes 737304
  38.9 4.0 %cached.1.own = f32[4,160,384]{2,1,0:T(8,128)S(1)} custom-call(f32[1,2304]{1,0:T(1,128)S(1)} %reshape.3.vectors, bf16[6,160,384]{2,1,0:T(8,128)(2,1)S(1)} %copy-done.1, bf16[6,160,384]{2,1,0:T(8,128)(2,1)S(1)} %collective-permute-done.partner, bf16[6,160,384]{2,1,0:T(8,128)(2,1)S(1)} %collective-permute-done.1.outer, bf16[3,3,3,384,384]{4,3,2,1,0:T(8,128)(2,1)} %weight_far.3), custom_call_target="tpu_custom_call" | custom-call | flops 1274019840 | bytes 8388608 | tf_op jit(solution)/shard_map/cached/pallas_call | solution.py:311
  42.9 8.0 %all-to-all-done.stats = f32[128,1,128]{2,1,0:T(1,128)S(1)} async-done(((f32[128,1,128]{2,1,0:T(1,128)}), f32[128,1,128]{2,1,0:T(1,128)S(1)}, u32[]{:S(2)}, u32[]{:S(2)}) %all-to-all-start) | async-done | bytes 65568 | tf_op jit(solution)/shard_map/all_to_all | solution.py:290
  50.9 0.0 copy-start.3
  50.9 4.5 %conv.1.block = bf16[2,160,384]{2,1,0:T(8,128)(2,1)S(1)} custom-call(f32[128,1,128]{2,1,0:T(1,128)S(1)} %all-to-all-done.stats, f32[1,2304]{1,0:T(1,128)S(1)} %reshape.3.vectors, f32[4,160,384]{2,1,0:T(8,128)S(1)} %cached.1.own, bf16[6,160,384]{2,1,0:T(8,128)(2,1)S(1)} %collective-permute-done.partner, ...), custom_call_target="tpu_custom_call" | custom-call | flops 1274019840 | bytes 8388608 | tf_op jit(solution)/shard_map/conv/pallas_call | solution.py:321
  55.4 0.0 copy-start
  55.4 0.0 copy-start.2
  55.4 2.8 %collective-permute-start.3 = (bf16[2,160,384]{2,1,0:T(8,128)(2,1)S(1)}, bf16[2,160,384]{2,1,0:T(8,128)(2,1)S(1)}, u32[]{:S(2)}, u32[]{:S(2)}) collective-permute-start(bf16[2,160,384]{2,1,0:T(8,128)(2,1)S(1)} %conv.1.block), channel_id=1, source_target_pairs={{1,2},{2,1},{3,4},{4,3},{5,6},{6,5},{7,8},{8,7},{9,10},{10,9},{11,... | collective-permute-start | bytes 737288 | tf_op jit(solution)/shard_map/ppermute | solution.py:256
  58.2 0.3 collective-permute-start.2
  58.5 0.0 copy-done.3
  58.5 0.5 subpixel.1.up_weight
  59.0 0.0 copy-done
  59.1 0.0 copy-done.2
  59.1 1.5 %mix.1 = (bf16[640,384]{1,0:T(8,128)(2,1)S(1)}, f32[2,320,768]{2,1,0:T(8,128)S(1)}) custom-call(bf16[6,160,384]{2,1,0:T(8,128)(2,1)S(1)} %copy-done.2, bf16[6,160,384]{2,1,0:T(8,128)(2,1)S(1)} %collective-permute-done.partner, bf16[6,160,384]{2,1,0:T(8,128)(2,1)S(1)} %collective-permute-done.1.outer, bf16[2,160,384]{2,1,0:T(8,128)(2,1)S(1)} %conv.1.block, ...), custom_call_target="tpu_custom_call" | custom-call | flops 2097152 | bytes 4194304 | tf_op jit(solution)/shard_map/mix/pallas_call | solution.py:332
  60.5 2.6 %collective-permute-done.3.block_outer = bf16[2,160,384]{2,1,0:T(8,128)(2,1)S(1)} collective-permute-done((bf16[2,160,384]{2,1,0:T(8,128)(2,1)S(1)}, bf16[2,160,384]{2,1,0:T(8,128)(2,1)S(1)}, u32[]{:S(2)}, u32[]{:S(2)}) %collective-permute-start.3) | collective-permute-done | bytes 245792 | tf_op jit(solution)/shard_map/ppermute | solution.py:256
  63.1 0.0 collective-permute-done.2.block_partner
  63.1 4.6 %up.1 = bf16[4,2,192,320]{3,2,1,0:T(8,128)(2,1)} custom-call(bf16[640,384]{1,0:T(8,128)(2,1)S(1)} %get-tuple-element.11.doubled, f32[2,320,768]{2,1,0:T(8,128)S(1)} %get-tuple-element.12.partial, bf16[2,160,384]{2,1,0:T(8,128)(2,1)S(1)} %collective-permute-done.2.block_partner, bf16[2,160,384]{2,1,0:T(8,128)(2,1)S(1)} %collective-permute-done.3.block_outer, ...), custom_call_target="tpu_custom_call" | custom-call | flops 1509949440 | bytes 8388608 | tf_op jit(solution)/shard_map/up/pallas_call | solution.py:345
  (1 shorter events, 0.0 us)
Async XLA Ops:
  2.4 35.4 %collective-permute-start.1 = (bf16[6,160,384]{2,1,0:T(8,128)(2,1)}, bf16[6,160,384]{2,1,0:T(8,128)(2,1)S(1)}, u32[]{:S(2)}, u32[]{:S(2)}) collective-permute-start(bf16[6,160,384]{2,1,0:T(8,128)(2,1)} %get-tuple-element.9.own), channel_id=1, source_target_pairs={{1,2},{2,1},{3,4},{4,3},{5,6},{6,5},{7,8},{8,7},{9,10},{10,9},{11,... | collective-permute-start | bytes 2211848 | tf_op jit(solution)/shard_map/ppermute | solution.py:256
  7.0 30.8 %collective-permute-start = (bf16[6,160,384]{2,1,0:T(8,128)(2,1)}, bf16[6,160,384]{2,1,0:T(8,128)(2,1)S(1)}, u32[]{:S(2)}, u32[]{:S(2)}) collective-permute-start(bf16[6,160,384]{2,1,0:T(8,128)(2,1)} %get-tuple-element.9.own), channel_id=1, source_target_pairs={{0,1},{1,0},{2,3},{3,2},{4,5},{5,4},{6,7},{7,6},{8,9},{9,8},{10,11... | collective-permute-start | bytes 2211848 | tf_op jit(solution)/shard_map/ppermute | solution.py:257
  23.6 27.3 %all-to-all-start = ((f32[128,1,128]{2,1,0:T(1,128)}), f32[128,1,128]{2,1,0:T(1,128)S(1)}, u32[]{:S(2)}, u32[]{:S(2)}) async-start(f32[128,1,128]{2,1,0:T(1,128)} %get-tuple-element.10), calls=%async_computation | async-start | bytes 131072 | tf_op jit(solution)/shard_map/all_to_all | solution.py:290
  37.8 1.1 %copy-start.1 = (bf16[6,160,384]{2,1,0:T(8,128)(2,1)S(1)}, bf16[6,160,384]{2,1,0:T(8,128)(2,1)}, u32[]{:S(2)}) copy-start(bf16[6,160,384]{2,1,0:T(8,128)(2,1)} %get-tuple-element.9.own) | copy-start | bytes 2211844
  50.9 7.6 %copy-start.3 = (bf16[3,3,384,192]{2,3,1,0:T(8,128)(2,1)S(1)}, bf16[3,3,384,192]{2,3,1,0:T(8,128)(2,1)}, u32[]{:S(2)}) copy-start(bf16[3,3,384,192]{2,3,1,0:T(8,128)(2,1)} %param.20) | copy-start | bytes 3981316
  55.4 3.7 %copy-start = (bf16[3,384,768]{2,1,0:T(8,128)(2,1)S(1)}, bf16[3,384,768]{2,1,0:T(8,128)(2,1)}, u32[]{:S(2)}) copy-start(bf16[3,384,768]{2,1,0:T(8,128)(2,1)} %time_weight.3) | copy-start | bytes 5308420
  55.4 3.7 %copy-start.2 = (bf16[6,160,384]{2,1,0:T(8,128)(2,1)S(1)}, bf16[6,160,384]{2,1,0:T(8,128)(2,1)}, u32[]{:S(2)}) copy-start(bf16[6,160,384]{2,1,0:T(8,128)(2,1)} %get-tuple-element.9.own) | copy-start | bytes 2211844
  55.4 7.7 %collective-permute-start.3 = (bf16[2,160,384]{2,1,0:T(8,128)(2,1)S(1)}, bf16[2,160,384]{2,1,0:T(8,128)(2,1)S(1)}, u32[]{:S(2)}, u32[]{:S(2)}) collective-permute-start(bf16[2,160,384]{2,1,0:T(8,128)(2,1)S(1)} %conv.1.block), channel_id=1, source_target_pairs={{1,2},{2,1},{3,4},{4,3},{5,6},{6,5},{7,8},{8,7},{9,10},{10,9},{11,... | collective-permute-start | bytes 737288 | tf_op jit(solution)/shard_map/ppermute | solution.py:256
  58.2 4.9 %collective-permute-start.2 = (bf16[2,160,384]{2,1,0:T(8,128)(2,1)S(1)}, bf16[2,160,384]{2,1,0:T(8,128)(2,1)S(1)}, u32[]{:S(2)}, u32[]{:S(2)}) collective-permute-start(bf16[2,160,384]{2,1,0:T(8,128)(2,1)S(1)} %conv.1.block), channel_id=1, source_target_pairs={{0,1},{1,0},{2,3},{3,2},{4,5},{5,4},{6,7},{7,6},{8,9},{9,8},{10,11... | collective-permute-start | bytes 737288 | tf_op jit(solution)/shard_map/ppermute | solution.py:257

commit v7 on v6

--- a/solution.py
+++ b/solution.py
@@ -147,7 +147,7 @@
         out[t] = (joined_columns(acc, lines) + own[t]).astype(BF16)
 
 
-def mix_kernel(own, partner, outer, block, vectors, time_weight, doubled, partial, taps):
+def mix_kernel(own, partner, outer, block, vectors, time_weight, up_weight, own_lift, partial, taps, doubled):
     frames, width, channels = block.shape
     time_bias = vectors[:, 3 * channels : 5 * channels]
     joined = [own[4], own[5], block[0], block[1]]
@@ -161,6 +161,8 @@
             lines = pl.ds((2 * t + k) * width, width)
             part = mixed[t * width : (t + 1) * width, k * channels : (k + 1) * channels]
             doubled[lines, :] = part.astype(BF16)
+    for p in range(2):
+        own_lift[p] = dot_nt(doubled[...], up_weight[p, :, (1 - p) * channels : (2 - p) * channels])
     for n, r in enumerate((0, 2)):
         for t in range(2):
             cached = row_at(r, own, partner, outer, 4 + t)
@@ -172,7 +174,7 @@
 
 
 def up_kernel(
-    doubled,
+    own_lift,
     partial,
     block_partner,
     block_outer,
@@ -195,8 +197,6 @@
         for t in range(2):
             item = row_at(r, None, block_partner, block_outer, t)
             taps[pl.ds(n * width, width), t * channels : (t + 1) * channels] = item
-    for p in range(2):
-        up_taps[p, :, (1 - p) * channels : (2 - p) * channels] = doubled[...]
     first = jnp.dot(taps[:, :channels], time_weight[2], preferred_element_type=F32)
     weights = time_weight[...].reshape(3 * channels, 2 * channels)[channels:]
     second = jnp.dot(taps[...], weights, preferred_element_type=F32)
@@ -207,17 +207,18 @@
             for k in range(2):
                 lines = pl.ds((2 * t + k) * width, width)
                 part = value[:, k * channels : (k + 1) * channels]
-                up_taps[n, lines, n * channels : (n + 1) * channels] = part
+                up_taps[n, lines, :] = part
 
     lane = lax.broadcasted_iota(jnp.int32, (width, 2 * outputs), 1)
     low = lax.broadcasted_iota(jnp.int32, (width, 2 * width), 0)
     high = lax.broadcasted_iota(jnp.int32, (width, 2 * width), 1)
     spread_out = [(high == 2 * low + q).astype(F32).astype(BF16) for q in range(2)]
     for p in range(2):
-        lifted[...] = dot_nt(up_taps[p], up_weight[p])
+        lifted[...] = dot_nt(up_taps[p], up_weight[p, :, p * channels : (p + 1) * channels])
         for f in range(2 * frames):
             lines = pl.ds(f * width, width)
-            inner, outer = lifted[lines, : 2 * outputs], lifted[lines, 2 * outputs :]
+            both = lifted[lines, :] + own_lift[p, lines, :]
+            inner, outer = both[:, : 2 * outputs], both[:, 2 * outputs :]
             outer = jnp.where(lane < outputs, shifted(outer, -1), shifted(outer, 1))
             value = (inner + outer + up_bias).T.astype(BF16)
             for q in range(2):
@@ -329,19 +330,19 @@
         name="conv",
     )(stats, vectors, base, partner, outer, conv_weight)
     block_partner, block_outer = swapped(block)
-    doubled, partial = pl.pallas_call(
+    own_lift, partial = pl.pallas_call(
         mix_kernel,
         out_shape=(
-            jax.ShapeDtypeStruct((2 * pixels, channels), BF16),
+            jax.ShapeDtypeStruct((2, 2 * pixels, 4 * outputs), F32),
             jax.ShapeDtypeStruct((frames, pixels, 2 * channels), F32),
         ),
-        in_specs=[VMEM] * 6,
+        in_specs=[VMEM] * 7,
         out_specs=(VMEM, VMEM),
-        scratch_shapes=[pltpu.VMEM((pixels, 3 * channels), BF16)],
+        scratch_shapes=[pltpu.VMEM((pixels, 3 * channels), BF16), pltpu.VMEM((2 * pixels, channels), BF16)],
         compiler_params=pltpu.CompilerParams(vmem_limit_bytes=16 * 2**20),
         cost_estimate=pl.CostEstimate(flops=2**21, bytes_accessed=2**22, transcendentals=0),
         name="mix",
-    )(near, partner, outer, block, vectors, time_weight)
+    )(near, partner, outer, block, vectors, time_weight, subpixel)
     out = pl.pallas_call(
         up_kernel,
         out_shape=jax.ShapeDtypeStruct((2 * frames, 2, outputs, 2 * width), BF16),
@@ -350,7 +351,7 @@
         scratch_shapes=[
             pltpu.VMEM((2, 2 * frames, outputs, 2 * width), BF16),
             pltpu.VMEM((pixels, 2 * channels), BF16),
-            pltpu.VMEM((2, 2 * pixels, 2 * channels), BF16),
+            pltpu.VMEM((2, 2 * pixels, channels), BF16),
             pltpu.VMEM((2 * pixels, 4 * outputs), F32),
             pltpu.VMEM((2, 2 * frames * outputs, width), BF16),
             pltpu.SemaphoreType.DMA((2,)),
@@ -360,7 +361,7 @@
             flops=8 * pixels * 4 * channels * outputs * 2, bytes_accessed=2**23, transcendentals=0
         ),
         name="up",
-    )(doubled, partial, block_partner, block_outer, vectors, time_weight, subpixel)
+    )(own_lift, partial, block_partner, block_outer, vectors, time_weight, subpixel)
     return jnp.swapaxes(out, 2, 3)
 
 

time: 68.2 us -> 68.1 us (level)
  Pallas kernels: 17.4 us -> 18.5 us
  waiting for transfers between devices: 10.6 us -> 9.81 us
    ppermute x2, starting transfers between devices: 17 us -> 21.1 us  [swapped(): lax.ppermute(value, ROWS, [(i, i ^ 1) for i in range(devices)])]
    ppermute x2, starting transfers between devices: 7.36 us -> 4.5 us  [swapped(): outer = lax.ppermute(value, ROWS, across)]
    all_to_all x1, starting transfers between devices: 13.3 us -> 11.7 us  [on_device(): stats = lax.all_to_all(sums, ROWS, 0, 0)]
    pallas_call x1, Pallas kernels: 1.47 us -> 2.76 us  [on_device(): pl.pallas_call(mix_kernel, out_shape=(jax.ShapeDtypeStruct((2, 2 * pixels...]
    ppermute x2, waiting for transfers between devices: 2.56 us -> 1.78 us  [swapped(): outer = lax.ppermute(value, ROWS, across)]
  transfers between devices with their start and end apart: 5 -> 5, of which waited for: 2 -> 2; matrix products, arithmetic and copies ran while one was open for 1% -> 1% of each run, Pallas kernels for 9% -> 11%
where the time goes in v7:
time: 68.1 us; the launch traced here: 67.8 us
  starting transfers between devices  37.2 us (55%)
  Pallas kernels  18.5 us (27%)
  waiting for transfers between devices  9.81 us (14%)
  local copies, waits for them, and re-layouts  1.98 us (3%)
    ppermute x2, starting transfers between devices, swapped(): lax.ppermute(value, ROWS, [(i, i ^ 1) for i in range(devices)])  21.1 us
    all_to_all x1, starting transfers between devices, on_device(): stats = lax.all_to_all(sums, ROWS, 0, 0)  11.7 us
    all_to_all x1, waiting for transfers between devices, on_device(): stats = lax.all_to_all(sums, ROWS, 0, 0)  8.02 us
    ppermute x2, starting transfers between devices, swapped(): outer = lax.ppermute(value, ROWS, across)  4.5 us
    pallas_call x1, Pallas kernels, on_device(): pl.pallas_call(functools.partial(conv_kernel, entries), out_shape=jax.Sha...  4.49 us
    pallas_call x1, Pallas kernels, on_device(): pl.pallas_call(up_kernel, out_shape=jax.ShapeDtypeStruct((2 * frames, 2,...  4.42 us
    pallas_call x1, Pallas kernels, on_device(): pl.pallas_call(cached_kernel, out_shape=jax.ShapeDtypeStruct((2 * frames,...  3.98 us
    pallas_call x1, Pallas kernels, on_device(): pl.pallas_call(mix_kernel, out_shape=(jax.ShapeDtypeStruct((2, 2 * pixels...  2.76 us
  transfers between devices with their start and end apart: 5, of which 2 were waited for; matrix products, arithmetic and copies ran while one was open for 1% of the time, Pallas kernels for 11%

profile of v7, /device:TPU:33, one launch (start us, length us, event | category | flops | bytes accessed | tf_op | source)
XLA Modules:
  0.0 67.8 jit_solution(16741100565206911111)
XLA Ops:
  0.0 2.4 %pack.1 = (bf16[6,160,384]{2,1,0:T(8,128)(2,1)}, f32[128,1,128]{2,1,0:T(1,128)}) custom-call(bf16[2,1,160,384]{3,2,1,0:T(8,128)(2,1)} %latent.1, bf16[2,1,160,384]{3,2,1,0:T(8,128)(2,1)} %conv_cache.1, bf16[2,1,160,384]{3,2,1,0:T(8,128)(2,1)} %time_cache.1), custom_call_target="tpu_custom_call" | custom-call | flops 2097152 | bytes 2097152 | tf_op jit(solution)/shard_map/pack/pallas_call | solution.py:277
  2.4 20.5 %collective-permute-start = (bf16[6,160,384]{2,1,0:T(8,128)(2,1)}, bf16[6,160,384]{2,1,0:T(8,128)(2,1)S(1)}, u32[]{:S(2)}, u32[]{:S(2)}) collective-permute-start(bf16[6,160,384]{2,1,0:T(8,128)(2,1)} %get-tuple-element.9.own), channel_id=1, source_target_pairs={{0,1},{1,0},{2,3},{3,2},{4,5},{5,4},{6,7},{7,6},{8,9},{9,8},{10,11... | collective-permute-start | bytes 2211848 | tf_op jit(solution)/shard_map/ppermute | solution.py:258
  22.9 1.9 %collective-permute-start.1 = (bf16[6,160,384]{2,1,0:T(8,128)(2,1)}, bf16[6,160,384]{2,1,0:T(8,128)(2,1)S(1)}, u32[]{:S(2)}, u32[]{:S(2)}) collective-permute-start(bf16[6,160,384]{2,1,0:T(8,128)(2,1)} %get-tuple-element.9.own), channel_id=1, source_target_pairs={{1,2},{2,1},{3,4},{4,3},{5,6},{6,5},{7,8},{8,7},{9,10},{10,9},{11,... | collective-permute-start | bytes 2211848 | tf_op jit(solution)/shard_map/ppermute | solution.py:257
  24.8 11.7 %all-to-all-start = ((f32[128,1,128]{2,1,0:T(1,128)}), f32[128,1,128]{2,1,0:T(1,128)S(1)}, u32[]{:S(2)}, u32[]{:S(2)}) async-start(f32[128,1,128]{2,1,0:T(1,128)} %get-tuple-element.10), calls=%async_computation | async-start | bytes 131072 | tf_op jit(solution)/shard_map/all_to_all | solution.py:291
  36.5 0.8 %concatenate.3 = f32[2304]{0:T(1024)S(1)} concatenate(f32[384]{0:T(512)} %param.14, f32[384]{0:T(512)} %param.15, f32[384]{0:T(512)} %param.17, f32[768]{0:T(1024)} %param.19, f32[192]{0:T(256)} %param.21, f32[192]{0:T(256)} %param.21), dimensions={0} | concatenate | bytes 18432 | tf_op jit(solution)/shard_map/concatenate | solution.py:302
  37.4 0.0 collective-permute-done.partner
  37.4 0.0 collective-permute-done.1.outer
  37.4 0.0 copy-start.1
  37.4 1.1 %copy-done.1 = bf16[6,160,384]{2,1,0:T(8,128)(2,1)S(1)} copy-done((bf16[6,160,384]{2,1,0:T(8,128)(2,1)S(1)}, bf16[6,160,384]{2,1,0:T(8,128)(2,1)}, u32[]{:S(2)}) %copy-start.1) | copy-done | bytes 737304
  38.5 4.0 %cached.1.own = f32[4,160,384]{2,1,0:T(8,128)S(1)} custom-call(f32[1,2304]{1,0:T(1,128)S(1)} %reshape.3.vectors, bf16[6,160,384]{2,1,0:T(8,128)(2,1)S(1)} %copy-done.1, bf16[6,160,384]{2,1,0:T(8,128)(2,1)S(1)} %collective-permute-done.partner, bf16[6,160,384]{2,1,0:T(8,128)(2,1)S(1)} %collective-permute-done.1.outer, bf16[3,3,3,384,384]{4,3,2,1,0:T(8,128)(2,1)} %weight_far.3), custom_call_target="tpu_custom_call" | custom-call | flops 1274019840 | bytes 8388608 | tf_op jit(solution)/shard_map/cached/pallas_call | solution.py:312
  42.5 8.0 %all-to-all-done.stats = f32[128,1,128]{2,1,0:T(1,128)S(1)} async-done(((f32[128,1,128]{2,1,0:T(1,128)}), f32[128,1,128]{2,1,0:T(1,128)S(1)}, u32[]{:S(2)}, u32[]{:S(2)}) %all-to-all-start) | async-done | bytes 65568 | tf_op jit(solution)/shard_map/all_to_all | solution.py:291
  50.5 0.0 copy-start.3
  50.5 4.5 %conv.1.block = bf16[2,160,384]{2,1,0:T(8,128)(2,1)S(1)} custom-call(f32[128,1,128]{2,1,0:T(1,128)S(1)} %all-to-all-done.stats, f32[1,2304]{1,0:T(1,128)S(1)} %reshape.3.vectors, f32[4,160,384]{2,1,0:T(8,128)S(1)} %cached.1.own, bf16[6,160,384]{2,1,0:T(8,128)(2,1)S(1)} %collective-permute-done.partner, ...), custom_call_target="tpu_custom_call" | custom-call | flops 1274019840 | bytes 8388608 | tf_op jit(solution)/shard_map/conv/pallas_call | solution.py:322
  55.0 0.0 copy-start
  55.0 0.0 copy-start.2
  55.1 0.5 collective-permute-start.2
  55.6 2.6 %collective-permute-start.3 = (bf16[2,160,384]{2,1,0:T(8,128)(2,1)S(1)}, bf16[2,160,384]{2,1,0:T(8,128)(2,1)S(1)}, u32[]{:S(2)}, u32[]{:S(2)}) collective-permute-start(bf16[2,160,384]{2,1,0:T(8,128)(2,1)S(1)} %conv.1.block), channel_id=1, source_target_pairs={{1,2},{2,1},{3,4},{4,3},{5,6},{6,5},{7,8},{8,7},{9,10},{10,9},{11,... | collective-permute-start | bytes 737288 | tf_op jit(solution)/shard_map/ppermute | solution.py:257
  58.2 0.0 copy-done.3
  58.2 0.5 subpixel.1.up_weight
  58.7 0.0 copy-done
  58.7 0.0 copy-done.2
  58.7 2.8 %mix.1 = (f32[2,640,768]{2,1,0:T(8,128)S(1)}, f32[2,320,768]{2,1,0:T(8,128)S(1)}) custom-call(bf16[6,160,384]{2,1,0:T(8,128)(2,1)S(1)} %copy-done.2, bf16[6,160,384]{2,1,0:T(8,128)(2,1)S(1)} %collective-permute-done.partner, bf16[6,160,384]{2,1,0:T(8,128)(2,1)S(1)} %collective-permute-done.1.outer, bf16[2,160,384]{2,1,0:T(8,128)(2,1)S(1)} %conv.1.block, ...), custom_call_target="tpu_custom_call" | custom-call | flops 2097152 | bytes 4194304 | tf_op jit(solution)/shard_map/mix/pallas_call | solution.py:333
  61.5 0.0 collective-permute-done.2.block_partner
  61.5 1.8 %collective-permute-done.3.block_outer = bf16[2,160,384]{2,1,0:T(8,128)(2,1)S(1)} collective-permute-done((bf16[2,160,384]{2,1,0:T(8,128)(2,1)S(1)}, bf16[2,160,384]{2,1,0:T(8,128)(2,1)S(1)}, u32[]{:S(2)}, u32[]{:S(2)}) %collective-permute-start.3) | collective-permute-done | bytes 245792 | tf_op jit(solution)/shard_map/ppermute | solution.py:257
  63.3 4.4 %up.1 = bf16[4,2,192,320]{3,2,1,0:T(8,128)(2,1)} custom-call(f32[2,640,768]{2,1,0:T(8,128)S(1)} %get-tuple-element.11.own_lift, f32[2,320,768]{2,1,0:T(8,128)S(1)} %get-tuple-element.12.partial, bf16[2,160,384]{2,1,0:T(8,128)(2,1)S(1)} %collective-permute-done.2.block_partner, bf16[2,160,384]{2,1,0:T(8,128)(2,1)S(1)} %collective-permute-done.3.block_outer, ...), custom_call_target="tpu_custom_call" | custom-call | flops 1509949440 | bytes 8388608 | tf_op jit(solution)/shard_map/up/pallas_call | solution.py:346
  (1 shorter events, 0.0 us)
Async XLA Ops:
  2.4 35.0 %collective-permute-start = (bf16[6,160,384]{2,1,0:T(8,128)(2,1)}, bf16[6,160,384]{2,1,0:T(8,128)(2,1)S(1)}, u32[]{:S(2)}, u32[]{:S(2)}) collective-permute-start(bf16[6,160,384]{2,1,0:T(8,128)(2,1)} %get-tuple-element.9.own), channel_id=1, source_target_pairs={{0,1},{1,0},{2,3},{3,2},{4,5},{5,4},{6,7},{7,6},{8,9},{9,8},{10,11... | collective-permute-start | bytes 2211848 | tf_op jit(solution)/shard_map/ppermute | solution.py:258
  22.9 14.5 %collective-permute-start.1 = (bf16[6,160,384]{2,1,0:T(8,128)(2,1)}, bf16[6,160,384]{2,1,0:T(8,128)(2,1)S(1)}, u32[]{:S(2)}, u32[]{:S(2)}) collective-permute-start(bf16[6,160,384]{2,1,0:T(8,128)(2,1)} %get-tuple-element.9.own), channel_id=1, source_target_pairs={{1,2},{2,1},{3,4},{4,3},{5,6},{6,5},{7,8},{8,7},{9,10},{10,9},{11,... | collective-permute-start | bytes 2211848 | tf_op jit(solution)/shard_map/ppermute | solution.py:257
  24.8 25.7 %all-to-all-start = ((f32[128,1,128]{2,1,0:T(1,128)}), f32[128,1,128]{2,1,0:T(1,128)S(1)}, u32[]{:S(2)}, u32[]{:S(2)}) async-start(f32[128,1,128]{2,1,0:T(1,128)} %get-tuple-element.10), calls=%async_computation | async-start | bytes 131072 | tf_op jit(solution)/shard_map/all_to_all | solution.py:291
  37.4 1.1 %copy-start.1 = (bf16[6,160,384]{2,1,0:T(8,128)(2,1)S(1)}, bf16[6,160,384]{2,1,0:T(8,128)(2,1)}, u32[]{:S(2)}) copy-start(bf16[6,160,384]{2,1,0:T(8,128)(2,1)} %get-tuple-element.9.own) | copy-start | bytes 2211844
  50.5 7.6 %copy-start.3 = (bf16[3,3,384,192]{2,3,1,0:T(8,128)(2,1)S(1)}, bf16[3,3,384,192]{2,3,1,0:T(8,128)(2,1)}, u32[]{:S(2)}) copy-start(bf16[3,3,384,192]{2,3,1,0:T(8,128)(2,1)} %param.20) | copy-start | bytes 3981316
  55.0 3.7 %copy-start = (bf16[3,384,768]{2,1,0:T(8,128)(2,1)S(1)}, bf16[3,384,768]{2,1,0:T(8,128)(2,1)}, u32[]{:S(2)}) copy-start(bf16[3,384,768]{2,1,0:T(8,128)(2,1)} %time_weight.3) | copy-start | bytes 5308420
  55.0 3.7 %copy-start.2 = (bf16[6,160,384]{2,1,0:T(8,128)(2,1)S(1)}, bf16[6,160,384]{2,1,0:T(8,128)(2,1)}, u32[]{:S(2)}) copy-start(bf16[6,160,384]{2,1,0:T(8,128)(2,1)} %get-tuple-element.9.own) | copy-start | bytes 2211844
  55.1 6.4 %collective-permute-start.2 = (bf16[2,160,384]{2,1,0:T(8,128)(2,1)S(1)}, bf16[2,160,384]{2,1,0:T(8,128)(2,1)S(1)}, u32[]{:S(2)}, u32[]{:S(2)}) collective-permute-start(bf16[2,160,384]{2,1,0:T(8,128)(2,1)S(1)} %conv.1.block), channel_id=1, source_target_pairs={{0,1},{1,0},{2,3},{3,2},{4,5},{5,4},{6,7},{7,6},{8,9},{9,8},{10,11... | collective-permute-start | bytes 737288 | tf_op jit(solution)/shard_map/ppermute | solution.py:258
  55.6 7.7 %collective-permute-start.3 = (bf16[2,160,384]{2,1,0:T(8,128)(2,1)S(1)}, bf16[2,160,384]{2,1,0:T(8,128)(2,1)S(1)}, u32[]{:S(2)}, u32[]{:S(2)}) collective-permute-start(bf16[2,160,384]{2,1,0:T(8,128)(2,1)S(1)} %conv.1.block), channel_id=1, source_target_pairs={{1,2},{2,1},{3,4},{4,3},{5,6},{6,5},{7,8},{8,7},{9,10},{10,9},{11,... | collective-permute-start | bytes 737288 | tf_op jit(solution)/shard_map/ppermute | solution.py:257

commit v8 on v6

--- a/solution.py
+++ b/solution.py
@@ -33,19 +33,22 @@
     return jnp.dot(a, b, preferred_element_type=F32, precision=lax.Precision.HIGHEST)
 
 
-def pack_kernel(latent, conv_cache, time_cache, near, sums, sems):
+def pack_kernel(latent, conv_cache, time_cache, near_far, sums, near, sems):
     frames, _, _, channels = latent.shape
-    jobs = []
+    copies, onward = [], []
     for n, source in enumerate((latent, conv_cache, time_cache)):
         for t in range(frames):
-            jobs.append((source.at[t, 0], near.at[n * frames + t]))
-    copies = [pltpu.make_async_copy(a, b, sems.at[i]) for i, (a, b) in enumerate(jobs)]
+            i = n * frames + t
+            copies.append(pltpu.make_async_copy(source.at[t, 0], near.at[i], sems.at[0, i]))
+            onward.append(pltpu.make_async_copy(near.at[i], near_far.at[i], sems.at[1, i]))
     for copy in copies:
         copy.start()
+    for copy, after in zip(copies, onward):
+        copy.wait()
+        after.start()
     total = jnp.zeros((8, channels), F32)
     square = jnp.zeros((8, channels), F32)
     for t in range(frames):
-        copies[t].wait()
         wide = near[t].astype(F32).reshape(-1, 8, channels)
         total = total + jnp.sum(wide, axis=0)
         square = square + jnp.sum(wide * wide, axis=0)
@@ -53,7 +56,7 @@
     grouped = grouped + exact_dot(square, group_matrix(channels, GROUPS, False))
     row = jnp.sum(grouped, axis=0, keepdims=True)
     sums[...] = jnp.broadcast_to(row[None], sums.shape)
-    for copy in copies[frames:]:
+    for copy in onward:
         copy.wait()
 
 
@@ -280,8 +283,11 @@
             jax.ShapeDtypeStruct((devices, 1, LANES), F32),
         ),
         in_specs=[HBM] * 3,
-        out_specs=(VMEM,) * 2,
-        scratch_shapes=[pltpu.SemaphoreType.DMA((3 * frames,))],
+        out_specs=(HBM, VMEM),
+        scratch_shapes=[
+            pltpu.VMEM((3 * frames, width, channels), BF16),
+            pltpu.SemaphoreType.DMA((2, 3 * frames)),
+        ],
         compiler_params=pltpu.CompilerParams(vmem_limit_bytes=ALL_VMEM),
         cost_estimate=pl.CostEstimate(flops=2**21, bytes_accessed=2**21, transcendentals=0),
         name="pack",

time: 68.2 us -> 68.4 us (level)
  no operation moved by 1% of the time
where the time goes in v8:
time: 68.4 us; the launch traced here: 68.1 us
  starting transfers between devices  37.6 us (55%)
  Pallas kernels  17.6 us (26%)
  waiting for transfers between devices  10.6 us (15%)
  local copies, waits for them, and re-layouts  1.98 us (3%)
    ppermute x2, starting transfers between devices, swapped(): lax.ppermute(value, ROWS, [(i, i ^ 1) for i in range(devices)])  17 us
    all_to_all x1, starting transfers between devices, on_device(): stats = lax.all_to_all(sums, ROWS, 0, 0)  13.3 us
    all_to_all x1, waiting for transfers between devices, on_device(): stats = lax.all_to_all(sums, ROWS, 0, 0)  8.02 us
    ppermute x2, starting transfers between devices, swapped(): outer = lax.ppermute(value, ROWS, across)  7.36 us
    pallas_call x1, Pallas kernels, on_device(): pl.pallas_call(up_kernel, out_shape=jax.ShapeDtypeStruct((2 * frames, 2,...  4.65 us
    pallas_call x1, Pallas kernels, on_device(): pl.pallas_call(functools.partial(conv_kernel, entries), out_shape=jax.Sha...  4.49 us
    pallas_call x1, Pallas kernels, on_device(): pl.pallas_call(cached_kernel, out_shape=jax.ShapeDtypeStruct((2 * frames,...  3.98 us
    pallas_call x1, Pallas kernels, on_device(): pl.pallas_call(pack_kernel, out_shape=(jax.ShapeDtypeStruct((3 * frames,...  2.57 us
  transfers between devices with their start and end apart: 5, of which 2 were waited for; matrix products, arithmetic and copies ran while one was open for 1% of the time, Pallas kernels for 9%

profile of v8, /device:TPU:33, one launch (start us, length us, event | category | flops | bytes accessed | tf_op | source)
XLA Modules:
  0.0 68.1 jit_solution(7661144928010878684)
XLA Ops:
  0.0 2.6 %pack.1 = (bf16[6,160,384]{2,1,0:T(8,128)(2,1)}, f32[128,1,128]{2,1,0:T(1,128)}) custom-call(bf16[2,1,160,384]{3,2,1,0:T(8,128)(2,1)} %latent.1, bf16[2,1,160,384]{3,2,1,0:T(8,128)(2,1)} %conv_cache.1, bf16[2,1,160,384]{3,2,1,0:T(8,128)(2,1)} %time_cache.1), custom_call_target="tpu_custom_call" | custom-call | flops 2097152 | bytes 2097152 | tf_op jit(solution)/shard_map/pack/pallas_call | solution.py:279
  2.6 4.6 %collective-permute-start.1 = (bf16[6,160,384]{2,1,0:T(8,128)(2,1)}, bf16[6,160,384]{2,1,0:T(8,128)(2,1)S(1)}, u32[]{:S(2)}, u32[]{:S(2)}) collective-permute-start(bf16[6,160,384]{2,1,0:T(8,128)(2,1)} %get-tuple-element.9.own), channel_id=1, source_target_pairs={{1,2},{2,1},{3,4},{4,3},{5,6},{6,5},{7,8},{8,7},{9,10},{10,9},{11,... | collective-permute-start | bytes 2211848 | tf_op jit(solution)/shard_map/ppermute | solution.py:259
  7.2 16.6 %collective-permute-start = (bf16[6,160,384]{2,1,0:T(8,128)(2,1)}, bf16[6,160,384]{2,1,0:T(8,128)(2,1)S(1)}, u32[]{:S(2)}, u32[]{:S(2)}) collective-permute-start(bf16[6,160,384]{2,1,0:T(8,128)(2,1)} %get-tuple-element.9.own), channel_id=1, source_target_pairs={{0,1},{1,0},{2,3},{3,2},{4,5},{5,4},{6,7},{7,6},{8,9},{9,8},{10,11... | collective-permute-start | bytes 2211848 | tf_op jit(solution)/shard_map/ppermute | solution.py:260
  23.8 13.3 %all-to-all-start = ((f32[128,1,128]{2,1,0:T(1,128)}), f32[128,1,128]{2,1,0:T(1,128)S(1)}, u32[]{:S(2)}, u32[]{:S(2)}) async-start(f32[128,1,128]{2,1,0:T(1,128)} %get-tuple-element.10), calls=%async_computation | async-start | bytes 131072 | tf_op jit(solution)/shard_map/all_to_all | solution.py:296
  37.1 0.8 %concatenate.3 = f32[2304]{0:T(1024)S(1)} concatenate(f32[384]{0:T(512)} %param.14, f32[384]{0:T(512)} %param.15, f32[384]{0:T(512)} %param.17, f32[768]{0:T(1024)} %param.19, f32[192]{0:T(256)} %param.21, f32[192]{0:T(256)} %param.21), dimensions={0} | concatenate | bytes 18432 | tf_op jit(solution)/shard_map/concatenate | solution.py:307
  38.0 0.0 collective-permute-done.1.outer
  38.0 0.0 collective-permute-done.partner
  38.0 0.0 copy-start.1
  38.0 1.1 %copy-done.1 = bf16[6,160,384]{2,1,0:T(8,128)(2,1)S(1)} copy-done((bf16[6,160,384]{2,1,0:T(8,128)(2,1)S(1)}, bf16[6,160,384]{2,1,0:T(8,128)(2,1)}, u32[]{:S(2)}) %copy-start.1) | copy-done | bytes 737304
  39.1 4.0 %cached.1.own = f32[4,160,384]{2,1,0:T(8,128)S(1)} custom-call(f32[1,2304]{1,0:T(1,128)S(1)} %reshape.3.vectors, bf16[6,160,384]{2,1,0:T(8,128)(2,1)S(1)} %copy-done.1, bf16[6,160,384]{2,1,0:T(8,128)(2,1)S(1)} %collective-permute-done.partner, bf16[6,160,384]{2,1,0:T(8,128)(2,1)S(1)} %collective-permute-done.1.outer, bf16[3,3,3,384,384]{4,3,2,1,0:T(8,128)(2,1)} %weight_far.3), custom_call_target="tpu_custom_call" | custom-call | flops 1274019840 | bytes 8388608 | tf_op jit(solution)/shard_map/cached/pallas_call | solution.py:317
  43.1 8.0 %all-to-all-done.stats = f32[128,1,128]{2,1,0:T(1,128)S(1)} async-done(((f32[128,1,128]{2,1,0:T(1,128)}), f32[128,1,128]{2,1,0:T(1,128)S(1)}, u32[]{:S(2)}, u32[]{:S(2)}) %all-to-all-start) | async-done | bytes 65568 | tf_op jit(solution)/shard_map/all_to_all | solution.py:296
  51.1 0.0 copy-start.3
  51.1 4.5 %conv.1.block = bf16[2,160,384]{2,1,0:T(8,128)(2,1)S(1)} custom-call(f32[128,1,128]{2,1,0:T(1,128)S(1)} %all-to-all-done.stats, f32[1,2304]{1,0:T(1,128)S(1)} %reshape.3.vectors, f32[4,160,384]{2,1,0:T(8,128)S(1)} %cached.1.own, bf16[6,160,384]{2,1,0:T(8,128)(2,1)S(1)} %collective-permute-done.partner, ...), custom_call_target="tpu_custom_call" | custom-call | flops 1274019840 | bytes 8388608 | tf_op jit(solution)/shard_map/conv/pallas_call | solution.py:327
  55.6 0.0 copy-start
  55.6 0.0 copy-start.2
  55.6 2.8 %collective-permute-start.3 = (bf16[2,160,384]{2,1,0:T(8,128)(2,1)S(1)}, bf16[2,160,384]{2,1,0:T(8,128)(2,1)S(1)}, u32[]{:S(2)}, u32[]{:S(2)}) collective-permute-start(bf16[2,160,384]{2,1,0:T(8,128)(2,1)S(1)} %conv.1.block), channel_id=1, source_target_pairs={{1,2},{2,1},{3,4},{4,3},{5,6},{6,5},{7,8},{8,7},{9,10},{10,9},{11,... | collective-permute-start | bytes 737288 | tf_op jit(solution)/shard_map/ppermute | solution.py:259
  58.4 0.3 collective-permute-start.2
  58.7 0.0 copy-done.3
  58.7 0.5 subpixel.1.up_weight
  59.3 0.0 copy-done
  59.3 0.0 copy-done.2
  59.3 1.5 %mix.1 = (bf16[640,384]{1,0:T(8,128)(2,1)S(1)}, f32[2,320,768]{2,1,0:T(8,128)S(1)}) custom-call(bf16[6,160,384]{2,1,0:T(8,128)(2,1)S(1)} %copy-done.2, bf16[6,160,384]{2,1,0:T(8,128)(2,1)S(1)} %collective-permute-done.partner, bf16[6,160,384]{2,1,0:T(8,128)(2,1)S(1)} %collective-permute-done.1.outer, bf16[2,160,384]{2,1,0:T(8,128)(2,1)S(1)} %conv.1.block, ...), custom_call_target="tpu_custom_call" | custom-call | flops 2097152 | bytes 4194304 | tf_op jit(solution)/shard_map/mix/pallas_call | solution.py:338
  60.7 2.6 %collective-permute-done.3.block_outer = bf16[2,160,384]{2,1,0:T(8,128)(2,1)S(1)} collective-permute-done((bf16[2,160,384]{2,1,0:T(8,128)(2,1)S(1)}, bf16[2,160,384]{2,1,0:T(8,128)(2,1)S(1)}, u32[]{:S(2)}, u32[]{:S(2)}) %collective-permute-start.3) | collective-permute-done | bytes 245792 | tf_op jit(solution)/shard_map/ppermute | solution.py:259
  63.3 0.0 collective-permute-done.2.block_partner
  63.3 4.6 %up.1 = bf16[4,2,192,320]{3,2,1,0:T(8,128)(2,1)} custom-call(bf16[640,384]{1,0:T(8,128)(2,1)S(1)} %get-tuple-element.11.doubled, f32[2,320,768]{2,1,0:T(8,128)S(1)} %get-tuple-element.12.partial, bf16[2,160,384]{2,1,0:T(8,128)(2,1)S(1)} %collective-permute-done.2.block_partner, bf16[2,160,384]{2,1,0:T(8,128)(2,1)S(1)} %collective-permute-done.3.block_outer, ...), custom_call_target="tpu_custom_call" | custom-call | flops 1509949440 | bytes 8388608 | tf_op jit(solution)/shard_map/up/pallas_call | solution.py:351
  (1 shorter events, 0.0 us)
Async XLA Ops:
  2.6 35.4 %collective-permute-start.1 = (bf16[6,160,384]{2,1,0:T(8,128)(2,1)}, bf16[6,160,384]{2,1,0:T(8,128)(2,1)S(1)}, u32[]{:S(2)}, u32[]{:S(2)}) collective-permute-start(bf16[6,160,384]{2,1,0:T(8,128)(2,1)} %get-tuple-element.9.own), channel_id=1, source_target_pairs={{1,2},{2,1},{3,4},{4,3},{5,6},{6,5},{7,8},{8,7},{9,10},{10,9},{11,... | collective-permute-start | bytes 2211848 | tf_op jit(solution)/shard_map/ppermute | solution.py:259
  7.2 30.8 %collective-permute-start = (bf16[6,160,384]{2,1,0:T(8,128)(2,1)}, bf16[6,160,384]{2,1,0:T(8,128)(2,1)S(1)}, u32[]{:S(2)}, u32[]{:S(2)}) collective-permute-start(bf16[6,160,384]{2,1,0:T(8,128)(2,1)} %get-tuple-element.9.own), channel_id=1, source_target_pairs={{0,1},{1,0},{2,3},{3,2},{4,5},{5,4},{6,7},{7,6},{8,9},{9,8},{10,11... | collective-permute-start | bytes 2211848 | tf_op jit(solution)/shard_map/ppermute | solution.py:260
  23.8 27.3 %all-to-all-start = ((f32[128,1,128]{2,1,0:T(1,128)}), f32[128,1,128]{2,1,0:T(1,128)S(1)}, u32[]{:S(2)}, u32[]{:S(2)}) async-start(f32[128,1,128]{2,1,0:T(1,128)} %get-tuple-element.10), calls=%async_computation | async-start | bytes 131072 | tf_op jit(solution)/shard_map/all_to_all | solution.py:296
  38.0 1.1 %copy-start.1 = (bf16[6,160,384]{2,1,0:T(8,128)(2,1)S(1)}, bf16[6,160,384]{2,1,0:T(8,128)(2,1)}, u32[]{:S(2)}) copy-start(bf16[6,160,384]{2,1,0:T(8,128)(2,1)} %get-tuple-element.9.own) | copy-start | bytes 2211844
  51.1 7.6 %copy-start.3 = (bf16[3,3,384,192]{2,3,1,0:T(8,128)(2,1)S(1)}, bf16[3,3,384,192]{2,3,1,0:T(8,128)(2,1)}, u32[]{:S(2)}) copy-start(bf16[3,3,384,192]{2,3,1,0:T(8,128)(2,1)} %param.20) | copy-start | bytes 3981316
  55.6 3.7 %copy-start = (bf16[3,384,768]{2,1,0:T(8,128)(2,1)S(1)}, bf16[3,384,768]{2,1,0:T(8,128)(2,1)}, u32[]{:S(2)}) copy-start(bf16[3,384,768]{2,1,0:T(8,128)(2,1)} %time_weight.3) | copy-start | bytes 5308420
  55.6 3.7 %copy-start.2 = (bf16[6,160,384]{2,1,0:T(8,128)(2,1)S(1)}, bf16[6,160,384]{2,1,0:T(8,128)(2,1)}, u32[]{:S(2)}) copy-start(bf16[6,160,384]{2,1,0:T(8,128)(2,1)} %get-tuple-element.9.own) | copy-start | bytes 2211844
  55.6 7.7 %collective-permute-start.3 = (bf16[2,160,384]{2,1,0:T(8,128)(2,1)S(1)}, bf16[2,160,384]{2,1,0:T(8,128)(2,1)S(1)}, u32[]{:S(2)}, u32[]{:S(2)}) collective-permute-start(bf16[2,160,384]{2,1,0:T(8,128)(2,1)S(1)} %conv.1.block), channel_id=1, source_target_pairs={{1,2},{2,1},{3,4},{4,3},{5,6},{6,5},{7,8},{8,7},{9,10},{10,9},{11,... | collective-permute-start | bytes 737288 | tf_op jit(solution)/shard_map/ppermute | solution.py:259
  58.4 4.9 %collective-permute-start.2 = (bf16[2,160,384]{2,1,0:T(8,128)(2,1)S(1)}, bf16[2,160,384]{2,1,0:T(8,128)(2,1)S(1)}, u32[]{:S(2)}, u32[]{:S(2)}) collective-permute-start(bf16[2,160,384]{2,1,0:T(8,128)(2,1)S(1)} %conv.1.block), channel_id=1, source_target_pairs={{0,1},{1,0},{2,3},{3,2},{4,5},{5,4},{6,7},{7,6},{8,9},{9,8},{10,11... | collective-permute-start | bytes 737288 | tf_op jit(solution)/shard_map/ppermute | solution.py:260
